TPU v7x, 256 devices: a whole 4x4x8 slice. The times are simulated.
256 devices in a mesh: context: 16 (over z, core), tensor: 4 (over x), fsdp: 4 (over y).
Axes of the slice: x: 4, y: 4, z: 8, core: 2. Of those that a mesh axis runs over, the one named last changes fastest.
Arguments:
- input_raw: bfloat16 [4, 8192, 5120], P('fsdp', ('context', 'tensor')), may hold values from -6 to 6
- state_proj_raw: bfloat16 [4, 8192, 256], P('fsdp', ('context', 'tensor')), may hold values from -6 to 6
- gate_branch: bfloat16 [4, 8192, 5120], P('fsdp', ('context', 'tensor')), may hold values from -6 to 6
- step_raw: bfloat16 [4, 8192, 80], P('fsdp', ('context', 'tensor')), may hold values from -6 to 6
- convolution_taps: float32 [4, 5376], replicated, may hold values from -3 to 3
- convolution_bias: float32 [5376], replicated, may hold values from -3 to 3
- step_bias: float32 [80], P('tensor'), may hold values from -1.5 to 0.5
- decay_log_rate: float32 [80], P('tensor'), may hold values from -13 to -2, as said below
- skip_weight: float32 [80], P('tensor'), may hold values from 0.5 to 2
- gated_norm_gain: float32 [5120], P('tensor'), may hold values from 0.1 to 1.9
- output_weight: bfloat16 [5120, 2560], P('tensor', 'fsdp'), may hold values from -0.078125 to 0.078125
- adapter_down: bfloat16 [5120, 16], P('tensor'), may hold values from -0.078125 to 0.078125
- adapter_up: bfloat16 [16, 2560], replicated, may hold values from -0.29882812 to 0.29882812
- cotangent: bfloat16 [4, 8192, 2560], P('fsdp', ('context', 'tensor')), may hold values from -6 to 6
Outputs:
- mixed: bfloat16 [4, 8192, 2560], P('fsdp', ('context', 'tensor'))
- grad_a: float32 [5120, 16], P('tensor')
- grad_b: float32 [16, 2560], replicated
Inputs may be any that keep to these rules, and one draw needn't show every extreme that they name: `decay_log_rate`: logarithms of positive decay rates.
All inputs are finite; a program needn't handle non-finite values.
Results may differ from a plain program's by a relative error of at most 0.017.
Values may be sent and summed in bfloat16 or wider, within the bound.
A program may use at most 128 MiB of HBM per device.

v0:
```python
import math

import jax
import jax.numpy as jnp
from jax import lax
from jax.sharding import Mesh
from jax.sharding import PartitionSpec as P

CONTEXT = ("context_0", "context_1")
CONTEXT_FSDP = ("context_0", "context_1", "fsdp")
CONTEXT_TENSOR = ("context_0", "context_1", "tensor")


epsilon = 1e-05


def sent_to_all(array, axis):
    copies = jnp.broadcast_to(array, (lax.axis_size(axis), *array.shape))
    return lax.all_to_all(copies, axis, split_axis=0, concat_axis=0, tiled=True)


def in_order(parts, dim):
    dims = list(parts.shape[1:])
    dims[dim] *= parts.shape[0]
    return jnp.moveaxis(parts, 0, dim).reshape(dims)


def gather_directly(array, axis, dim):
    parts = sent_to_all(array, axis)
    return in_order(parts, dim)


def passed_along(value, axis, steps):
    count = lax.axis_size(axis)
    leading, last = (max(0, -steps), min(count, count - steps))
    return lax.ppermute(value, axis, [(source, source + steps) for source in range(leading, last)])


def filled_with(array, identity):
    return jax.tree.map(
        lambda part, zero: jnp.zeros_like(part) + jnp.asarray(zero, part.dtype), array, identity
    )


def carried_in(array, axes, combine, identity):
    before = start = filled_with(array, identity)
    subtotal = array
    for axis in reversed(axes):
        devices, index = (lax.axis_size(axis), lax.axis_index(axis))
        pieces = jax.tree.map(lambda part: lax.all_gather(part, axis), subtotal)
        inside, subtotal = (start, start)
        for k in range(devices):
            passed = k < index
            subtotal = combine(subtotal, jax.tree.map(lambda part: part[k], pieces))
            inside = jax.tree.map(lambda new, old: jnp.where(passed, new, old), subtotal, inside)
        before = combine(inside, before)
    return before


def cut_along(array, dim, devices):
    dims = array.shape
    parts = array.reshape(*dims[:dim], devices, dims[dim] // devices, *dims[dim + 1 :])
    return jnp.moveaxis(parts, dim, 0)


def summed_on_arrival(array, axis, dim):
    devices = lax.axis_size(axis)
    parts = lax.all_to_all(cut_along(array, dim, devices), axis, 0, 0, tiled=True)
    return jnp.sum(parts.astype(jnp.float32), axis=0)


def summed_on_arrival_2(array, axis, dim):
    devices = lax.axis_size(axis)
    parts = lax.all_to_all(cut_along(array, dim, devices), axis, 0, 0, tiled=True)
    return jnp.sum(parts, axis=0)


def rows_for(lines, devices):
    spare = -lines.shape[0] % devices
    if not spare:
        return lines
    return jnp.concatenate([lines, jnp.zeros((spare, *lines.shape[1:]), lines.dtype)])


def sum_by_parts(array, axes):
    lines = array.reshape(-1)
    own = summed_on_arrival_2(rows_for(lines, lax.axis_size(axes)), axes, 0)
    whole = gather_directly(own, axes, 0)
    return whole[: len(lines)].reshape(array.shape)


def of_everyone(array, axis):
    return sent_to_all(array, axis).astype(jnp.float32).sum(axis=0)


def convolve(values, before, weight, bias_row):
    length = values.shape[0]
    extended = jnp.concatenate([before, values], axis=0)
    pre_act = bias_row[None, :] + weight[0][None, :] * extended[0:length].astype(jnp.float32)
    for tap_index in range(1, weight.shape[0]):
        pre_act = pre_act + weight[tap_index][None, :] * extended[
            tap_index : tap_index + length
        ].astype(jnp.float32)
    return jax.nn.silu(pre_act).astype(jnp.bfloat16)


def ssd_blocks(x_heads, b_rows, c_rows, step_size, log_decay, block_len):
    highest = lax.Precision.DEFAULT
    length = x_heads.shape[0]
    head_count = x_heads.shape[1]
    head_size = x_heads.shape[2]
    state_size = b_rows.shape[1]
    blocks = length // block_len
    causal = jnp.arange(block_len)[:, None] >= jnp.arange(block_len)[None, :]

    def advance(state_now, pieces):
        x_block, b_block, c_block, step_block, decay_block = pieces
        cum_decay = jnp.cumsum(decay_block, axis=0)
        cum_heads = cum_decay.T
        gap_decay = cum_heads[:, :, None] - cum_heads[:, None, :]
        decay_mat = jnp.where(causal[None], jnp.exp(jnp.where(causal[None], gap_decay, 0.0)), 0.0)
        gram_mat = jnp.dot(c_block, b_block.T, precision=highest)
        x_scaled = x_block * step_block[:, :, None]
        y_inner = jnp.einsum(
            "hij,jhp->ihp", decay_mat * gram_mat[None], x_scaled, precision=highest
        )
        y_state = jnp.exp(cum_decay)[:, :, None] * jnp.einsum(
            "in,hpn->ihp", c_block, state_now, precision=highest
        )
        tail_decay = jnp.exp(cum_decay[-1][None, :] - cum_decay)
        state_next = jnp.exp(cum_decay[-1])[:, None, None] * state_now + jnp.einsum(
            "jhp,jn->hpn", x_scaled * tail_decay[:, :, None], b_block, precision=highest
        )
        return (state_next, y_inner + y_state)

    start_state = jnp.zeros((head_count, head_size, state_size), jnp.float32)
    state_end, y_blocks = lax.scan(
        advance,
        start_state,
        (
            x_heads.reshape(blocks, block_len, head_count, head_size),
            b_rows.reshape(blocks, block_len, state_size),
            c_rows.reshape(blocks, block_len, state_size),
            step_size.reshape(blocks, block_len, head_count),
            log_decay.reshape(blocks, block_len, head_count),
        ),
    )
    return (y_blocks.reshape(length, head_count, head_size), state_end)


def chain_states(earlier, later):
    return (earlier[0] + later[0], jnp.exp(later[0])[:, None, None] * earlier[1] + later[1])


def shards(
    input_raw,
    state_proj_raw,
    gate_branch,
    step_raw,
    convolution_taps,
    convolution_bias,
    step_bias,
    decay_log_rate,
    skip_weight,
    gated_norm_gain,
    output_weight,
    adapter_down,
    adapter_up,
    cotangent,
):
    highest = lax.Precision.DEFAULT
    tok_rows = input_raw.shape[1]
    inner_width = input_raw.shape[2]
    state_size = state_proj_raw.shape[2] // 2
    rim_width = convolution_taps.shape[0] - 1
    x_part, z_heads, dt_heads = (
        lax.all_to_all(input_raw[0], "tensor", split_axis=1, concat_axis=0, tiled=True),
        lax.all_to_all(gate_branch[0], "tensor", split_axis=1, concat_axis=0, tiled=True),
        lax.all_to_all(step_raw[0], "tensor", split_axis=1, concat_axis=0, tiled=True),
    )
    shared_in = gather_directly(state_proj_raw[0], "tensor", 0)
    local_width = x_part.shape[1]
    first_channel = lax.axis_index("tensor") * local_width
    joined = jnp.concatenate([x_part, shared_in], axis=1)
    before = passed_along(joined[joined.shape[0] - rim_width :], CONTEXT, 1)
    weight_cut = jnp.concatenate(
        [
            lax.dynamic_slice_in_dim(convolution_taps, first_channel, local_width, 1),
            convolution_taps[:, inner_width:],
        ],
        axis=1,
    )
    bias_cut = jnp.concatenate(
        [
            lax.dynamic_slice_in_dim(convolution_bias, first_channel, local_width, 0),
            convolution_bias[inner_width:],
        ],
        axis=0,
    )
    convolved = convolve(joined, before, weight_cut, bias_cut)
    x_heads_bf = convolved[:, :local_width]
    shared = convolved[:, local_width:]
    span_rows = x_heads_bf.shape[0]
    local_heads = dt_heads.shape[1]
    local_width = x_heads_bf.shape[1]
    head_size = local_width // local_heads
    x_heads = x_heads_bf.astype(jnp.float32).reshape(span_rows, local_heads, head_size)
    b_rows = shared[:, :state_size].astype(jnp.float32)
    c_rows = shared[:, state_size:].astype(jnp.float32)
    step_size = jax.nn.softplus(dt_heads.astype(jnp.float32) + step_bias[None, :])
    log_decay = -step_size * jnp.exp(decay_log_rate)[None, :]
    y_local, state_end = ssd_blocks(
        x_heads, b_rows, c_rows, step_size, log_decay, math.gcd(span_rows, 256)
    )
    log_total = jnp.sum(log_decay, axis=0)
    prior_total, incoming = carried_in(
        (log_total, state_end),
        CONTEXT,
        chain_states,
        (jnp.zeros_like(log_total), jnp.zeros_like(state_end)),
    )
    reach_decay = jnp.exp(jnp.cumsum(log_decay, axis=0))
    y_heads = y_local + reach_decay[:, :, None] * jnp.einsum(
        "tn,hpn->thp", c_rows, incoming, precision=highest
    )
    y_heads = y_heads + skip_weight[None, :, None] * x_heads
    gated = y_heads.reshape(span_rows, local_width) * jax.nn.silu(z_heads.astype(jnp.float32))
    squares = jnp.sum(gated * gated, axis=1)
    gated_output = (gated * gated_norm_gain[None, :]).astype(jnp.bfloat16)
    adapter_piece = jnp.dot(gated_output, adapter_down, preferred_element_type=jnp.float32)
    full_width = local_width * lax.axis_size("tensor")
    columns = lax.all_gather(output_weight, "fsdp", axis=1, tiled=True)
    sum_squares, adapter_sum = (
        summed_on_arrival(squares.astype(jnp.bfloat16), "tensor", 0),
        summed_on_arrival(adapter_piece.astype(jnp.bfloat16), "tensor", 0),
    )
    summed = summed_on_arrival(
        jnp.dot(gated_output, columns, preferred_element_type=jnp.float32).astype(jnp.bfloat16),
        "tensor",
        0,
    )
    row_norm_scale = lax.rsqrt(sum_squares / full_width + epsilon)
    adapter_branch = adapter_sum.astype(jnp.bfloat16)
    mixed = (
        row_norm_scale[:, None]
        * (summed + 2.0 * jnp.dot(adapter_branch, adapter_up, preferred_element_type=jnp.float32))
    ).astype(jnp.bfloat16)
    cotangent_rows = cotangent[0]
    token_total = (
        tok_rows * lax.axis_size(CONTEXT) * lax.axis_size("tensor") * lax.axis_size("fsdp")
    )
    lowrank_factor = 2.0 / math.sqrt(token_total)
    weighted = lowrank_factor * row_norm_scale[:, None] * adapter_branch.astype(jnp.float32)
    grad_b_local = jnp.dot(weighted.T, cotangent_rows.astype(jnp.float32), precision=highest)
    adapter_gradient = (
        lowrank_factor
        * row_norm_scale[:, None]
        * jnp.dot(cotangent_rows, adapter_up.T, preferred_element_type=jnp.float32)
    )
    adapter_span = gather_directly(adapter_gradient, "tensor", 0)
    grad_a_local = jnp.dot(gated_output.astype(jnp.float32).T, adapter_span, precision=highest)
    grad_a, grad_b_part = (
        sum_by_parts(grad_a_local, CONTEXT_FSDP),
        sum_by_parts(grad_b_local, CONTEXT_FSDP),
    )
    grad_b = of_everyone(grad_b_part.astype(jnp.bfloat16), "tensor").astype(jnp.float32)
    return (mixed[None], grad_a, grad_b)


def solution(mesh):
    torus = Mesh(
        mesh.devices.reshape(8, 2, mesh.shape["tensor"], mesh.shape["fsdp"]),
        ("context_0", "context_1", "tensor", "fsdp"),
    )
    placed = (
        P("fsdp", CONTEXT_TENSOR, None),
        P("fsdp", CONTEXT_TENSOR, None),
        P("fsdp", CONTEXT_TENSOR, None),
        P("fsdp", CONTEXT_TENSOR, None),
        P(),
        P(),
        P("tensor"),
        P("tensor"),
        P("tensor"),
        P("tensor"),
        P("tensor", "fsdp"),
        P("tensor", None),
        P(),
        P("fsdp", CONTEXT_TENSOR, None),
    )
    return jax.shard_map(
        shards,
        mesh=torus,
        in_specs=placed,
        out_specs=(P("fsdp", CONTEXT_TENSOR, None), P("tensor", None), P()),
        check_vma=False,
    )
```

profile of v0, /device:TPU:1, one launch (start us, length us, event | category | flops | bytes accessed | tf_op | source)
XLA Modules:
  0.0 392.2 jit_solution(16728284458805882028)
XLA Ops:
  8.0 8.9 %all_to_all.108 = bf16[128,4,20]{0,2,1:T(8,128)(2,1)S(1)} all-to-all(bf16[128,4,20]{0,2,1:T(8,128)(2,1)S(1)} %all_to_all.73), channel_id=1, replica_groups=mesh['context_0'=8,'context_1'=2,'tensor'=4,'fsdp'=4] {'tensor'}, dimensions={1} | all-to-all | bytes 40960 | tf_op jit(solution)/shard_map/all_to_all | solution.py:179
  31.3 14.0 %all-to-all-done.1 = bf16[128,4,1280]{2,0,1:T(8,128)(2,1)S(1)} async-done(((bf16[128,4,1280]{2,0,1:T(8,128)(2,1)}), bf16[128,4,1280]{2,0,1:T(8,128)(2,1)S(1)}, u32[]{:S(2)}, u32[]{:S(2)}) %all-to-all-start.1) | async-done | bytes 1310752 | tf_op jit(solution)/shard_map/all_to_all | solution.py:177
  45.3 7.8 %collective-permute-start = (bf16[3,1536]{1,0:T(4,128)(2,1)S(1)}, bf16[3,1536]{1,0:T(4,128)(2,1)S(1)}, u32[]{:S(2)}, u32[]{:S(2)}) collective-permute-start(bf16[3,1536]{1,0:T(4,128)(2,1)S(1)} %fusion.141), channel_id=1, source_target_pairs={{0,16},{16,32},{32,48},{48,64},{64,80},{80,96},{96,112},{112,128},... | collective-permute-start | bytes 27656 | tf_op jit(solution)/shard_map/ppermute | solution.py:36
  62.0 4.4 %reshape_reshape.4 = f32[2,256,20,64]{1,0,3,2:T(2,128)} reshape(f32[512,1280]{0,1:T(8,128)} %copy.111) | data formatting | bytes 5242880 | tf_op jit(solution)/shard_map/reshape;reshape | solution.py:141
  66.5 75.6 %while.14 = (s32[]{:T(128)}, f32[20,64,128]{2,1,0:T(8,128)S(1)}, f32[2,256,20,64]{1,0,3,2:T(2,128)}, f32[2,256,20]{1,0,2:T(2,128)S(1)}, f32[2,256,20,64]{1,0,3,2...) while((s32[]{:T(128)}, f32[20,64,128]{2,1,0:T(8,128)S(1)}, ...), condition=%wide.region_3.4_spmd.clone.clone, body=%wide.region_0.3_spmd.clone.clone.sunk | while | flops 360584256 | bytes 17943776 | solution.py:137
  77.2 27.0 %dynamic_update_slice.7 = f32[2,256,20,64]{1,0,3,2:T(2,128)} dynamic-update-slice(f32[2,256,20,64]{1,0,3,2:T(2,128)} %get-tuple-element.285, f32[1,256,20,64]{1,0,3,2:T(1,128)S(1)} %copy.186, s32[]{:T(128)S(6)} %copy.191, s32[]{:T(128)} %constant.31.clone.1..sunk, s32[]{:T(128)} %constant.31.clone.1..sunk, s32[]{:T(128)} %constant.31.clone.1..sunk) | dynamic-update-slice | bytes 2621444 | tf_op jit(solution)/shard_map/while/body/jit(dynamic_update_index_in_dim)/dynamic_update_slice | solution.py:137
  115.0 27.0 %dynamic_update_slice.7 = f32[2,256,20,64]{1,0,3,2:T(2,128)} dynamic-update-slice(f32[2,256,20,64]{1,0,3,2:T(2,128)} %get-tuple-element.285, f32[1,256,20,64]{1,0,3,2:T(1,128)S(1)} %copy.186, s32[]{:T(128)S(6)} %copy.191, s32[]{:T(128)} %constant.31.clone.1..sunk, s32[]{:T(128)} %constant.31.clone.1..sunk, s32[]{:T(128)} %constant.31.clone.1..sunk) | dynamic-update-slice | bytes 2621444 | tf_op jit(solution)/shard_map/while/body/jit(dynamic_update_index_in_dim)/dynamic_update_slice | solution.py:137
  148.5 12.4 %all-gather.11.cloned.1.call-done = f32[40,64,128]{2,1,0:T(8,128)} async-done(((f32[20,64,128]{2,1,0:T(8,128)}), f32[40,64,128]{2,1,0:T(8,128)}) %all-gather.11.cloned.1.call-update) | async-done | bytes 1310736 | tf_op jit(solution)/shard_map/all_gather | solution.py:50
  171.0 15.7 %all-reduce.1 = f32[160]{0:T(256)S(1)} all-reduce(f32[160]{0:T(256)S(1)} %get-tuple-element.211), channel_id=4, replica_groups=mesh['context_0'=8,'context_1'=2,'tensor'=4,'fsdp'=4] {'context_0'}, use_global_device_ids=true, to_apply=%add.1 | all-reduce | flops 160 | bytes 1280
  193.2 4.2 %reshape.301 = f32[512,20,64]{0,2,1:T(8,128)} reshape(f32[4,128,1280]{1,0,2:T(4,128)} %copy.122) | data formatting | bytes 5242880 | tf_op jit(solution)/shard_map/convert_element_type | solution.py:227
  197.4 4.9 %reshape.285 = f32[512,20,64]{0,2,1:T(8,128)} reshape(f32[2,256,20,64]{1,0,3,2:T(2,128)} %get-tuple-element.54) | data formatting | bytes 5242880 | tf_op jit(solution)/shard_map/reshape | solution.py:148
  202.3 26.4 %all-gather.7.cloned.1.call-done = f32[8,20,64,128]{3,2,1,0:T(8,128)} async-done(((f32[1,20,64,128]{3,2,1,0:T(8,128)}), f32[8,20,64,128]{3,2,1,0:T(8,128)}) %all-gather.7.cloned.1.call-update) | async-done | bytes 5242896 | tf_op jit(solution)/shard_map/all_gather | solution.py:50
  228.7 9.4 %multiply_convert_fusion.1 = (bf16[512,20,64]{0,2,1:T(8,128)(2,1)}, f32[512,20,64]{0,2,1:T(8,128)}, f32[512,20,64]{0,2,1:T(8,128)}) fusion(f32[20,64]{1,0:T(8,128)S(1)} %mul.367, f32[512,20,64]{0,2,1:T(8,128)} %reshape.301, f32[512,20,64]{0,2,1:T(8,128)} %bitcast.277, f32[20]{0:T(128)S(1)} %copy-done.16, f32[512,20,64]{0,2,1:T(8,128)} %reshape.285, ...), kind=kOutput, calls=%fused_computation.71 | convolution fusion | flops 179896320 | bytes 21149642 | tf_op jit(solution)/shard_map/tn,hpn->thp/dot_general | solution.py:223
  268.7 11.0 %all-to-all-start.10 = ((f32[64,1,640]{2,1,0:T(1,128)}), f32[64,1,640]{2,1,0:T(1,128)S(1)}, u32[]{:S(2)}, u32[]{:S(2)}) async-start(f32[64,1,640]{2,1,0:T(1,128)} %all_to_all.94), calls=%async_computation.10 | async-start | bytes 327680 | tf_op jit(solution)/shard_map/all_to_all | solution.py:74
  282.5 7.6 %all-to-all-done.10 = f32[64,1,640]{2,1,0:T(1,128)S(1)} async-done(((f32[64,1,640]{2,1,0:T(1,128)}), f32[64,1,640]{2,1,0:T(1,128)S(1)}, u32[]{:S(2)}, u32[]{:S(2)}) %all-to-all-start.10) | async-done | bytes 163872 | tf_op jit(solution)/shard_map/all_to_all | solution.py:74
  290.1 6.1 %all-to-all-start.8 = ((f32[64,1,320]{2,1,0:T(1,128)}), f32[64,1,320]{2,1,0:T(1,128)S(1)}, u32[]{:S(2)}, u32[]{:S(2)}) async-start(f32[64,1,320]{2,1,0:T(1,128)} %all_to_all.93), calls=%async_computation.8 | async-start | bytes 196608 | tf_op jit(solution)/shard_map/all_to_all | solution.py:74
  298.9 6.9 %all-to-all-done.8 = f32[64,1,320]{2,1,0:T(1,128)S(1)} async-done(((f32[64,1,320]{2,1,0:T(1,128)}), f32[64,1,320]{2,1,0:T(1,128)S(1)}, u32[]{:S(2)}, u32[]{:S(2)}) %all-to-all-start.8) | async-done | bytes 81952 | tf_op jit(solution)/shard_map/all_to_all | solution.py:74
  305.8 6.0 %all-to-all-start.11 = ((bf16[64,2,320]{2,1,0:T(2,128)(2,1)}), bf16[64,2,320]{2,1,0:T(2,128)(2,1)S(1)}, u32[]{:S(2)}, u32[]{:S(2)}) async-start(bf16[64,2,320]{2,1,0:T(2,128)(2,1)} %reshape.376), calls=%async_computation.11 | async-start | bytes 196608 | tf_op jit(solution)/shard_map/all_to_all | solution.py:19
  311.9 9.4 %all-to-all-done.11 = bf16[64,2,320]{2,1,0:T(2,128)(2,1)S(1)} async-done(((bf16[64,2,320]{2,1,0:T(2,128)(2,1)}), bf16[64,2,320]{2,1,0:T(2,128)(2,1)S(1)}, u32[]{:S(2)}, u32[]{:S(2)}) %all-to-all-start.11) | async-done | bytes 81952 | tf_op jit(solution)/shard_map/all_to_all | solution.py:19
  322.1 5.8 %all-to-all-start.9 = ((f32[64,1,320]{2,1,0:T(1,128)}), f32[64,1,320]{2,1,0:T(1,128)S(1)}, u32[]{:S(2)}, u32[]{:S(2)}) async-start(f32[64,1,320]{2,1,0:T(1,128)} %broadcast_in_dim.49), calls=%async_computation.9 | async-start | bytes 196608 | tf_op jit(solution)/shard_map/all_to_all | solution.py:19
  328.6 8.9 %all-to-all-done.9 = f32[64,1,320]{2,1,0:T(1,128)S(1)} async-done(((f32[64,1,320]{2,1,0:T(1,128)}), f32[64,1,320]{2,1,0:T(1,128)S(1)}, u32[]{:S(2)}, u32[]{:S(2)}) %all-to-all-start.9) | async-done | bytes 81952 | tf_op jit(solution)/shard_map/all_to_all | solution.py:19
  341.7 7.8 %convolution_convert_fusion = bf16[512,2560]{1,0:T(8,128)(2,1)} fusion(bf16[512,1280]{1,0:T(8,128)(2,1)S(1)} %fusion.56, bf16[1280,2560]{1,0:T(8,128)(2,1)} %all-gather.9.cloned.1.call-done), kind=kOutput, calls=%fused_computation.56 | convolution fusion | flops 3356753920 | bytes 10485760 | tf_op jit(solution)/shard_map/dot_general | solution.py:238
  350.2 4.2 %all-to-all-start.5 = ((bf16[4,128,2560]{2,1,0:T(8,128)(2,1)}), bf16[4,128,2560]{2,1,0:T(8,128)(2,1)S(1)}, u32[]{:S(2)}, u32[]{:S(2)}) async-start(bf16[4,128,2560]{2,1,0:T(8,128)(2,1)} %bitcast.287), calls=%async_computation.5 | async-start | bytes 5242880 | tf_op jit(solution)/shard_map/all_to_all | solution.py:68
  359.2 24.8 %all-to-all-done.5 = bf16[4,128,2560]{2,1,0:T(8,128)(2,1)S(1)} async-done(((bf16[4,128,2560]{2,1,0:T(8,128)(2,1)}), bf16[4,128,2560]{2,1,0:T(8,128)(2,1)S(1)}, u32[]{:S(2)}, u32[]{:S(2)}) %all-to-all-start.5) | async-done | bytes 2621472 | tf_op jit(solution)/shard_map/all_to_all | solution.py:68
  (191 shorter events, 115.7 us)
Async XLA Ops:
  7.2 249.8 %copy-start = (bf16[1,128,2560]{2,1,0:T(8,128)(2,1)S(1)}, bf16[1,128,2560]{2,1,0:T(8,128)(2,1)}, u32[]{:S(2)}) copy-start(bf16[1,128,2560]{2,1,0:T(8,128)(2,1)} %param.29) | copy-start | bytes 1966084
  18.4 8.9 %all-to-all-start.2 = ((bf16[4,128,256]{2,1,0:T(8,128)(2,1)}), bf16[4,128,256]{2,1,0:T(8,128)(2,1)S(1)}, u32[]{:S(2)}, u32[]{:S(2)}) async-start(bf16[4,128,256]{2,1,0:T(8,128)(2,1)} %broadcast_in_dim.46), calls=%async_computation.2 | async-start | bytes 524288 | tf_op jit(solution)/shard_map/all_to_all | solution.py:19
  27.3 18.0 %all-to-all-start.1 = ((bf16[128,4,1280]{2,0,1:T(8,128)(2,1)}), bf16[128,4,1280]{2,0,1:T(8,128)(2,1)S(1)}, u32[]{:S(2)}, u32[]{:S(2)}) async-start(bf16[128,4,1280]{2,0,1:T(8,128)(2,1)} %copy.110), calls=%async_computation.1 | async-start | bytes 2621440 | tf_op jit(solution)/shard_map/all_to_all | solution.py:177
  30.9 130.1 %all-gather.11.cloned.1.call-start = ((), (), s32[]{:S(2)}) async-start(), calls=%async_computation.15 | async-start | bytes 1966080 | tf_op jit(solution)/shard_map/all_gather | solution.py:50
  45.3 8.7 %collective-permute-start = (bf16[3,1536]{1,0:T(4,128)(2,1)S(1)}, bf16[3,1536]{1,0:T(4,128)(2,1)S(1)}, u32[]{:S(2)}, u32[]{:S(2)}) collective-permute-start(bf16[3,1536]{1,0:T(4,128)(2,1)S(1)} %fusion.141), channel_id=1, source_target_pairs={{0,16},{16,32},{32,48},{48,64},{64,80},{80,96},{96,112},{112,128},... | collective-permute-start | bytes 27656 | tf_op jit(solution)/shard_map/ppermute | solution.py:36
  66.5 76.5 %copy-start.18 = (u32[256]{0:T(256)S(1)}, u32[256]{0:T(256)}, u32[]{:S(2)}) copy-start(u32[256]{0:T(256)} %constant.90) | copy-start | bytes 3076
  66.5 77.1 %copy-start.17 = (u32[256]{0:T(256)S(1)}, u32[256]{0:T(256)}, u32[]{:S(2)}) copy-start(u32[256]{0:T(256)} %constant.95) | copy-start | bytes 3076
  142.9 85.8 %all-gather.7.cloned.1.call-start = ((), (), s32[]{:S(2)}) async-start(), calls=%async_computation.13 | async-start | bytes 5898240 | tf_op jit(solution)/shard_map/all_gather | solution.py:50
  163.3 178.4 %all-gather.9.cloned.1.call-start = ((), (), s32[]{:S(2)}) async-start(), calls=%async_computation.14 | async-start | bytes 8192000 | tf_op jit(solution)/shard_map/all_gather | solution.py:232
  165.5 21.3 %all-to-all-start.3 = ((bf16[128,4,1280]{0,2,1:T(8,128)(2,1)}), bf16[128,4,1280]{0,2,1:T(8,128)(2,1)S(1)}, u32[]{:S(2)}, u32[]{:S(2)}) async-start(bf16[128,4,1280]{0,2,1:T(8,128)(2,1)} %bitcast.24), calls=%async_computation.3 | async-start | bytes 2621440 | tf_op jit(solution)/shard_map/all_to_all | solution.py:178
  197.4 31.3 %copy-start.4 = (f32[40,64,128]{2,1,0:T(8,128)S(1)}, f32[40,64,128]{2,1,0:T(8,128)}, u32[]{:S(2)}) copy-start(f32[40,64,128]{2,1,0:T(8,128)} %all-gather.11.cloned.1.call-done) | copy-start | bytes 3932164
  197.4 31.3 %copy-start.16 = (f32[20]{0:T(128)S(1)}, f32[20]{0:T(128)}, u32[]{:S(2)}) copy-start(f32[20]{0:T(128)} %param.24) | copy-start | bytes 244
  244.3 8.2 %all-to-all-start.4 = ((bf16[4,1,128]{2,1,0:T(2,128)(2,1)}), bf16[4,1,128]{2,1,0:T(2,128)(2,1)S(1)}, u32[]{:S(2)}, u32[]{:S(2)}) async-start(bf16[4,1,128]{2,1,0:T(2,128)(2,1)} %copy.123), calls=%async_computation.4 | async-start | bytes 4096 | tf_op jit(solution)/shard_map/all_to_all | solution.py:68
  252.5 8.1 %all-to-all-start.6 = ((bf16[4,128,16]{1,2,0:T(8,128)(2,1)}), bf16[4,128,16]{1,2,0:T(8,128)(2,1)S(1)}, u32[]{:S(2)}, u32[]{:S(2)}) async-start(bf16[4,128,16]{1,2,0:T(8,128)(2,1)} %bitcast.244), calls=%async_computation.6 | async-start | bytes 32768 | tf_op jit(solution)/shard_map/all_to_all | solution.py:68
  261.2 7.5 %all-to-all-start.7 = ((bf16[4,128,16]{1,2,0:T(8,128)(2,1)}), bf16[4,128,16]{1,2,0:T(8,128)(2,1)S(1)}, u32[]{:S(2)}, u32[]{:S(2)}) async-start(bf16[4,128,16]{1,2,0:T(8,128)(2,1)} %broadcast_in_dim.48), calls=%async_computation.7 | async-start | bytes 32768 | tf_op jit(solution)/shard_map/all_to_all | solution.py:19
  264.5 32.0 %copy-start.8 = (bf16[128,16]{0,1:T(8,128)(2,1)}, bf16[128,16]{0,1:T(8,128)(2,1)S(1)}, u32[]{:S(2)}) copy-start(bf16[128,16]{0,1:T(8,128)(2,1)S(1)} %reduce_sum.79) | copy-start | bytes 12292
  268.7 21.4 %all-to-all-start.10 = ((f32[64,1,640]{2,1,0:T(1,128)}), f32[64,1,640]{2,1,0:T(1,128)S(1)}, u32[]{:S(2)}, u32[]{:S(2)}) async-start(f32[64,1,640]{2,1,0:T(1,128)} %all_to_all.94), calls=%async_computation.10 | async-start | bytes 327680 | tf_op jit(solution)/shard_map/all_to_all | solution.py:74
  290.1 15.6 %all-to-all-start.8 = ((f32[64,1,320]{2,1,0:T(1,128)}), f32[64,1,320]{2,1,0:T(1,128)S(1)}, u32[]{:S(2)}, u32[]{:S(2)}) async-start(f32[64,1,320]{2,1,0:T(1,128)} %all_to_all.93), calls=%async_computation.8 | async-start | bytes 196608 | tf_op jit(solution)/shard_map/all_to_all | solution.py:74
  305.8 15.6 %all-to-all-start.11 = ((bf16[64,2,320]{2,1,0:T(2,128)(2,1)}), bf16[64,2,320]{2,1,0:T(2,128)(2,1)S(1)}, u32[]{:S(2)}, u32[]{:S(2)}) async-start(bf16[64,2,320]{2,1,0:T(2,128)(2,1)} %reshape.376), calls=%async_computation.11 | async-start | bytes 196608 | tf_op jit(solution)/shard_map/all_to_all | solution.py:19
  322.1 15.4 %all-to-all-start.9 = ((f32[64,1,320]{2,1,0:T(1,128)}), f32[64,1,320]{2,1,0:T(1,128)S(1)}, u32[]{:S(2)}, u32[]{:S(2)}) async-start(f32[64,1,320]{2,1,0:T(1,128)} %broadcast_in_dim.49), calls=%async_computation.9 | async-start | bytes 196608 | tf_op jit(solution)/shard_map/all_to_all | solution.py:19
  338.2 11.3 %all-to-all-start.12 = ((bf16[4,16,2560]{2,1,0:T(8,128)(2,1)}), bf16[4,16,2560]{2,1,0:T(8,128)(2,1)S(1)}, u32[]{:S(2)}, u32[]{:S(2)}) async-start(bf16[4,16,2560]{2,1,0:T(8,128)(2,1)} %broadcast_in_dim.51), calls=%async_computation.12 | async-start | bytes 655360 | tf_op jit(solution)/shard_map/all_to_all | solution.py:19
  350.2 33.9 %all-to-all-start.5 = ((bf16[4,128,2560]{2,1,0:T(8,128)(2,1)}), bf16[4,128,2560]{2,1,0:T(8,128)(2,1)S(1)}, u32[]{:S(2)}, u32[]{:S(2)}) async-start(bf16[4,128,2560]{2,1,0:T(8,128)(2,1)} %bitcast.287), calls=%async_computation.5 | async-start | bytes 5242880 | tf_op jit(solution)/shard_map/all_to_all | solution.py:68
  355.6 28.8 %copy-start.9 = (bf16[128,16]{0,1:T(8,128)(2,1)S(1)}, bf16[128,16]{0,1:T(8,128)(2,1)}, u32[]{:S(2)}) copy-start(bf16[128,16]{0,1:T(8,128)(2,1)} %copy-done.8) | copy-start | bytes 12292
  355.6 28.8 %copy-start.14 = (f32[128]{0:T(128)S(1)}, f32[128]{0:T(128)}, u32[]{:S(2)}) copy-start(f32[128]{0:T(128)} %get-tuple-element.209) | copy-start | bytes 1540
  (13 other events, 100.8 us)
Sparse Core Ops, SparseCore 0:
  143.0 17.8 all-gather.10
  163.4 65.2 all-gather.6
  230.5 70.8 all-gather.8
where the time goes:
time: 399 us; the launch traced here: 392 us
  waiting for transfers between devices  120 us (30%)
  local copies, waits for them, and re-layouts  110 us (28%)
  starting transfers between devices  66.3 us (17%)
  matrix products  30.8 us (8%)
  blocking collectives  27 us (7%)
  other arithmetic  21.6 us (5%)
  between operations  15.6 us (4%)
    dynamic_update_slice x4, local copies, waits for them, and re-layouts, ssd_blocks(): lax.scan(advance, start_state, (x_heads.reshape(blocks, block_len, head_c...  56.8 us
    all_gather x2, waiting for transfers between devices, carried_in(): pieces = jax.tree.map(lambda part: lax.all_gather(part, axis), subtotal)  38.8 us
    all_to_all x3, waiting for transfers between devices, summed_on_arrival(): lax.all_to_all(cut_along(array, dim, devices), axis, 0, 0, tiled=True)  28.7 us
    all_to_all x5, waiting for transfers between devices, sent_to_all(): return lax.all_to_all(copies, axis, split_axis=0, concat_axis=0, tiled=True)  22.8 us
    all_to_all x5, starting transfers between devices, sent_to_all(): return lax.all_to_all(copies, axis, split_axis=0, concat_axis=0, tiled=True)  22 us
    unnamed x2, blocking collectives  18.1 us
    all_to_all x2, starting transfers between devices, summed_on_arrival_2(): lax.all_to_all(cut_along(array, dim, devices), axis, 0, 0, tiled=True)  17.1 us
    all_to_all x2, waiting for transfers between devices, summed_on_arrival_2(): lax.all_to_all(cut_along(array, dim, devices), axis, 0, 0, tiled=True)  14.5 us
  transfers between devices with their start and end apart: 16, of which 13 were waited for; matrix products, arithmetic and copies ran while one was open for 16% of the time, Pallas kernels for 0%

commit v1 on v0

v1 whole, which is shorter than its diff:
```python
import functools

import jax
import jax.numpy as jnp
from jax import lax
from jax.experimental import pallas as pl
from jax.experimental.pallas import tpu as pltpu
from jax.sharding import Mesh
from jax.sharding import PartitionSpec as P

MESH = pl.DeviceIdType.MESH
CONTEXT_TENSOR = ("context_0", "context_1", "tensor")
F32 = jnp.float32
BF16 = jnp.bfloat16

ROWS = 128
WIDTH = 1280
STATE = 128
OUT = 2560
HALF = 1280
RANK = 16
HEADS = 20
COLS = 640
TOKENS = 32768
EPS = 1e-05

NT = (((1,), (1,)), ((), ()))
TN = (((0,), (0,)), ((), ()))


def silu(v):
    half = 0.5 * v
    return half + half * jnp.tanh(half)


def dot(a, b, dims=(((1,), (0,)), ((), ())), precision=None):
    return lax.dot_general(a, b, dims, precision=precision, preferred_element_type=F32)


def kernel(
    x_in, bc_in, z_in, dt_in, w_in, cot_in, par, down_t, up,
    mixed, grad_a, grad_b,
    x_ext, xr, xc, bc_ext, bcc, dt_all, gate, zr, wt, cot,
    spread, step, cum, log_dec, y_in, blocks, state, st_send, st_recv, dec_all, dec_wide, back_send, back_recv,
    gated, gt, sq, ap_send, ap_recv,
    rs_send, rs_recv, own,
    v_send, v_recv, xy_recv, v_all,
    sx, rx, sl, sc, rc_, sd, rd, sb, rb, sv, rv, sxy, rxy, sg, rg,
):
    z, k = lax.axis_index("context_0"), lax.axis_index("context_1")
    t, s = lax.axis_index("tensor"), lax.axis_index("fsdp")
    c = 2 * z + k
    right, left, far = lax.rem(t + 1, 4), lax.rem(t + 3, 4), lax.rem(t + 2, 4)
    up_y, down_y = lax.rem(s + 1, 4), lax.rem(s + 3, 4)
    started = []

    def remote(src, dst, index, where):
        return pltpu.make_async_remote_copy(
            src_ref=src, dst_ref=dst, send_sem=sx.at[index], recv_sem=rx.at[index],
            device_id=where, device_id_type=MESH,
        )

    def send(src, dst, index, where):
        copy = remote(src, dst, index, where)
        copy.start()
        started.append(copy)

    def arrived(dst, index):
        remote(dst, dst, index, {"tensor": right}).wait_recv()

    def context_peer(j):
        target = lax.rem(c + j, 16)
        return {"context_0": lax.div(target, 2), "context_1": lax.rem(target, 2)}

    def plane_peer(j):
        return {"tensor": lax.rem(t + lax.div(j, 4), 4), "fsdp": lax.rem(s + lax.rem(j, 4), 4)}

    def exchange(make, how_many=16):
        def go(j, carry):
            make(j).start()
            return carry

        lax.fori_loop(1, how_many, go, 0)

    def settle(make, how_many=16, received=True):
        def go(j, carry):
            if received:
                make(j).wait_recv()
            else:
                make(j).wait_send()
            return carry

        lax.fori_loop(1, how_many, go, 0)

    barrier = pltpu.get_barrier_semaphore()

    def greet(j, carry):
        pl.semaphore_signal(barrier, inc=1, device_id=context_peer(j), device_id_type=MESH)
        pl.semaphore_signal(barrier, inc=1, device_id=plane_peer(j), device_id_type=MESH)
        return carry

    lax.fori_loop(1, 16, greet, 0)
    before = lax.rem(c + 15, 16)
    after = lax.rem(c + 1, 16)

    @pl.when(c > 0)
    def _():
        pl.semaphore_signal(
            barrier, inc=1,
            device_id={"context_0": lax.div(before, 2), "context_1": lax.rem(before, 2), "tensor": 3},
            device_id_type=MESH,
        )

    gives_rim = jnp.logical_and(t == 3, c < 15)

    @pl.when(gives_rim)
    def _():
        pl.semaphore_wait(barrier, 34)

    @pl.when(jnp.logical_not(gives_rim))
    def _():
        pl.semaphore_wait(barrier, 30)

    def rim_copies():
        copies = []
        for p in range(4):
            where = {"context_0": lax.div(after, 2), "context_1": lax.rem(after, 2), "tensor": p}
            copies.append(pltpu.make_async_remote_copy(
                src_ref=x_in.at[pl.ds(112, 16), pl.ds(p * WIDTH, WIDTH)], dst_ref=x_ext.at[pl.ds(0, 16)],
                send_sem=sl.at[16 + p], recv_sem=rx.at[30], device_id=where, device_id_type=MESH))
            copies.append(pltpu.make_async_remote_copy(
                src_ref=bc_in.at[pl.ds(112, 16)], dst_ref=bc_ext.at[pl.ds(0, 16)],
                send_sem=sl.at[20 + p], recv_sem=rx.at[31], device_id=where, device_id_type=MESH))
        return copies

    @pl.when(gives_rim)
    def _():
        for copy in rim_copies():
            copy.start()

    def columns(p):
        return pl.ds(pl.multiple_of(p * WIDTH, WIDTH), WIDTH)

    def x_rows(p, first, count):
        return x_ext.at[pl.ds(pl.multiple_of(16 + p * ROWS + first, 16), count)]

    def z_rows(p, first, count):
        return gate.at[p, pl.ds(first, count)]

    def spread_start(src, rows, relay, base):
        send(src.at[pl.ds(0, 64), columns(far)], relay.at[0], base, {"tensor": right})
        send(src.at[pl.ds(64, 64), columns(far)], relay.at[1], base + 1, {"tensor": left})
        send(src.at[:, columns(right)], rows(t, 0, ROWS), base + 2, {"tensor": right})
        send(src.at[:, columns(left)], rows(t, 0, ROWS), base + 3, {"tensor": left})

    def spread_forward(rows, relay, base):
        arrived(relay.at[0], base)
        send(relay.at[0], rows(left, 0, 64), base + 4, {"tensor": right})
        arrived(relay.at[1], base + 1)
        send(relay.at[1], rows(right, 64, 64), base + 5, {"tensor": left})

    def spread_wait(rows, base):
        arrived(rows(left, 0, ROWS), base + 2)
        arrived(rows(right, 0, ROWS), base + 3)
        arrived(rows(far, 0, 64), base + 4)
        arrived(rows(far, 64, 64), base + 5)

    for j in range(1, 4):
        peer = {"tensor": lax.rem(t + j, 4)}
        send(bc_in, bc_ext.at[pl.ds(pl.multiple_of(16 + t * ROWS, 16), ROWS)], 12 + j, peer)
        send(dt_in, dt_all.at[t], 15 + j, peer)
    spread_start(x_in, x_rows, xr, 0)

    def w_part(rows_from, count, y):
        return wt.at[
            pl.ds(pl.multiple_of(rows_from, 64), count), pl.ds(pl.multiple_of(y * COLS, COLS), COLS)
        ]

    mine, other = k * 640, (1 - k) * 640

    def w_src(first):
        return w_in.at[pl.ds(pl.multiple_of(mine + first, 64), 320)]

    send(w_src(0), w_part(mine, 320, s), 32, {"fsdp": up_y})
    send(w_src(320), w_part(mine + 320, 320, s), 33, {"fsdp": down_y})
    send(w_src(320), w_part(mine + 320, 320, s), 34, {"fsdp": up_y})
    send(w_src(0), w_part(mine, 320, s), 35, {"fsdp": down_y})

    local = [
        pltpu.make_async_copy(cot_in, cot, sl.at[0]),
        pltpu.make_async_copy(bc_in, bc_ext.at[pl.ds(pl.multiple_of(16 + t * ROWS, 16), ROWS)], sl.at[1]),
        pltpu.make_async_copy(dt_in, dt_all.at[t], sl.at[2]),
        pltpu.make_async_copy(x_in.at[:, columns(t)], x_rows(t, 0, ROWS), sl.at[3]),
        pltpu.make_async_copy(z_in.at[:, columns(t)], gate.at[t], sl.at[4]),
        pltpu.make_async_copy(w_in, w_part(0, 1280, s), sl.at[5]),
    ]
    for copy in local:
        copy.start()

    def head_mask(i, carry):
        lanes = pl.ds(pl.multiple_of(i * 128, 128), 128)
        head = lax.broadcasted_iota(jnp.int32, (256, 128), 0)
        head = jnp.where(head >= 128, head - 128, head)
        lane = lax.broadcasted_iota(jnp.int32, (256, 128), 1)
        own_head = 2 * i + jnp.where(lane >= 64, 1, 0)
        spread[:, lanes] = jnp.where(head == own_head, 1.0, 0.0).astype(BF16)
        return carry

    lax.fori_loop(0, 10, head_mask, 0)

    def widen(v):
        high = v.astype(BF16)
        low = (v - high.astype(F32)).astype(BF16)
        return dot(jnp.concatenate([high, low], axis=1), spread[...])

    scale = 2.0 / (TOKENS ** 0.5)

    local[0].wait()
    gt[t] = dot(up[...], cot[...], NT) * scale
    for j in range(1, 4):
        send(gt.at[t], gt.at[t], 18 + j, {"tensor": lax.rem(t + j, 4)})

    local[1].wait()
    local[2].wait()
    for j in range(1, 4):
        source = lax.rem(t + 4 - j, 4)
        arrived(bc_ext.at[pl.ds(pl.multiple_of(16 + source * ROWS, 16), ROWS)], 12 + j)
        arrived(dt_all.at[source], 15 + j)

    row = lax.broadcasted_iota(jnp.int32, (128, 128), 0)
    col = lax.broadcasted_iota(jnp.int32, (128, 128), 1)
    causal = row >= col

    def steps(p, carry):
        pick_row = lax.broadcasted_iota(jnp.int32, (80, 128), 0)
        pick_col = lax.broadcasted_iota(jnp.int32, (80, 128), 1)
        hit = jnp.logical_and(pick_row == pick_col + t * HEADS, pick_col < HEADS)
        raw = dot(dt_all[p], jnp.where(hit, 1.0, 0.0).astype(BF16))
        raw = raw + par[7:8, 0:128]
        step_now = jnp.maximum(raw, 0.0) + jnp.log1p(jnp.exp(-jnp.abs(raw)))
        decay = -step_now * jnp.exp(par[8:9, 0:128])
        tri = jnp.where(row >= col, 1.0, 0.0)
        step[p] = step_now
        cum[p] = dot(tri, decay, precision=lax.Precision.HIGHEST)
        return carry

    lax.fori_loop(0, 4, steps, 0)

    @pl.when(c == 0)
    def _():
        x_ext[0:16, :] = jnp.zeros((16, WIDTH), BF16)
        bc_ext[0:16, :] = jnp.zeros((16, 256), BF16)

    @pl.when(c > 0)
    def _():
        arrived(x_ext.at[pl.ds(0, 16)], 30)
        arrived(bc_ext.at[pl.ds(0, 16)], 31)

    def convolved(ext, p, lanes, taps):
        v = ext[pl.ds(pl.multiple_of(p * ROWS, 16), ROWS + 16), lanes].astype(F32)
        acc = par[4:5, taps] + par[0:1, taps] * pltpu.roll(v, 3, 0)
        acc = acc + par[1:2, taps] * pltpu.roll(v, 2, 0)
        acc = acc + par[2:3, taps] * pltpu.roll(v, 1, 0)
        acc = acc + par[3:4, taps] * v
        return silu(acc[16:]).astype(BF16)

    def conv_shared(p, carry):
        for i in range(2):
            bcc[p, :, pl.ds(i * 128, 128)] = convolved(
                bc_ext, p, pl.ds(i * 128, 128), pl.ds(WIDTH + i * 128, 128))
        return carry

    lax.fori_loop(0, 4, conv_shared, 0)

    spread_forward(x_rows, xr, 0)
    spread_start(z_in, z_rows, zr, 6)
    local[3].wait()
    spread_wait(x_rows, 0)

    def conv_own(p, carry):
        def tile(i, inner):
            lanes = pl.ds(pl.multiple_of(i * 128, 128), 128)
            xc[p, :, lanes] = convolved(x_ext, p, lanes, lanes)
            return inner

        return lax.fori_loop(0, 10, tile, carry)

    lax.fori_loop(0, 4, conv_own, 0)

    state[...] = jnp.zeros((STATE, WIDTH), F32)
    log_dec[...] = jnp.zeros((4, 8, 128), F32)

    def advance(p, total):
        cum_now = cum[p]
        last = cum_now[127:128, :]
        weight = widen(step[p] * jnp.exp(last - cum_now))
        scaled = (xc[p].astype(F32) * weight).astype(BF16)
        fresh = dot(bcc[p, :, 0:128], scaled, TN)
        kept = widen(jnp.broadcast_to(jnp.exp(last), (8, 128)))[0:1, :]
        blocks[p] = state[...]
        state[...] = kept * state[...] + fresh
        log_dec[p] = jnp.broadcast_to(total, (8, 128))
        return total + last

    total = lax.fori_loop(0, 4, advance, jnp.zeros((1, 128), F32))
    dec_all[c] = jnp.broadcast_to(jnp.exp(total), (8, 128))

    def pack_state(i, carry):
        st_send[i] = state[pl.ds(pl.multiple_of(i * 8, 8), 8), :].astype(BF16)
        return carry

    lax.fori_loop(0, 16, pack_state, 0)
    st_recv[c] = st_send[c]

    def state_copy(j):
        return pltpu.make_async_remote_copy(
            src_ref=st_send.at[lax.rem(c + j, 16)], dst_ref=st_recv.at[c],
            send_sem=sc.at[j], recv_sem=rc_.at[j], device_id=context_peer(j), device_id_type=MESH)

    def decay_copy(j):
        return pltpu.make_async_remote_copy(
            src_ref=dec_all.at[c], dst_ref=dec_all.at[c],
            send_sem=sd.at[j], recv_sem=rd.at[j], device_id=context_peer(j), device_id_type=MESH)

    exchange(decay_copy)
    exchange(state_copy)

    arrived(w_part(mine, 320, down_y), 32)
    send(w_part(mine, 320, down_y), w_part(mine, 320, down_y), 36, {"fsdp": up_y})
    arrived(w_part(mine + 320, 320, up_y), 33)
    send(w_part(mine + 320, 320, up_y), w_part(mine + 320, 320, up_y), 37, {"fsdp": down_y})
    spread_forward(z_rows, zr, 6)

    def inside(p, carry):
        b_now, c_now = bcc[p, :, 0:128], bcc[p, :, 128:256]
        gram = dot(c_now, b_now, NT)
        cum_now = cum[p]
        shifted = (cum_now - jnp.log(step[p])).T
        lane = lax.broadcasted_iota(jnp.int32, (1, 128), 1)
        low = jnp.where(lane < 64, 1.0, 0.0)
        for q in range(HEADS // 2):
            mats = []
            for h in (2 * q, 2 * q + 1):
                gap = cum_now[:, h : h + 1] - shifted[h : h + 1, :]
                mats.append(jnp.exp(jnp.where(causal, gap, -1e30)) * gram)
            both = jnp.concatenate(mats, axis=1).astype(BF16)
            x_pair = xc[p, :, pl.ds(q * 128, 128)].astype(F32)
            x_two = jnp.concatenate([x_pair * low, x_pair * (1.0 - low)], axis=0).astype(BF16)
            y_in[p, :, pl.ds(q * 128, 128)] = dot(both, x_two) + x_pair * par[6:7, pl.ds(q * 128, 128)]
        return carry

    lax.fori_loop(0, 4, inside, 0)

    settle(decay_copy)
    dec_wide[...] = widen(dec_all[...].reshape(128, 128))
    settle(state_copy)

    def chain(i, held):
        back_send[i] = held.astype(BF16)
        return dec_wide[pl.ds(pl.multiple_of(i * 8, 8), 8), :] * held + st_recv[i].astype(F32)

    lax.fori_loop(0, 16, chain, jnp.zeros((8, WIDTH), F32))
    back_recv[c] = back_send[c]

    def back_copy(j):
        return pltpu.make_async_remote_copy(
            src_ref=back_send.at[lax.rem(c + j, 16)], dst_ref=back_recv.at[c],
            send_sem=sb.at[j], recv_sem=rb.at[j], device_id=context_peer(j), device_id_type=MESH)

    exchange(back_copy)

    core = {"context_1": 1 - k}
    arrived(w_part(mine + 320, 320, down_y), 34)
    send(w_part(mine, 640, down_y), w_part(mine, 640, down_y), 38, core)
    arrived(w_part(mine, 320, up_y), 35)
    send(w_part(mine, 640, up_y), w_part(mine, 640, up_y), 39, core)
    far_y = lax.rem(s + 2, 4)
    arrived(w_part(mine, 320, far_y), 36)
    arrived(w_part(mine + 320, 320, far_y), 37)
    send(w_part(mine, 640, far_y), w_part(mine, 640, far_y), 40, core)

    local[4].wait()
    spread_wait(z_rows, 6)

    settle(back_copy)

    def unpack_state(i, carry):
        state[pl.ds(pl.multiple_of(i * 8, 8), 8), :] = back_recv[i].astype(F32)
        return carry

    lax.fori_loop(0, 16, unpack_state, 0)

    def finish(p, carry):
        start = blocks[p] + widen(jnp.exp(log_dec[p]))[0:1, :] * state[...]
        reach = widen(jnp.exp(cum[p]))
        y_now = y_in[p] + reach * dot(bcc[p, :, 128:256], start.astype(BF16))
        now = y_now * silu(gate[p].astype(F32))
        squares = (now * now).astype(BF16)
        sq[t, p] = dot(jnp.ones((8, WIDTH), BF16), squares, NT)
        out = (now * par[5:6, 0:WIDTH]).astype(BF16)
        gated[p] = out
        ap_send[p] = dot(down_t[...], out, NT)
        return carry

    lax.fori_loop(0, 4, finish, 0)
    ap_recv[t] = ap_send[t]
    for j in range(1, 4):
        peer = lax.rem(t + j, 4)
        send(sq.at[t], sq.at[t], 21 + j, {"tensor": peer})
        send(ap_send.at[peer], ap_recv.at[t], 24 + j, {"tensor": peer})

    local[5].wait()
    arrived(w_part(other, 640, down_y), 38)
    arrived(w_part(other, 640, up_y), 39)
    arrived(w_part(other, 640, far_y), 40)

    def project(p, half, store):
        def piece(i, carry):
            lanes = pl.ds(pl.multiple_of(i * 256, 256), 256)
            lanes_w = pl.ds(pl.multiple_of(half * HALF + i * 256, 256), 256)
            store(lanes, dot(gated[p], wt[:, lanes_w]))
            return carry

        lax.fori_loop(0, 5, piece, 0)

    def to_slot(slot, extra=None):
        def store(lanes, v):
            if extra is not None:
                v = v + rs_recv[extra, :, lanes].astype(F32)
            rs_send[slot, :, lanes] = v.astype(BF16)

        return store

    project(far, 0, to_slot(0))
    send(rs_send.at[0], rs_recv.at[0], 41, {"tensor": right})
    project(far, 1, to_slot(1))
    send(rs_send.at[1], rs_recv.at[1], 42, {"tensor": left})
    project(right, 1, to_slot(2))
    send(rs_send.at[2], rs_recv.at[2], 43, {"tensor": right})
    project(left, 0, to_slot(3))
    send(rs_send.at[3], rs_recv.at[3], 44, {"tensor": left})

    for j in range(1, 4):
        source = lax.rem(t + 4 - j, 4)
        arrived(gt.at[source], 18 + j)
        arrived(sq.at[source], 21 + j)
        arrived(ap_recv.at[source], 24 + j)

    def row_scale(p):
        squares = (sq[0, p] + sq[1, p]) + (sq[2, p] + sq[3, p])
        return lax.rsqrt(squares * (1.0 / 5120.0) + EPS)

    adapter = ((ap_recv[0] + ap_recv[1]) + (ap_recv[2] + ap_recv[3])).astype(BF16)
    own_scale = row_scale(t)
    weighted = (scale * own_scale[0:1, :] * adapter.astype(F32)).astype(BF16)
    grad_a_now = jnp.zeros((RANK, WIDTH), F32)
    for p in range(4):
        rows_grad = (row_scale(p)[0:1, :] * gt[p]).astype(BF16)
        grad_a_now = grad_a_now + dot(rows_grad, gated[p])
    grad_b_now = dot(weighted, cot[...])
    for i in range(30):
        v_send[i // 2, i % 2] = (
            grad_a_now[:, i * 128 : i * 128 + 128] if i < 10
            else grad_b_now[:, (i - 10) * 128 : (i - 10) * 128 + 128])
    v_send[15] = jnp.zeros((2, RANK, 128), F32)
    v_recv[c] = v_send[c]

    def v_copy(j):
        return pltpu.make_async_remote_copy(
            src_ref=v_send.at[lax.rem(c + j, 16)], dst_ref=v_recv.at[c],
            send_sem=sv.at[j], recv_sem=rv.at[j], device_id=context_peer(j), device_id_type=MESH)

    exchange(v_copy)

    arrived(rs_recv.at[0], 41)
    project(right, 0, to_slot(4, 0))
    send(rs_send.at[4], rs_recv.at[4], 45, {"tensor": right})
    arrived(rs_recv.at[1], 42)
    project(left, 1, to_slot(5, 1))
    send(rs_send.at[5], rs_recv.at[5], 46, {"tensor": left})

    settle(v_copy)

    def add_v(i, held):
        return held + v_recv[i]

    me = 4 * t + s
    xy_recv[me] = lax.fori_loop(1, 16, add_v, v_recv[0])

    def xy_copy(j):
        return pltpu.make_async_remote_copy(
            src_ref=xy_recv.at[me], dst_ref=xy_recv.at[me],
            send_sem=sxy.at[j], recv_sem=rxy.at[j], device_id=plane_peer(j), device_id_type=MESH)

    exchange(xy_copy)

    def own_part(half):
        def store(lanes, v):
            lanes_up = pl.ds(pl.multiple_of(half * HALF + lanes.start, 256), 256)
            own[half, :, lanes] = v + 2.0 * dot(adapter, up[:, lanes_up], TN)

        return store

    project(t, 0, own_part(0))
    project(t, 1, own_part(1))

    settle(xy_copy)

    def add_xy(i, held):
        keep = jnp.where(jnp.logical_or(c >= 5, lax.div(i, 4) == t), 1.0, 0.0)
        return held + keep * xy_recv[i]

    v_all[c] = lax.fori_loop(0, 16, add_xy, jnp.zeros((2, RANK, 128), F32))

    def all_copy(j):
        return pltpu.make_async_remote_copy(
            src_ref=v_all.at[c], dst_ref=v_all.at[c],
            send_sem=sg.at[j], recv_sem=rg.at[j], device_id=context_peer(j), device_id_type=MESH)

    exchange(all_copy)

    arrived(rs_recv.at[2], 43)
    arrived(rs_recv.at[3], 44)
    arrived(rs_recv.at[4], 45)
    arrived(rs_recv.at[5], 46)
    scale_col = jnp.broadcast_to(own_scale[0:1, :], (128, 128)).T

    def close(i, carry):
        lanes = pl.ds(pl.multiple_of(i * 128, 128), 128)
        first = own[0, :, lanes] + rs_recv[4, :, lanes].astype(F32) + rs_recv[3, :, lanes].astype(F32)
        second = own[1, :, lanes] + rs_recv[2, :, lanes].astype(F32) + rs_recv[5, :, lanes].astype(F32)
        mixed[:, lanes] = (scale_col * first).astype(BF16)
        mixed[:, pl.ds(pl.multiple_of(HALF + i * 128, 128), 128)] = (scale_col * second).astype(BF16)
        return carry

    lax.fori_loop(0, 10, close, 0)

    settle(all_copy)
    for i in range(10):
        grad_a[:, i * 128 : i * 128 + 128] = v_all[i // 2, i % 2]
    for i in range(20):
        grad_b[:, i * 128 : i * 128 + 128] = v_all[5 + i // 2, i % 2]

    for make in (decay_copy, state_copy, back_copy, v_copy, xy_copy, all_copy):
        settle(make, received=False)
    for copy in started:
        copy.wait_send()

    @pl.when(gives_rim)
    def _():
        for copy in rim_copies():
            copy.wait_send()


def shards(
    input_raw, state_proj_raw, gate_branch, step_raw, convolution_taps, convolution_bias, step_bias,
    decay_log_rate, skip_weight, gated_norm_gain, output_weight, adapter_down, adapter_up, cotangent,
):
    first = lax.axis_index("tensor") * WIDTH
    conv = jnp.concatenate([convolution_taps, convolution_bias[None, :]], axis=0)
    conv = jnp.concatenate(
        [lax.dynamic_slice_in_dim(conv, first, WIDTH, 1), conv[:, 4 * WIDTH :]], axis=1)

    def line(v):
        return jnp.pad(v, (0, WIDTH + 256 - v.shape[0]))[None, :]

    par = jnp.concatenate(
        [conv, line(gated_norm_gain), line(jnp.repeat(skip_weight, 64)), line(step_bias),
         line(decay_log_rate), jnp.zeros((7, WIDTH + 256), F32)], axis=0)
    hbm = pl.BlockSpec(memory_space=pl.ANY)
    vmem = pl.BlockSpec(memory_space=pltpu.VMEM)
    dma = pltpu.SemaphoreType.DMA
    mixed, grad_a, grad_b = pl.pallas_call(
        kernel,
        out_shape=(
            jax.ShapeDtypeStruct((ROWS, OUT), BF16),
            jax.ShapeDtypeStruct((RANK, WIDTH), F32),
            jax.ShapeDtypeStruct((RANK, OUT), F32),
        ),
        in_specs=[hbm] * 6 + [vmem] * 3,
        out_specs=(vmem, vmem, vmem),
        scratch_shapes=[
            pltpu.VMEM((16 + 512, WIDTH), BF16),
            pltpu.VMEM((2, 64, WIDTH), BF16),
            pltpu.VMEM((4, ROWS, WIDTH), BF16),
            pltpu.VMEM((16 + 512, 256), BF16),
            pltpu.VMEM((4, ROWS, 256), BF16),
            pltpu.VMEM((4, ROWS, 80), BF16),
            pltpu.VMEM((4, ROWS, WIDTH), BF16),
            pltpu.VMEM((2, 64, WIDTH), BF16),
            pltpu.VMEM((WIDTH, OUT), BF16),
            pltpu.VMEM((ROWS, OUT), BF16),
            pltpu.VMEM((256, WIDTH), BF16),
            pltpu.VMEM((4, ROWS, 128), F32),
            pltpu.VMEM((4, ROWS, 128), F32),
            pltpu.VMEM((4, 8, 128), F32),
            pltpu.VMEM((4, ROWS, WIDTH), F32),
            pltpu.VMEM((4, STATE, WIDTH), F32),
            pltpu.VMEM((STATE, WIDTH), F32),
            pltpu.VMEM((16, 8, WIDTH), BF16),
            pltpu.VMEM((16, 8, WIDTH), BF16),
            pltpu.VMEM((16, 8, 128), F32),
            pltpu.VMEM((128, WIDTH), F32),
            pltpu.VMEM((16, 8, WIDTH), BF16),
            pltpu.VMEM((16, 8, WIDTH), BF16),
            pltpu.VMEM((4, ROWS, WIDTH), BF16),
            pltpu.VMEM((4, RANK, 128), F32),
            pltpu.VMEM((4, 4, 8, 128), F32),
            pltpu.VMEM((4, RANK, 128), F32),
            pltpu.VMEM((4, RANK, 128), F32),
            pltpu.VMEM((6, ROWS, HALF), BF16),
            pltpu.VMEM((6, ROWS, HALF), BF16),
            pltpu.VMEM((2, ROWS, HALF), F32),
            pltpu.VMEM((16, 2, RANK, 128), F32),
            pltpu.VMEM((16, 2, RANK, 128), F32),
            pltpu.VMEM((16, 2, RANK, 128), F32),
            pltpu.VMEM((16, 2, RANK, 128), F32),
            dma((48,)), dma((48,)), dma((24,)),
            dma((16,)), dma((16,)), dma((16,)), dma((16,)), dma((16,)), dma((16,)),
            dma((16,)), dma((16,)), dma((16,)), dma((16,)), dma((16,)), dma((16,)),
        ],
        compiler_params=pltpu.CompilerParams(
            collective_id=0, has_side_effects=True, vmem_limit_bytes=64 * 1000 * 1000),
    )(
        input_raw[0], state_proj_raw[0], gate_branch[0], step_raw[0], output_weight, cotangent[0],
        par, adapter_down.T, adapter_up,
    )
    return (mixed[None], grad_a.T, grad_b)


def solution(mesh):
    torus = Mesh(
        mesh.devices.reshape(8, 2, mesh.shape["tensor"], mesh.shape["fsdp"]),
        ("context_0", "context_1", "tensor", "fsdp"),
    )
    tokens = P("fsdp", CONTEXT_TENSOR, None)
    return jax.shard_map(
        shards,
        mesh=torus,
        in_specs=(
            tokens, tokens, tokens, tokens, P(), P(), P("tensor"), P("tensor"), P("tensor"), P("tensor"),
            P("tensor", "fsdp"), P("tensor", None), P(), tokens,
        ),
        out_specs=(tokens, P("tensor", None), P()),
        check_vma=False,
    )
```

time: 399 us -> 116 us (0.29); the launches traced: 392 us -> 115 us
  waiting for transfers between devices: 120 us -> 0 us
  Pallas kernels: 0 us -> 104 us
  local copies, waits for them, and re-layouts: 110 us -> 9.67 us
  starting transfers between devices: 66.3 us -> 0 us
  matrix products: 30.8 us -> 0 us
  blocking collectives: 27 us -> 0 us
  other arithmetic: 21.6 us -> 1.56 us
  between operations: 15.6 us -> 0.68 us
    pallas_call x0 -> x1, Pallas kernels: none -> 104 us  [shards(): pl.pallas_call(kernel, out_shape=(jax.ShapeDtypeStruct((ROWS, OUT), BF16)...]
    all_to_all x12 -> x0, waiting for transfers between devices: 80 us -> none  [the longest x3 28.7 us: summed_on_arrival(): lax.all_to_all(cut_along(array, dim, devices), axis, 0, 0, tiled=True)]
    all_to_all x12 -> x0, starting transfers between devices: 58.3 us -> none  [the longest x5 22 us: sent_to_all(): return lax.all_to_all(copies, axis, split_axis=0, concat_axis=0, tiled=True)]
    dynamic_update_slice x4 -> x0, local copies, waits for them, and re-layouts: 56.8 us -> none  [ssd_blocks(): lax.scan(advance, start_state, (x_heads.reshape(blocks, block_len, head_c...]
    all_gather x3 -> x0, waiting for transfers between devices: 38.9 us -> none  [the longest x2 38.8 us: carried_in(): pieces = jax.tree.map(lambda part: lax.all_gather(part, axis), subtotal)]
    dot_general x15 -> x0, matrix products: 30.8 us -> none  [the longest x1 9.39 us: shards(): jnp.einsum('tn,hpn->thp', c_rows, incoming, precision=highest)]
    unnamed x2 -> x0, blocking collectives: 18.1 us -> none
    convert_element_type x9 -> x0, local copies, waits for them, and re-layouts: 12.7 us -> none  [the longest x2 8.28 us: shards(): z_heads.astype(jnp.float32)]
  transfers between devices with their start and end apart: 16 -> 0, of which waited for: 13 -> 0; matrix products, arithmetic and copies ran while one was open for 16% -> 0% of each run, Pallas kernels for 0% -> 0%
where the time goes in v1:
time: 116 us; the launch traced here: 115 us
  Pallas kernels  104 us (90%)
  local copies, waits for them, and re-layouts  9.67 us (8%)
  other arithmetic  1.56 us (1%)
    pallas_call x1, Pallas kernels, shards(): pl.pallas_call(kernel, out_shape=(jax.ShapeDtypeStruct((ROWS, OUT), BF16)...  104 us
    unnamed x8, local copies, waits for them, and re-layouts  4.76 us

profile of v1, /device:TPU:1, one launch (start us, length us, event | category | flops | bytes accessed | tf_op | source)
XLA Modules:
  0.0 115.5 jit_solution(3639144706536129830)
XLA Ops:
  0.6 0.7 pad.16
  1.3 0.7 pad.17
  2.0 0.7 pad.14
  2.7 0.7 broadcast_in_dim.26
  3.4 0.1 reshape.9
  3.5 0.8 broadcast_in_dim.24
  4.3 1.4 %copy.17 = bf16[1,128,80]{2,1,0:T(8,128)(2,1)} copy(bf16[1,128,80]{1,2,0:T(8,128)(2,1)} %param.17) | data formatting | bytes 40960 | tf_op args[3]
  5.7 0.8 fusion.1
  6.5 0.7 fusion
  7.3 1.3 %concatenate.11.par = f32[16,1536]{1,0:T(8,128)} concatenate(f32[5,1536]{1,0:T(8,128)S(1)} %fusion, f32[1,1536]{1,0:T(1,128)S(1)} %broadcast_in_dim.25, f32[1,1536]{1,0:T(1,128)S(1)} %broadcast_in_dim.27, f32[1,1536]{1,0:T(1,128)S(1)} %broadcast_in_dim.28, f32[1,1536]{1,0:T(1,128)S(1)} %broadcast_in_dim.29, f32[7,1536]{1,0:T(8,128)S(1)} %broadcast_in_dim.30), dimensions={0} | concatenate | bytes 196608 | tf_op jit(solution)/shard_map/concatenate | solution.py:567
  8.6 103.6 %shard_map.157 = (bf16[128,2560]{1,0:T(8,128)(2,1)}, f32[16,1280]{1,0:T(8,128)}, f32[16,2560]{1,0:T(8,128)}) custom-call(bf16[128,5120]{1,0:T(8,128)(2,1)} %bitcast.8, bf16[128,256]{1,0:T(8,128)(2,1)} %bitcast.14, bf16[128,5120]{1,0:T(8,128)(2,1)} %bitcast.9, bf16[128,80]{1,0:T(8,128)(2,1)} %bitcast.12, bf16[1280,640]{1,0:T(8,128)(2,1)} %w_in.1, ...), custom_call_target="tpu_custom_call" | custom-call | tf_op jit(solution)/shard_map/pallas_call | solution.py:573
  112.2 0.0 copy-start.1
  112.2 0.0 copy-start
  112.2 2.0 %copy.21 = bf16[1,128,2560]{2,1,0:T(8,128)(2,1)} copy(bf16[1,128,2560]{2,1,0:T(8,128)(2,1)} %bitcast.11) | data formatting | bytes 1310720
  114.2 0.0 copy-done.1
  114.2 0.6 copy.22
  114.8 0.0 copy-done
  114.8 0.7 copy.23
  (6 shorter events, 0.0 us)
Async XLA Ops:
  112.2 2.0 %copy-start.1 = (f32[16,1280]{1,0:T(8,128)S(1)}, f32[16,1280]{1,0:T(8,128)}, u32[]{:S(2)}) copy-start(f32[16,1280]{1,0:T(8,128)} %get-tuple-element.7) | copy-start | bytes 245764
  112.2 2.7 %copy-start = (f32[16,2560]{1,0:T(8,128)S(1)}, f32[16,2560]{1,0:T(8,128)}, u32[]{:S(2)}) copy-start(f32[16,2560]{1,0:T(8,128)} %get-tuple-element.14) | copy-start | bytes 491524

commit v2 on v1

v2 whole, which is shorter than its diff:
```python
import functools

import jax
import jax.numpy as jnp
from jax import lax
from jax.experimental import pallas as pl
from jax.experimental.pallas import tpu as pltpu
from jax.sharding import Mesh
from jax.sharding import PartitionSpec as P

MESH = pl.DeviceIdType.MESH
CONTEXT_TENSOR = ("context_0", "context_1", "tensor")
F32 = jnp.float32
BF16 = jnp.bfloat16

ROWS = 128
WIDTH = 1280
STATE = 128
OUT = 2560
HALF = 1280
RANK = 16
HEADS = 20
COLS = 640
TOKENS = 32768
EPS = 1e-05

NT = (((1,), (1,)), ((), ()))
TN = (((0,), (0,)), ((), ()))


def silu(v):
    half = 0.5 * v
    return half + half * jnp.tanh(half)


def dot(a, b, dims=(((1,), (0,)), ((), ())), precision=None):
    return lax.dot_general(a, b, dims, precision=precision, preferred_element_type=F32)


def kernel(
    x_in, bc_in, z_in, dt_in, w_in, cot_in, taps_in, bias_in, step_bias_in, rate_in, skip_in, gain_in, down_in, up_in,
    mixed, grad_a, grad_b,
    x_ext, xr, xc, bc_ext, bcc, dt_all, gate, zr, wt, cot,
    taps_x, taps_bc, bias_x, bias_bc, head_par, gain, down_t, up, skip,
    spread, step, cum, log_start, log_tail, y_in, blocks, kept, state, peer_state,
    st_send, st_recv, dec_all, dec_wide, back_send, back_recv, in_send, in_recv, s_in,
    gated, gt, sq, ap_send, ap_recv,
    rs_send, rs_recv, own,
    v_send, v_recv, y_recv, t_recv, v_all,
    sx, rx, sl, sc, rc_, sd, rd, sb, rb, sv, rv, sg, rg,
):
    z, k = lax.axis_index("context_0"), lax.axis_index("context_1")
    t, s = lax.axis_index("tensor"), lax.axis_index("fsdp")
    c = 2 * z + k
    right, left, far = lax.rem(t + 1, 4), lax.rem(t + 3, 4), lax.rem(t + 2, 4)
    up_y, down_y, far_y = lax.rem(s + 1, 4), lax.rem(s + 3, 4), lax.rem(s + 2, 4)
    started = []
    slots = {}

    def slot(name):
        return slots.setdefault(name, len(slots))

    def remote(src, dst, name, where):
        return pltpu.make_async_remote_copy(
            src_ref=src, dst_ref=dst, send_sem=sx.at[slot(name)], recv_sem=rx.at[slot(name)],
            device_id=where, device_id_type=MESH,
        )

    def send(src, dst, name, where):
        copy = remote(src, dst, name, where)
        copy.start()
        started.append(copy)

    def arrived(dst, name):
        remote(dst, dst, name, {"tensor": right}).wait_recv()

    def context_peer(j):
        target = lax.rem(c + j, 16)
        return {"context_0": lax.div(target, 2), "context_1": lax.rem(target, 2)}

    def chip_peer(j):
        return {"context_0": lax.rem(z + j, 8)}

    def exchange(make, how_many=16):
        def go(j, carry):
            make(j).start()
            return carry

        lax.fori_loop(1, how_many, go, 0)

    def settle(make, how_many=16, received=True):
        def go(j, carry):
            if received:
                make(j).wait_recv()
            else:
                make(j).wait_send()
            return carry

        lax.fori_loop(1, how_many, go, 0)

    def tile(i):
        return pl.ds(pl.multiple_of(i * 128, 128), 128)

    barrier = pltpu.get_barrier_semaphore()

    def greet(j, carry):
        pl.semaphore_signal(barrier, inc=1, device_id=context_peer(j), device_id_type=MESH)
        return carry

    for j in range(1, 4):
        pl.semaphore_signal(barrier, inc=1, device_id={"tensor": lax.rem(t + j, 4)}, device_id_type=MESH)
        pl.semaphore_signal(barrier, inc=1, device_id={"fsdp": lax.rem(s + j, 4)}, device_id_type=MESH)
    lax.fori_loop(1, 16, greet, 0)
    before = lax.rem(c + 15, 16)
    after = lax.rem(c + 1, 16)

    @pl.when(c > 0)
    def _():
        pl.semaphore_signal(
            barrier, inc=1,
            device_id={"context_0": lax.div(before, 2), "context_1": lax.rem(before, 2), "tensor": 3},
            device_id_type=MESH,
        )

    def columns(p):
        return pl.ds(pl.multiple_of(p * WIDTH, WIDTH), WIDTH)

    def x_rows(p, first, count):
        return x_ext.at[pl.ds(pl.multiple_of(16 + p * ROWS + first, 16), count)]

    def z_rows(p, first, count):
        return gate.at[p, pl.ds(first, count)]

    def bc_rows(p, first, count):
        return bc_ext.at[pl.ds(pl.multiple_of(16 + p * ROWS + first, 16), count)]

    def w_part(rows_from, count, y):
        return wt.at[
            pl.ds(pl.multiple_of(rows_from, 64), count), pl.ds(pl.multiple_of(y * COLS, COLS), COLS)
        ]

    def dt_window(p):
        return dt_in.at[pl.ds(pl.multiple_of(8 * lax.div(5 * p, 2), 8), 24)]

    local = {}

    def copy_here(name, src, dst):
        local[name] = pltpu.make_async_copy(src, dst, sl.at[len(local)])
        local[name].start()

    copy_here("cot", cot_in, cot)
    copy_here("up", up_in, up)
    copy_here("step_bias", step_bias_in, head_par.at[0])
    copy_here("rate", rate_in, head_par.at[1])
    copy_here("skip", skip_in, head_par.at[2])
    copy_here("bc", bc_in, bc_rows(t, 0, ROWS))
    copy_here("dt", dt_window(t), dt_all.at[t])
    copy_here("taps_x", taps_in.at[:, columns(t)], taps_x)
    copy_here("taps_bc", taps_in.at[:, pl.ds(4 * WIDTH, 256)], taps_bc)
    copy_here("bias_x", bias_in.at[:, columns(t)], bias_x)
    copy_here("bias_bc", bias_in.at[:, pl.ds(4 * WIDTH, 256)], bias_bc)
    copy_here("x", x_in.at[:, columns(t)], x_rows(t, 0, ROWS))
    copy_here("gain", gain_in, gain)
    copy_here("down", down_in, down_t)
    copy_here("gate", z_in.at[:, columns(t)], gate.at[t])
    copy_here("w", w_in, w_part(0, 1280, s))

    def head_mask(i, carry):
        head = lax.broadcasted_iota(jnp.int32, (256, 128), 0)
        head = jnp.where(head >= 128, head - 128, head)
        lane = lax.broadcasted_iota(jnp.int32, (256, 128), 1)
        own_head = 2 * i + jnp.where(lane >= 64, 1, 0)
        spread[:, tile(i)] = jnp.where(head == own_head, 1.0, 0.0).astype(BF16)
        return carry

    lax.fori_loop(0, 10, head_mask, 0)

    def widen(v):
        high = v.astype(BF16)
        low = (v - high.astype(F32)).astype(BF16)
        return dot(jnp.concatenate([high, low], axis=1), spread[...])

    scale = 2.0 / (TOKENS ** 0.5)

    local["cot"].wait()
    local["up"].wait()
    gt[t] = dot(up[...], cot[...], NT) * scale

    gives_rim = jnp.logical_and(t == 3, c < 15)

    @pl.when(gives_rim)
    def _():
        pl.semaphore_wait(barrier, 25)

    @pl.when(jnp.logical_not(gives_rim))
    def _():
        pl.semaphore_wait(barrier, 21)

    def far_start(src, relay, name):
        send(src.at[pl.ds(0, 64), columns(far)], relay.at[0], name + "0", {"tensor": right})
        send(src.at[pl.ds(64, 64), columns(far)], relay.at[1], name + "1", {"tensor": left})

    def near_start(src, rows, name):
        send(src.at[:, columns(right)], rows(t, 0, ROWS), name + "2", {"tensor": right})
        send(src.at[:, columns(left)], rows(t, 0, ROWS), name + "3", {"tensor": left})

    def far_forward(rows, relay, name):
        arrived(relay.at[0], name + "0")
        send(relay.at[0], rows(left, 0, 64), name + "4", {"tensor": right})
        arrived(relay.at[1], name + "1")
        send(relay.at[1], rows(right, 64, 64), name + "5", {"tensor": left})

    def near_wait(rows, name):
        arrived(rows(left, 0, ROWS), name + "2")
        arrived(rows(right, 0, ROWS), name + "3")

    def far_wait(rows, name):
        arrived(rows(far, 0, 64), name + "4")
        arrived(rows(far, 64, 64), name + "5")

    far_start(x_in, xr, "x")
    send(bc_in.at[pl.ds(0, 64)], bc_rows(t, 0, 64), "b0", {"tensor": right})
    send(bc_in.at[pl.ds(64, 64)], bc_rows(t, 64, 64), "b1", {"tensor": left})
    send(bc_in.at[pl.ds(64, 64)], bc_rows(t, 64, 64), "b2", {"tensor": right})
    send(bc_in.at[pl.ds(0, 64)], bc_rows(t, 0, 64), "b3", {"tensor": left})
    for j in (1, 3, 2):
        peer = lax.rem(t + j, 4)
        send(dt_window(peer), dt_all.at[t], "dt%d" % j, {"tensor": peer})
    near_start(x_in, x_rows, "x")

    def rim_copies():
        copies = []
        for p in range(4):
            where = {"context_0": lax.div(after, 2), "context_1": lax.rem(after, 2), "tensor": p}
            copies.append(pltpu.make_async_remote_copy(
                src_ref=x_in.at[pl.ds(112, 16), pl.ds(p * WIDTH, WIDTH)], dst_ref=x_ext.at[pl.ds(0, 16)],
                send_sem=sl.at[16 + p], recv_sem=rx.at[slot("rim_x")], device_id=where, device_id_type=MESH))
            copies.append(pltpu.make_async_remote_copy(
                src_ref=bc_in.at[pl.ds(112, 16)], dst_ref=bc_ext.at[pl.ds(0, 16)],
                send_sem=sl.at[20 + p], recv_sem=rx.at[slot("rim_b")], device_id=where, device_id_type=MESH))
        return copies

    @pl.when(gives_rim)
    def _():
        for copy in rim_copies():
            copy.start()

    @pl.when(c == 0)
    def _():
        x_ext[0:16, :] = jnp.zeros((16, WIDTH), BF16)
        bc_ext[0:16, :] = jnp.zeros((16, 256), BF16)

    mine, other = k * 640, (1 - k) * 640

    def w_src(first):
        return w_in.at[pl.ds(pl.multiple_of(mine + first, 64), 320)]

    send(w_src(0), w_part(mine, 320, s), "w0", {"fsdp": up_y})
    send(w_src(320), w_part(mine + 320, 320, s), "w1", {"fsdp": down_y})
    send(w_src(320), w_part(mine + 320, 320, s), "w2", {"fsdp": up_y})
    send(w_src(0), w_part(mine, 320, s), "w3", {"fsdp": down_y})

    for name in ("step_bias", "rate", "skip", "bc", "dt", "taps_x", "taps_bc", "bias_x", "bias_bc", "x", "gain", "down"):
        local[name].wait()
    pick20 = jnp.where(
        lax.broadcasted_iota(jnp.int32, (HEADS, 128), 0) == lax.broadcasted_iota(jnp.int32, (HEADS, 128), 1), 1.0, 0.0)

    def head_row(i):
        return dot(jnp.broadcast_to(head_par[i], (8, HEADS)), pick20, precision=lax.Precision.HIGHEST)

    step_bias = head_row(0)[0:1, :]
    rate = jnp.exp(head_row(1))[0:1, :]
    skip[...] = widen(head_row(2))

    for j in range(1, 4):
        arrived(dt_all.at[lax.rem(t + 4 - j, 4)], "dt%d" % j)

    row = lax.broadcasted_iota(jnp.int32, (128, 128), 0)
    col = lax.broadcasted_iota(jnp.int32, (128, 128), 1)
    causal = row >= col
    tri = jnp.where(causal, 1.0, 0.0)
    pick_row = lax.broadcasted_iota(jnp.int32, (24, 128), 0)
    pick_col = lax.broadcasted_iota(jnp.int32, (24, 128), 1)
    hit = jnp.logical_and(pick_row == pick_col + 4 * lax.rem(t, 2), pick_col < HEADS)
    pick = jnp.where(hit, 1.0, 0.0).astype(BF16)

    total = jnp.zeros((1, 128), F32)
    for p in range(4):
        raw = dot(dt_all[p], pick, TN) + step_bias
        step_now = jnp.maximum(raw, 0.0) + jnp.log1p(jnp.exp(-jnp.abs(raw)))
        cum_now = dot(tri, -step_now * rate, precision=lax.Precision.HIGHEST)
        step[p] = step_now
        cum[p] = cum_now
        log_start[p] = jnp.broadcast_to(total, (8, 128))
        total = total + cum_now[127:128, :]
    for p in range(4):
        log_tail[p] = total - log_start[p] - cum[p, 127:128, :]
        kept[p] = widen(jnp.broadcast_to(jnp.exp(cum[p, 127:128, :]), (8, 128)))
    dec_all[c] = jnp.broadcast_to(jnp.exp(total), (8, 128))

    arrived(bc_rows(left, 0, 64), "b0")
    send(bc_rows(left, 0, 64), bc_rows(left, 0, 64), "b4", {"tensor": right})
    arrived(bc_rows(right, 64, 64), "b1")
    send(bc_rows(right, 64, 64), bc_rows(right, 64, 64), "b5", {"tensor": left})
    far_forward(x_rows, xr, "x")
    far_start(z_in, zr, "z")
    near_start(z_in, z_rows, "z")

    def decay_copy(j):
        return pltpu.make_async_remote_copy(
            src_ref=dec_all.at[c], dst_ref=dec_all.at[c],
            send_sem=sd.at[j], recv_sem=rd.at[j], device_id=context_peer(j), device_id_type=MESH)

    exchange(decay_copy)
    for j in range(1, 4):
        send(gt.at[t], gt.at[t], "g%d" % j, {"tensor": lax.rem(t + j, 4)})

    def convolved(ext, p, lanes, taps, bias):
        v = ext[pl.ds(pl.multiple_of(p * ROWS, 16), ROWS + 16), lanes].astype(F32)
        acc = bias[:, lanes] + taps[0:1, lanes] * pltpu.roll(v, 3, 0)
        acc = acc + taps[1:2, lanes] * pltpu.roll(v, 2, 0)
        acc = acc + taps[2:3, lanes] * pltpu.roll(v, 1, 0)
        acc = acc + taps[3:4, lanes] * v
        return silu(acc[16:]).astype(BF16)

    @pl.when(c > 0)
    def _():
        arrived(x_ext.at[pl.ds(0, 16)], "rim_x")
        arrived(bc_ext.at[pl.ds(0, 16)], "rim_b")

    state[...] = jnp.zeros((STATE, WIDTH), F32)

    def block(i, carry):
        p = lax.rem(t + i, 4)
        for half in range(2):
            bcc[p, :, pl.ds(half * 128, 128)] = convolved(bc_ext, p, pl.ds(half * 128, 128), taps_bc, bias_bc)

        def lanes_of(j, inner):
            xc[p, :, tile(j)] = convolved(x_ext, p, tile(j), taps_x, bias_x)
            return inner

        lax.fori_loop(0, 10, lanes_of, 0)
        cum_now = cum[p]
        weight = widen(step[p] * jnp.exp(cum_now[127:128, :] - cum_now))
        scaled = (xc[p].astype(F32) * weight).astype(BF16)
        fresh = dot(bcc[p, :, 0:128], scaled, TN)
        blocks[p] = fresh
        state[...] = state[...] + widen(jnp.exp(log_tail[p]))[0:1, :] * fresh
        return carry

    arrived(bc_rows(left, 64, 64), "b2")
    arrived(bc_rows(right, 0, 64), "b3")
    near_wait(x_rows, "x")
    lax.fori_loop(0, 2, block, 0)
    arrived(bc_rows(far, 0, 64), "b4")
    arrived(bc_rows(far, 64, 64), "b5")
    far_wait(x_rows, "x")
    lax.fori_loop(2, 4, block, 0)

    core = {"context_1": 1 - k}

    def half_lanes(i):
        return pl.ds(pl.multiple_of(i * 640, 640), 640)

    send(state.at[:, half_lanes(1 - k)], peer_state, "pair", core)
    settle(decay_copy)
    dec_wide[...] = widen(dec_all[...].reshape(128, 128))
    arrived(peer_state, "pair")

    def chip_decay(of):
        return dec_wide[pl.ds(pl.multiple_of(16 * of, 16), 8), half_lanes(k)] * dec_wide[
            pl.ds(pl.multiple_of(16 * of + 8, 8), 8), half_lanes(k)]

    decay_second = dec_wide[pl.ds(pl.multiple_of(16 * z + 8, 8), 8), half_lanes(k)][0:1, :]
    weight_mine = jnp.where(k == 0, decay_second, jnp.ones_like(decay_second))
    weight_peer = jnp.where(k == 0, jnp.ones_like(decay_second), decay_second)

    def pack_state(i, carry):
        rows = pl.ds(pl.multiple_of(i * 16, 16), 16)
        both = weight_mine * state[rows, half_lanes(k)] + weight_peer * peer_state[rows, :]
        st_send[i] = both.astype(BF16)
        return carry

    lax.fori_loop(0, 8, pack_state, 0)

    def state_copy(j):
        return pltpu.make_async_remote_copy(
            src_ref=st_send.at[lax.rem(z + j, 8)], dst_ref=st_recv.at[z],
            send_sem=sc.at[j], recv_sem=rc_.at[j], device_id=chip_peer(j), device_id_type=MESH)

    exchange(state_copy, 8)
    st_recv[z] = st_send[z]

    arrived(w_part(mine, 320, down_y), "w0")
    send(w_part(mine, 320, down_y), w_part(mine, 320, down_y), "w4", {"fsdp": up_y})
    arrived(w_part(mine + 320, 320, up_y), "w1")
    send(w_part(mine + 320, 320, up_y), w_part(mine + 320, 320, up_y), "w5", {"fsdp": down_y})
    far_forward(z_rows, zr, "z")

    def inside(p, carry):
        b_now, c_now = bcc[p, :, 0:128], bcc[p, :, 128:256]
        gram = dot(c_now, b_now, NT)
        cum_now = cum[p]
        shifted = (cum_now - jnp.log(step[p])).T
        lane = lax.broadcasted_iota(jnp.int32, (1, 128), 1)
        low = jnp.where(lane < 64, 1.0, 0.0)
        for q in range(HEADS // 2):
            mats = []
            for h in (2 * q, 2 * q + 1):
                gap = cum_now[:, h : h + 1] - shifted[h : h + 1, :]
                mats.append(jnp.exp(jnp.where(causal, gap, -1e30)) * gram)
            both = jnp.concatenate(mats, axis=1).astype(BF16)
            x_pair = xc[p, :, pl.ds(q * 128, 128)].astype(F32)
            x_two = jnp.concatenate([x_pair * low, x_pair * (1.0 - low)], axis=0).astype(BF16)
            y_in[p, :, pl.ds(q * 128, 128)] = dot(both, x_two) + x_pair * skip[0:1, pl.ds(q * 128, 128)]
        return carry

    lax.fori_loop(0, 4, inside, 0)

    settle(state_copy, 8)

    def chain(i, held):
        back_send[i] = held.astype(BF16)
        return chip_decay(i)[0:1, :] * held + st_recv[i].astype(F32)

    lax.fori_loop(0, 8, chain, jnp.zeros((16, 640), F32))

    def back_copy(j):
        return pltpu.make_async_remote_copy(
            src_ref=back_send.at[lax.rem(z + j, 8)], dst_ref=back_recv.at[z],
            send_sem=sb.at[j], recv_sem=rb.at[j], device_id=chip_peer(j), device_id_type=MESH)

    exchange(back_copy, 8)
    back_recv[z] = back_send[z]

    def starts(j, carry):
        held = jnp.zeros((STATE, 128), F32)
        for p in range(4):
            fresh = blocks[p, :, tile(j)]
            blocks[p, :, tile(j)] = held
            held = kept[p, 0:1, tile(j)] * held + fresh
        return carry

    lax.fori_loop(0, 10, starts, 0)

    arrived(w_part(mine + 320, 320, down_y), "w2")
    send(w_part(mine, 640, down_y), w_part(mine, 640, down_y), "w6", core)
    arrived(w_part(mine, 320, up_y), "w3")
    send(w_part(mine, 640, up_y), w_part(mine, 640, up_y), "w7", core)
    arrived(w_part(mine, 320, far_y), "w4")
    arrived(w_part(mine + 320, 320, far_y), "w5")
    send(w_part(mine, 640, far_y), w_part(mine, 640, far_y), "w8", core)

    local["gate"].wait()
    near_wait(z_rows, "z")
    far_wait(z_rows, "z")
    settle(back_copy, 8)

    decay_first = dec_wide[pl.ds(pl.multiple_of(16 * z, 8), 8), half_lanes(k)][0:1, :]

    def unpack_state(i, carry):
        rows = pl.ds(pl.multiple_of(i * 16, 16), 16)
        first = back_recv[i].astype(F32)
        span = jnp.where(k == 0, state[rows, half_lanes(k)], peer_state[rows, :])
        second = decay_first * first + span
        s_in[rows, half_lanes(k)] = jnp.where(k == 0, first, second)
        in_send[rows, :] = jnp.where(k == 0, second, first).astype(BF16)
        return carry

    lax.fori_loop(0, 8, unpack_state, 0)
    send(in_send, in_recv, "in", core)

    local["w"].wait()
    arrived(w_part(other, 640, down_y), "w6")
    arrived(w_part(other, 640, up_y), "w7")
    arrived(w_part(other, 640, far_y), "w8")
    arrived(in_recv, "in")
    s_in[:, half_lanes(1 - k)] = in_recv[...].astype(F32)

    def finish(i, carry):
        p = lax.rem(t + i, 4)
        start = blocks[p] + widen(jnp.exp(log_start[p]))[0:1, :] * s_in[...]
        reach = widen(jnp.exp(cum[p]))
        y_now = y_in[p] + reach * dot(bcc[p, :, 128:256], start.astype(BF16))
        now = y_now * silu(gate[p].astype(F32))
        squares = (now * now).astype(BF16)
        sq[t, p] = dot(jnp.ones((8, WIDTH), BF16), squares, NT)
        out = (now * gain[...]).astype(BF16)
        gated[p] = out
        ap_send[p] = dot(down_t[...], out, NT)
        return carry

    def project(p, half, store, first=0, count=5):
        def piece(i, carry):
            lanes = pl.ds(pl.multiple_of(i * 256, 256), 256)
            lanes_w = pl.ds(pl.multiple_of(half * HALF + i * 256, 256), 256)
            store(lanes, dot(gated[p], wt[:, lanes_w]))
            return carry

        lax.fori_loop(first, first + count, piece, 0)

    def to_slot(which, extra=None):
        def store(lanes, v):
            if extra is not None:
                v = v + rs_recv[extra, :, lanes].astype(F32)
            rs_send[which, :, lanes] = v.astype(BF16)

        return store

    def ship(which, where, first=0, count=5):
        part = pl.ds(first * 256, count * 256)
        send(rs_send.at[which, :, part], rs_recv.at[which, :, part], "r%d_%d" % (which, first), {"tensor": where})

    def landed(which, first=0, count=5):
        arrived(rs_recv.at[which, :, pl.ds(first * 256, count * 256)], "r%d_%d" % (which, first))

    lax.fori_loop(2, 3, finish, 0)
    project(far, 0, to_slot(0))
    ship(0, right)
    project(far, 1, to_slot(1))
    ship(1, left)
    lax.fori_loop(3, 6, finish, 0)
    ap_recv[t] = ap_send[t]
    for j in range(1, 4):
        peer = lax.rem(t + j, 4)
        send(sq.at[t], sq.at[t], "q%d" % j, {"tensor": peer})
        send(ap_send.at[peer], ap_recv.at[t], "a%d" % j, {"tensor": peer})
    project(right, 1, to_slot(2))
    ship(2, right)
    project(left, 0, to_slot(3))
    ship(3, left)

    for j in range(1, 4):
        source = lax.rem(t + 4 - j, 4)
        arrived(gt.at[source], "g%d" % j)
        arrived(sq.at[source], "q%d" % j)
        arrived(ap_recv.at[source], "a%d" % j)

    def row_scale(p):
        squares = (sq[0, p] + sq[1, p]) + (sq[2, p] + sq[3, p])
        return lax.rsqrt(squares * (1.0 / 5120.0) + EPS)

    adapter = ((ap_recv[0] + ap_recv[1]) + (ap_recv[2] + ap_recv[3])).astype(BF16)
    own_scale = row_scale(t)
    weighted = (scale * own_scale[0:1, :] * adapter.astype(F32)).astype(BF16)
    grad_a_now = jnp.zeros((RANK, WIDTH), F32)
    for p in range(4):
        rows_grad = (row_scale(p)[0:1, :] * gt[p]).astype(BF16)
        grad_a_now = grad_a_now + dot(rows_grad, gated[p])
    grad_b_now = dot(weighted, cot[...])
    for i in range(30):
        v_send[i // 2, i % 2] = (
            grad_a_now[:, i * 128 : i * 128 + 128] if i < 10
            else grad_b_now[:, (i - 10) * 128 : (i - 10) * 128 + 128]).astype(BF16)
    v_send[15] = jnp.zeros((2, RANK, 128), BF16)
    v_recv[c] = v_send[c]

    def v_copy(j):
        return pltpu.make_async_remote_copy(
            src_ref=v_send.at[lax.rem(c + j, 16)], dst_ref=v_recv.at[c],
            send_sem=sv.at[j], recv_sem=rv.at[j], device_id=context_peer(j), device_id_type=MESH)

    exchange(v_copy)

    landed(0)
    project(right, 0, to_slot(4, 0), 0, 3)
    ship(4, right, 0, 3)
    landed(1)
    project(left, 1, to_slot(5, 1), 0, 3)
    ship(5, left, 0, 3)

    settle(v_copy)

    def add_v(i, held):
        return held + v_recv[i].astype(F32)

    y_recv[s] = lax.fori_loop(0, 16, add_v, jnp.zeros((2, RANK, 128), F32))
    for j in range(1, 4):
        send(y_recv.at[s], y_recv.at[s], "y%d" % j, {"fsdp": lax.rem(s + j, 4)})
    project(right, 0, to_slot(4, 0), 3, 2)
    project(left, 1, to_slot(5, 1), 3, 2)
    for j in range(1, 4):
        arrived(y_recv.at[lax.rem(s + 4 - j, 4)], "y%d" % j)
    t_recv[t] = ((y_recv[0] + y_recv[1]) + (y_recv[2] + y_recv[3])).astype(BF16)
    for j in range(1, 4):
        send(t_recv.at[t], t_recv.at[t], "t%d" % j, {"tensor": lax.rem(t + j, 4)})
    ship(4, right, 3, 2)
    ship(5, left, 3, 2)

    def own_part(half):
        def store(lanes, v):
            lanes_up = pl.ds(pl.multiple_of(half * HALF + lanes.start, 256), 256)
            own[half, :, lanes] = v + 2.0 * dot(adapter, up[:, lanes_up], TN)

        return store

    project(t, 0, own_part(0))
    project(t, 1, own_part(1))

    for j in range(1, 4):
        arrived(t_recv.at[lax.rem(t + 4 - j, 4)], "t%d" % j)

    def add_t(i, held):
        keep = jnp.where(jnp.logical_or(c >= 5, i == t), 1.0, 0.0)
        return held + keep * t_recv[i].astype(F32)

    v_all[c] = lax.fori_loop(0, 4, add_t, jnp.zeros((2, RANK, 128), F32)).astype(BF16)

    def all_copy(j):
        return pltpu.make_async_remote_copy(
            src_ref=v_all.at[c], dst_ref=v_all.at[c],
            send_sem=sg.at[j], recv_sem=rg.at[j], device_id=context_peer(j), device_id_type=MESH)

    exchange(all_copy)

    landed(2)
    landed(3)
    landed(4, 0, 3)
    landed(5, 0, 3)
    landed(4, 3, 2)
    landed(5, 3, 2)
    scale_col = jnp.broadcast_to(own_scale[0:1, :], (128, 128)).T

    def close(i, carry):
        lanes = tile(i)
        first = own[0, :, lanes] + rs_recv[4, :, lanes].astype(F32) + rs_recv[3, :, lanes].astype(F32)
        second = own[1, :, lanes] + rs_recv[2, :, lanes].astype(F32) + rs_recv[5, :, lanes].astype(F32)
        mixed[:, lanes] = (scale_col * first).astype(BF16)
        mixed[:, pl.ds(pl.multiple_of(HALF + i * 128, 128), 128)] = (scale_col * second).astype(BF16)
        return carry

    lax.fori_loop(0, 10, close, 0)

    settle(all_copy)
    for i in range(10):
        grad_a[:, i * 128 : i * 128 + 128] = v_all[i // 2, i % 2].astype(F32)
    for i in range(20):
        grad_b[:, i * 128 : i * 128 + 128] = v_all[5 + i // 2, i % 2].astype(F32)

    for make, how_many in (
        (decay_copy, 16), (state_copy, 8), (back_copy, 8), (v_copy, 16), (all_copy, 16)
    ):
        settle(make, how_many, received=False)
    for copy in started:
        copy.wait_send()

    @pl.when(gives_rim)
    def _():
        for copy in rim_copies():
            copy.wait_send()


def shards(
    input_raw, state_proj_raw, gate_branch, step_raw, convolution_taps, convolution_bias, step_bias,
    decay_log_rate, skip_weight, gated_norm_gain, output_weight, adapter_down, adapter_up, cotangent,
):
    hbm = pl.BlockSpec(memory_space=pl.ANY)
    vmem = pl.BlockSpec(memory_space=pltpu.VMEM)
    dma = pltpu.SemaphoreType.DMA
    mixed, grad_a, grad_b = pl.pallas_call(
        kernel,
        out_shape=(
            jax.ShapeDtypeStruct((ROWS, OUT), BF16),
            jax.ShapeDtypeStruct((RANK, WIDTH), F32),
            jax.ShapeDtypeStruct((RANK, OUT), F32),
        ),
        in_specs=[hbm] * 14,
        out_specs=(vmem, vmem, vmem),
        scratch_shapes=[
            pltpu.VMEM((16 + 512, WIDTH), BF16),
            pltpu.VMEM((2, 64, WIDTH), BF16),
            pltpu.VMEM((4, ROWS, WIDTH), BF16),
            pltpu.VMEM((16 + 512, 256), BF16),
            pltpu.VMEM((4, ROWS, 256), BF16),
            pltpu.VMEM((4, 24, 128), BF16),
            pltpu.VMEM((4, ROWS, WIDTH), BF16),
            pltpu.VMEM((2, 64, WIDTH), BF16),
            pltpu.VMEM((WIDTH, OUT), BF16),
            pltpu.VMEM((ROWS, OUT), BF16),
            pltpu.VMEM((4, WIDTH), F32),
            pltpu.VMEM((4, 256), F32),
            pltpu.VMEM((1, WIDTH), F32),
            pltpu.VMEM((1, 256), F32),
            pltpu.VMEM((3, 1, HEADS), F32),
            pltpu.VMEM((1, WIDTH), F32),
            pltpu.VMEM((RANK, WIDTH), BF16),
            pltpu.VMEM((RANK, OUT), BF16),
            pltpu.VMEM((8, WIDTH), F32),
            pltpu.VMEM((256, WIDTH), BF16),
            pltpu.VMEM((4, ROWS, 128), F32),
            pltpu.VMEM((4, ROWS, 128), F32),
            pltpu.VMEM((4, 8, 128), F32),
            pltpu.VMEM((4, 8, 128), F32),
            pltpu.VMEM((4, ROWS, WIDTH), F32),
            pltpu.VMEM((4, STATE, WIDTH), F32),
            pltpu.VMEM((4, 8, WIDTH), F32),
            pltpu.VMEM((STATE, WIDTH), F32),
            pltpu.VMEM((STATE, 640), F32),
            pltpu.VMEM((8, 16, 640), BF16),
            pltpu.VMEM((8, 16, 640), BF16),
            pltpu.VMEM((16, 8, 128), F32),
            pltpu.VMEM((128, WIDTH), F32),
            pltpu.VMEM((8, 16, 640), BF16),
            pltpu.VMEM((8, 16, 640), BF16),
            pltpu.VMEM((STATE, 640), BF16),
            pltpu.VMEM((STATE, 640), BF16),
            pltpu.VMEM((STATE, WIDTH), F32),
            pltpu.VMEM((4, ROWS, WIDTH), BF16),
            pltpu.VMEM((4, RANK, 128), F32),
            pltpu.VMEM((4, 4, 8, 128), F32),
            pltpu.VMEM((4, RANK, 128), F32),
            pltpu.VMEM((4, RANK, 128), F32),
            pltpu.VMEM((6, ROWS, HALF), BF16),
            pltpu.VMEM((6, ROWS, HALF), BF16),
            pltpu.VMEM((2, ROWS, HALF), F32),
            pltpu.VMEM((16, 2, RANK, 128), BF16),
            pltpu.VMEM((16, 2, RANK, 128), BF16),
            pltpu.VMEM((4, 2, RANK, 128), F32),
            pltpu.VMEM((4, 2, RANK, 128), BF16),
            pltpu.VMEM((16, 2, RANK, 128), BF16),
            dma((72,)), dma((72,)), dma((24,)),
            dma((8,)), dma((8,)), dma((16,)), dma((16,)), dma((8,)), dma((8,)),
            dma((16,)), dma((16,)), dma((16,)), dma((16,)),
        ],
        compiler_params=pltpu.CompilerParams(
            collective_id=0, has_side_effects=True, vmem_limit_bytes=64 * 1000 * 1000),
    )(
        input_raw[0], state_proj_raw[0], gate_branch[0], step_raw[0].T, output_weight, cotangent[0],
        convolution_taps, convolution_bias[None, :], step_bias[None, :], decay_log_rate[None, :],
        skip_weight[None, :], gated_norm_gain[None, :], adapter_down.T, adapter_up,
    )
    return (mixed[None], grad_a.T, grad_b)


def solution(mesh):
    torus = Mesh(
        mesh.devices.reshape(8, 2, mesh.shape["tensor"], mesh.shape["fsdp"]),
        ("context_0", "context_1", "tensor", "fsdp"),
    )
    tokens = P("fsdp", CONTEXT_TENSOR, None)
    return jax.shard_map(
        shards,
        mesh=torus,
        in_specs=(
            tokens, tokens, tokens, tokens, P(), P(), P("tensor"), P("tensor"), P("tensor"), P("tensor"),
            P("tensor", "fsdp"), P("tensor", None), P(), tokens,
        ),
        out_specs=(tokens, P("tensor", None), P()),
        check_vma=False,
    )
```

time: 116 us -> 94.2 us (0.81)
  Pallas kernels: 104 us -> 87.3 us
  local copies, waits for them, and re-layouts: 9.67 us -> 5.97 us
  other arithmetic: 1.56 us -> 0 us
    pallas_call x1, Pallas kernels: 104 us -> 87.3 us  [shards(): pl.pallas_call(kernel, out_shape=(jax.ShapeDtypeStruct((ROWS, OUT), BF16)...]
    pad x4 -> x0, local copies, waits for them, and re-layouts: 2.03 us -> none  [line(): return jnp.pad(v, (0, WIDTH + 256 - v.shape[0]))[None, :]]
    concatenate x2 -> x0, other arithmetic: 1.56 us -> none  [the longest x1 0.81 us: shards(): jnp.concatenate([convolution_taps, convolution_bias[None, :]], axis=0)]
    unnamed x8 -> x7, local copies, waits for them, and re-layouts: 4.76 us -> 3.32 us
    concatenate x1 -> x0, local copies, waits for them, and re-layouts: 1.3 us -> none  [shards(): jnp.concatenate([conv, line(gated_norm_gain), line(jnp.repeat(skip_weight...]
where the time goes in v2:
time: 94.2 us; the launch traced here: 94 us
  Pallas kernels  87.3 us (93%)
  local copies, waits for them, and re-layouts  5.97 us (6%)
    pallas_call x1, Pallas kernels, shards(): pl.pallas_call(kernel, out_shape=(jax.ShapeDtypeStruct((ROWS, OUT), BF16)...  87.3 us
    unnamed x7, local copies, waits for them, and re-layouts  3.32 us

profile of v2, /device:TPU:1, one launch (start us, length us, event | category | flops | bytes accessed | tf_op | source)
XLA Modules:
  0.0 94.0 jit_solution(12345344836139772478)
XLA Ops:
  0.6 1.3 %broadcast_in_dim.22.gain_in = f32[1,1280]{1,0:T(1,128)} reshape(f32[1280]{0:T(1024)} %param.23) | data formatting | bytes 10240 | tf_op jit(solution)/shard_map/broadcast_in_dim | solution.py:730
  1.9 1.4 %broadcast_in_dim.18.bias_in = f32[1,5376]{1,0:T(1,128)} reshape(f32[5376]{0:T(1024)} %param.19) | data formatting | bytes 43008 | tf_op jit(solution)/shard_map/broadcast_in_dim | solution.py:729
  3.3 87.3 %shard_map.157 = (bf16[128,2560]{1,0:T(8,128)(2,1)}, f32[16,1280]{1,0:T(8,128)}, f32[16,2560]{1,0:T(8,128)}) custom-call(bf16[128,5120]{1,0:T(8,128)(2,1)} %bitcast.13, bf16[128,256]{1,0:T(8,128)(2,1)} %bitcast.18, bf16[128,5120]{1,0:T(8,128)(2,1)} %bitcast.14, bf16[80,128]{1,0:T(8,128)(2,1)} %bitcast.20, bf16[1280,640]{1,0:T(8,128)(2,1)} %w_in.1, ...), custom_call_target="tpu_custom_call" | custom-call | tf_op jit(solution)/shard_map/pallas_call | solution.py:660
  90.6 0.0 copy-start.1
  90.6 0.0 copy-start
  90.7 2.0 %copy.20 = bf16[1,128,2560]{2,1,0:T(8,128)(2,1)} copy(bf16[1,128,2560]{2,1,0:T(8,128)(2,1)} %bitcast.15) | data formatting | bytes 1310720
  92.7 0.0 copy-done.1
  92.7 0.6 copy.21
  93.3 0.0 copy-done
  93.3 0.7 copy.22
Async XLA Ops:
  90.6 2.0 %copy-start.1 = (f32[16,1280]{1,0:T(8,128)S(1)}, f32[16,1280]{1,0:T(8,128)}, u32[]{:S(2)}) copy-start(f32[16,1280]{1,0:T(8,128)} %get-tuple-element.7) | copy-start | bytes 245764
  90.6 2.7 %copy-start = (f32[16,2560]{1,0:T(8,128)S(1)}, f32[16,2560]{1,0:T(8,128)}, u32[]{:S(2)}) copy-start(f32[16,2560]{1,0:T(8,128)} %get-tuple-element.14) | copy-start | bytes 491524

commit v3 on v2

--- a/solution.py
+++ b/solution.py
@@ -41,12 +41,12 @@
     x_in, bc_in, z_in, dt_in, w_in, cot_in, taps_in, bias_in, step_bias_in, rate_in, skip_in, gain_in, down_in, up_in,
     mixed, grad_a, grad_b,
     x_ext, xr, xc, bc_ext, bcc, dt_all, gate, zr, wt, cot,
-    taps_x, taps_bc, bias_x, bias_bc, head_par, gain, down_t, up, skip,
+    taps_x, taps_bc, bias, head_par, gain_rows, gain, down_t, up, skip, weights, tails,
     spread, step, cum, log_start, log_tail, y_in, blocks, kept, state, peer_state,
     st_send, st_recv, dec_all, dec_wide, back_send, back_recv, in_send, in_recv, s_in,
     gated, gt, sq, ap_send, ap_recv,
     rs_send, rs_recv, own,
-    v_send, v_recv, y_recv, t_recv, v_all,
+    v_send, v_recv, y_recv, t_recv, v_all, mixed_here, a_here, b_here,
     sx, rx, sl, sc, rc_, sd, rd, sb, rb, sv, rv, sg, rg,
 ):
     z, k = lax.axis_index("context_0"), lax.axis_index("context_1")
@@ -74,12 +74,21 @@
     def arrived(dst, name):
         remote(dst, dst, name, {"tensor": right}).wait_recv()
 
+    def chip_at(i):
+        step_now = lax.div(i + 1, 2)
+        return lax.rem(z + 4 + (1 - 2 * lax.rem(i, 2)) * step_now, 8)
+
+    def core_at(j):
+        return lax.rem(k + j, 2)
+
+    def context_index(j):
+        return 2 * chip_at(lax.div(j - 1, 2)) + core_at(j)
+
     def context_peer(j):
-        target = lax.rem(c + j, 16)
-        return {"context_0": lax.div(target, 2), "context_1": lax.rem(target, 2)}
+        return {"context_0": chip_at(lax.div(j - 1, 2)), "context_1": core_at(j)}
 
     def chip_peer(j):
-        return {"context_0": lax.rem(z + j, 8)}
+        return {"context_0": chip_at(j - 1)}
 
     def exchange(make, how_many=16):
         def go(j, carry):
@@ -145,7 +154,7 @@
     local = {}
 
     def copy_here(name, src, dst):
-        local[name] = pltpu.make_async_copy(src, dst, sl.at[len(local)])
+        local[name] = pltpu.make_async_copy(src, dst, sl.at[8 + len(local)])
         local[name].start()
 
     copy_here("cot", cot_in, cot)
@@ -157,10 +166,9 @@
     copy_here("dt", dt_window(t), dt_all.at[t])
     copy_here("taps_x", taps_in.at[:, columns(t)], taps_x)
     copy_here("taps_bc", taps_in.at[:, pl.ds(4 * WIDTH, 256)], taps_bc)
-    copy_here("bias_x", bias_in.at[:, columns(t)], bias_x)
-    copy_here("bias_bc", bias_in.at[:, pl.ds(4 * WIDTH, 256)], bias_bc)
+    copy_here("bias", bias_in, bias)
     copy_here("x", x_in.at[:, columns(t)], x_rows(t, 0, ROWS))
-    copy_here("gain", gain_in, gain)
+    copy_here("gain", gain_in, gain_rows)
     copy_here("down", down_in, down_t)
     copy_here("gate", z_in.at[:, columns(t)], gate.at[t])
     copy_here("w", w_in, w_part(0, 1280, s))
@@ -234,10 +242,10 @@
             where = {"context_0": lax.div(after, 2), "context_1": lax.rem(after, 2), "tensor": p}
             copies.append(pltpu.make_async_remote_copy(
                 src_ref=x_in.at[pl.ds(112, 16), pl.ds(p * WIDTH, WIDTH)], dst_ref=x_ext.at[pl.ds(0, 16)],
-                send_sem=sl.at[16 + p], recv_sem=rx.at[slot("rim_x")], device_id=where, device_id_type=MESH))
+                send_sem=sl.at[p], recv_sem=rx.at[slot("rim_x")], device_id=where, device_id_type=MESH))
             copies.append(pltpu.make_async_remote_copy(
                 src_ref=bc_in.at[pl.ds(112, 16)], dst_ref=bc_ext.at[pl.ds(0, 16)],
-                send_sem=sl.at[20 + p], recv_sem=rx.at[slot("rim_b")], device_id=where, device_id_type=MESH))
+                send_sem=sl.at[4 + p], recv_sem=rx.at[slot("rim_b")], device_id=where, device_id_type=MESH))
         return copies
 
     @pl.when(gives_rim)
@@ -260,7 +268,7 @@
     send(w_src(320), w_part(mine + 320, 320, s), "w2", {"fsdp": up_y})
     send(w_src(0), w_part(mine, 320, s), "w3", {"fsdp": down_y})
 
-    for name in ("step_bias", "rate", "skip", "bc", "dt", "taps_x", "taps_bc", "bias_x", "bias_bc", "x", "gain", "down"):
+    for name in ("step_bias", "rate", "skip", "bc", "dt", "taps_x", "taps_bc", "bias", "x", "gain", "down"):
         local[name].wait()
     pick20 = jnp.where(
         lax.broadcasted_iota(jnp.int32, (HEADS, 128), 0) == lax.broadcasted_iota(jnp.int32, (HEADS, 128), 1), 1.0, 0.0)
@@ -271,6 +279,8 @@
     step_bias = head_row(0)[0:1, :]
     rate = jnp.exp(head_row(1))[0:1, :]
     skip[...] = widen(head_row(2))
+    for i in range(10):
+        gain[:, i * 128 : i * 128 + 128] = gain_rows[i : i + 1, :]
 
     for j in range(1, 4):
         arrived(dt_all.at[lax.rem(t + 4 - j, 4)], "dt%d" % j)
@@ -315,9 +325,9 @@
     for j in range(1, 4):
         send(gt.at[t], gt.at[t], "g%d" % j, {"tensor": lax.rem(t + j, 4)})
 
-    def convolved(ext, p, lanes, taps, bias):
+    def convolved(ext, p, lanes, taps, bias_row):
         v = ext[pl.ds(pl.multiple_of(p * ROWS, 16), ROWS + 16), lanes].astype(F32)
-        acc = bias[:, lanes] + taps[0:1, lanes] * pltpu.roll(v, 3, 0)
+        acc = bias[pl.ds(bias_row, 1), :] + taps[0:1, lanes] * pltpu.roll(v, 3, 0)
         acc = acc + taps[1:2, lanes] * pltpu.roll(v, 2, 0)
         acc = acc + taps[2:3, lanes] * pltpu.roll(v, 1, 0)
         acc = acc + taps[3:4, lanes] * v
@@ -333,21 +343,26 @@
     def block(i, carry):
         p = lax.rem(t + i, 4)
         for half in range(2):
-            bcc[p, :, pl.ds(half * 128, 128)] = convolved(bc_ext, p, pl.ds(half * 128, 128), taps_bc, bias_bc)
+            bcc[p, :, pl.ds(half * 128, 128)] = convolved(bc_ext, p, pl.ds(half * 128, 128), taps_bc, 40 + half)
 
         def lanes_of(j, inner):
-            xc[p, :, tile(j)] = convolved(x_ext, p, tile(j), taps_x, bias_x)
+            xc[p, :, tile(j)] = convolved(x_ext, p, tile(j), taps_x, 10 * t + j)
             return inner
 
         lax.fori_loop(0, 10, lanes_of, 0)
-        cum_now = cum[p]
-        weight = widen(step[p] * jnp.exp(cum_now[127:128, :] - cum_now))
-        scaled = (xc[p].astype(F32) * weight).astype(BF16)
+        scaled = (xc[p].astype(F32) * weights[p]).astype(BF16)
         fresh = dot(bcc[p, :, 0:128], scaled, TN)
         blocks[p] = fresh
-        state[...] = state[...] + widen(jnp.exp(log_tail[p]))[0:1, :] * fresh
-        return carry
-
+        state[...] = state[...] + tails[p, 0:1, :] * fresh
+        return carry
+
+    def weigh(p, carry):
+        cum_now = cum[p]
+        weights[p] = widen(step[p] * jnp.exp(cum_now[127:128, :] - cum_now))
+        tails[p] = widen(jnp.exp(log_tail[p]))
+        return carry
+
+    lax.fori_loop(0, 4, weigh, 0)
     arrived(bc_rows(left, 64, 64), "b2")
     arrived(bc_rows(right, 0, 64), "b3")
     near_wait(x_rows, "x")
@@ -385,7 +400,7 @@
 
     def state_copy(j):
         return pltpu.make_async_remote_copy(
-            src_ref=st_send.at[lax.rem(z + j, 8)], dst_ref=st_recv.at[z],
+            src_ref=st_send.at[chip_at(j - 1)], dst_ref=st_recv.at[z],
             send_sem=sc.at[j], recv_sem=rc_.at[j], device_id=chip_peer(j), device_id_type=MESH)
 
     exchange(state_copy, 8)
@@ -427,7 +442,7 @@
 
     def back_copy(j):
         return pltpu.make_async_remote_copy(
-            src_ref=back_send.at[lax.rem(z + j, 8)], dst_ref=back_recv.at[z],
+            src_ref=back_send.at[chip_at(j - 1)], dst_ref=back_recv.at[z],
             send_sem=sb.at[j], recv_sem=rb.at[j], device_id=chip_peer(j), device_id_type=MESH)
 
     exchange(back_copy, 8)
@@ -484,7 +499,7 @@
         y_now = y_in[p] + reach * dot(bcc[p, :, 128:256], start.astype(BF16))
         now = y_now * silu(gate[p].astype(F32))
         squares = (now * now).astype(BF16)
-        sq[t, p] = dot(jnp.ones((8, WIDTH), BF16), squares, NT)
+        sq[t, pl.ds(p, 1), :] = dot(jnp.ones((8, WIDTH), BF16), squares, NT)[0:1, :]
         out = (now * gain[...]).astype(BF16)
         gated[p] = out
         ap_send[p] = dot(down_t[...], out, NT)
@@ -507,28 +522,36 @@
 
         return store
 
-    def ship(which, where, first=0, count=5):
-        part = pl.ds(first * 256, count * 256)
-        send(rs_send.at[which, :, part], rs_recv.at[which, :, part], "r%d_%d" % (which, first), {"tensor": where})
-
-    def landed(which, first=0, count=5):
-        arrived(rs_recv.at[which, :, pl.ds(first * 256, count * 256)], "r%d_%d" % (which, first))
+    def piece_at(ref, which, i):
+        return ref.at[which, :, pl.ds(i * 256, 256)]
+
+    def ship(which, where, i):
+        send(piece_at(rs_send, which, i), piece_at(rs_recv, which, i), "r%d_%d" % (which, i), {"tensor": where})
+
+    def landed(which, i):
+        arrived(piece_at(rs_recv, which, i), "r%d_%d" % (which, i))
 
     lax.fori_loop(2, 3, finish, 0)
-    project(far, 0, to_slot(0))
-    ship(0, right)
-    project(far, 1, to_slot(1))
-    ship(1, left)
+    for i in range(5):
+        project(far, 0, to_slot(0), i, 1)
+        project(far, 1, to_slot(1), i, 1)
+        if i < 3:
+            ship(0, right, i)
+            ship(1, left, i)
     lax.fori_loop(3, 6, finish, 0)
     ap_recv[t] = ap_send[t]
-    for j in range(1, 4):
+    for j in (2, 1, 3):
         peer = lax.rem(t + j, 4)
         send(sq.at[t], sq.at[t], "q%d" % j, {"tensor": peer})
         send(ap_send.at[peer], ap_recv.at[t], "a%d" % j, {"tensor": peer})
-    project(right, 1, to_slot(2))
-    ship(2, right)
-    project(left, 0, to_slot(3))
-    ship(3, left)
+    for i in range(3, 5):
+        ship(0, right, i)
+        ship(1, left, i)
+    for i in range(5):
+        project(right, 1, to_slot(2), i, 1)
+        ship(2, right, i)
+        project(left, 0, to_slot(3), i, 1)
+        ship(3, left, i)
 
     for j in range(1, 4):
         source = lax.rem(t + 4 - j, 4)
@@ -537,7 +560,8 @@
         arrived(ap_recv.at[source], "a%d" % j)
 
     def row_scale(p):
-        squares = (sq[0, p] + sq[1, p]) + (sq[2, p] + sq[3, p])
+        rows = pl.ds(p, 1)
+        squares = (sq[0, rows, :] + sq[1, rows, :]) + (sq[2, rows, :] + sq[3, rows, :])
         return lax.rsqrt(squares * (1.0 / 5120.0) + EPS)
 
     adapter = ((ap_recv[0] + ap_recv[1]) + (ap_recv[2] + ap_recv[3])).astype(BF16)
@@ -557,17 +581,18 @@
 
     def v_copy(j):
         return pltpu.make_async_remote_copy(
-            src_ref=v_send.at[lax.rem(c + j, 16)], dst_ref=v_recv.at[c],
+            src_ref=v_send.at[context_index(j)], dst_ref=v_recv.at[c],
             send_sem=sv.at[j], recv_sem=rv.at[j], device_id=context_peer(j), device_id_type=MESH)
 
     exchange(v_copy)
 
-    landed(0)
-    project(right, 0, to_slot(4, 0), 0, 3)
-    ship(4, right, 0, 3)
-    landed(1)
-    project(left, 1, to_slot(5, 1), 0, 3)
-    ship(5, left, 0, 3)
+    for i in range(2):
+        landed(0, i)
+        project(right, 0, to_slot(4, 0), i, 1)
+        ship(4, right, i)
+        landed(1, i)
+        project(left, 1, to_slot(5, 1), i, 1)
+        ship(5, left, i)
 
     settle(v_copy)
 
@@ -577,15 +602,19 @@
     y_recv[s] = lax.fori_loop(0, 16, add_v, jnp.zeros((2, RANK, 128), F32))
     for j in range(1, 4):
         send(y_recv.at[s], y_recv.at[s], "y%d" % j, {"fsdp": lax.rem(s + j, 4)})
-    project(right, 0, to_slot(4, 0), 3, 2)
-    project(left, 1, to_slot(5, 1), 3, 2)
+    for i in range(2, 5):
+        landed(0, i)
+        project(right, 0, to_slot(4, 0), i, 1)
+        landed(1, i)
+        project(left, 1, to_slot(5, 1), i, 1)
     for j in range(1, 4):
         arrived(y_recv.at[lax.rem(s + 4 - j, 4)], "y%d" % j)
     t_recv[t] = ((y_recv[0] + y_recv[1]) + (y_recv[2] + y_recv[3])).astype(BF16)
     for j in range(1, 4):
         send(t_recv.at[t], t_recv.at[t], "t%d" % j, {"tensor": lax.rem(t + j, 4)})
-    ship(4, right, 3, 2)
-    ship(5, left, 3, 2)
+    for i in range(2, 5):
+        ship(4, right, i)
+        ship(5, left, i)
 
     def own_part(half):
         def store(lanes, v):
@@ -613,29 +642,32 @@
 
     exchange(all_copy)
 
-    landed(2)
-    landed(3)
-    landed(4, 0, 3)
-    landed(5, 0, 3)
-    landed(4, 3, 2)
-    landed(5, 3, 2)
     scale_col = jnp.broadcast_to(own_scale[0:1, :], (128, 128)).T
+    for i in range(5):
+        landed(2, i)
+        landed(3, i)
+    for i in range(5):
+        landed(4, i)
+        landed(5, i)
 
     def close(i, carry):
         lanes = tile(i)
         first = own[0, :, lanes] + rs_recv[4, :, lanes].astype(F32) + rs_recv[3, :, lanes].astype(F32)
         second = own[1, :, lanes] + rs_recv[2, :, lanes].astype(F32) + rs_recv[5, :, lanes].astype(F32)
-        mixed[:, lanes] = (scale_col * first).astype(BF16)
-        mixed[:, pl.ds(pl.multiple_of(HALF + i * 128, 128), 128)] = (scale_col * second).astype(BF16)
+        mixed_here[:, lanes] = (scale_col * first).astype(BF16)
+        mixed_here[:, pl.ds(pl.multiple_of(HALF + i * 128, 128), 128)] = (scale_col * second).astype(BF16)
         return carry
 
     lax.fori_loop(0, 10, close, 0)
+    copy_here("mixed", mixed_here, mixed)
 
     settle(all_copy)
     for i in range(10):
-        grad_a[:, i * 128 : i * 128 + 128] = v_all[i // 2, i % 2].astype(F32)
+        a_here[:, i * 128 : i * 128 + 128] = v_all[i // 2, i % 2].astype(F32)
     for i in range(20):
-        grad_b[:, i * 128 : i * 128 + 128] = v_all[5 + i // 2, i % 2].astype(F32)
+        b_here[:, i * 128 : i * 128 + 128] = v_all[5 + i // 2, i % 2].astype(F32)
+    copy_here("grad_a", a_here, grad_a)
+    copy_here("grad_b", b_here, grad_b)
 
     for make, how_many in (
         (decay_copy, 16), (state_copy, 8), (back_copy, 8), (v_copy, 16), (all_copy, 16)
@@ -649,13 +681,15 @@
         for copy in rim_copies():
             copy.wait_send()
 
+    for name in ("mixed", "grad_a", "grad_b"):
+        local[name].wait()
+
 
 def shards(
     input_raw, state_proj_raw, gate_branch, step_raw, convolution_taps, convolution_bias, step_bias,
     decay_log_rate, skip_weight, gated_norm_gain, output_weight, adapter_down, adapter_up, cotangent,
 ):
     hbm = pl.BlockSpec(memory_space=pl.ANY)
-    vmem = pl.BlockSpec(memory_space=pltpu.VMEM)
     dma = pltpu.SemaphoreType.DMA
     mixed, grad_a, grad_b = pl.pallas_call(
         kernel,
@@ -665,7 +699,7 @@
             jax.ShapeDtypeStruct((RANK, OUT), F32),
         ),
         in_specs=[hbm] * 14,
-        out_specs=(vmem, vmem, vmem),
+        out_specs=(hbm, hbm, hbm),
         scratch_shapes=[
             pltpu.VMEM((16 + 512, WIDTH), BF16),
             pltpu.VMEM((2, 64, WIDTH), BF16),
@@ -679,13 +713,15 @@
             pltpu.VMEM((ROWS, OUT), BF16),
             pltpu.VMEM((4, WIDTH), F32),
             pltpu.VMEM((4, 256), F32),
-            pltpu.VMEM((1, WIDTH), F32),
-            pltpu.VMEM((1, 256), F32),
+            pltpu.VMEM((42, 128), F32),
             pltpu.VMEM((3, 1, HEADS), F32),
+            pltpu.VMEM((10, 128), F32),
             pltpu.VMEM((1, WIDTH), F32),
             pltpu.VMEM((RANK, WIDTH), BF16),
             pltpu.VMEM((RANK, OUT), BF16),
             pltpu.VMEM((8, WIDTH), F32),
+            pltpu.VMEM((4, ROWS, WIDTH), F32),
+            pltpu.VMEM((4, 8, WIDTH), F32),
             pltpu.VMEM((256, WIDTH), BF16),
             pltpu.VMEM((4, ROWS, 128), F32),
             pltpu.VMEM((4, ROWS, 128), F32),
@@ -707,7 +743,7 @@
             pltpu.VMEM((STATE, WIDTH), F32),
             pltpu.VMEM((4, ROWS, WIDTH), BF16),
             pltpu.VMEM((4, RANK, 128), F32),
-            pltpu.VMEM((4, 4, 8, 128), F32),
+            pltpu.VMEM((4, 8, 128), F32),
             pltpu.VMEM((4, RANK, 128), F32),
             pltpu.VMEM((4, RANK, 128), F32),
             pltpu.VMEM((6, ROWS, HALF), BF16),
@@ -718,7 +754,10 @@
             pltpu.VMEM((4, 2, RANK, 128), F32),
             pltpu.VMEM((4, 2, RANK, 128), BF16),
             pltpu.VMEM((16, 2, RANK, 128), BF16),
-            dma((72,)), dma((72,)), dma((24,)),
+            pltpu.VMEM((ROWS, OUT), BF16),
+            pltpu.VMEM((RANK, WIDTH), F32),
+            pltpu.VMEM((RANK, OUT), F32),
+            dma((100,)), dma((100,)), dma((32,)),
             dma((8,)), dma((8,)), dma((16,)), dma((16,)), dma((8,)), dma((8,)),
             dma((16,)), dma((16,)), dma((16,)), dma((16,)),
         ],
@@ -726,8 +765,8 @@
             collective_id=0, has_side_effects=True, vmem_limit_bytes=64 * 1000 * 1000),
     )(
         input_raw[0], state_proj_raw[0], gate_branch[0], step_raw[0].T, output_weight, cotangent[0],
-        convolution_taps, convolution_bias[None, :], step_bias[None, :], decay_log_rate[None, :],
-        skip_weight[None, :], gated_norm_gain[None, :], adapter_down.T, adapter_up,
+        convolution_taps, convolution_bias.reshape(42, 128), step_bias[None, :], decay_log_rate[None, :],
+        skip_weight[None, :], gated_norm_gain.reshape(10, 128), adapter_down.T, adapter_up,
     )
     return (mixed[None], grad_a.T, grad_b)
 

time: 94.2 us -> 84.2 us (0.89)
  Pallas kernels: 87.3 us -> 80.1 us
  local copies, waits for them, and re-layouts: 5.97 us -> 3.32 us
    pallas_call x1, Pallas kernels: 87.3 us -> 80.1 us  [shards(): pl.pallas_call(kernel, out_shape=(jax.ShapeDtypeStruct((ROWS, OUT), BF16)...]
    broadcast_in_dim x2 -> x0, local copies, waits for them, and re-layouts: 2.65 us -> none  [the longest x1 1.36 us: shards(): convolution_bias[None, :]]
where the time goes in v3:
time: 84.2 us; the launch traced here: 84.1 us
  Pallas kernels  80.1 us (95%)
  local copies, waits for them, and re-layouts  3.32 us (4%)
    pallas_call x1, Pallas kernels, shards(): pl.pallas_call(kernel, out_shape=(jax.ShapeDtypeStruct((ROWS, OUT), BF16)...  80.1 us
    unnamed x7, local copies, waits for them, and re-layouts  3.32 us

profile of v3, /device:TPU:1, one launch (start us, length us, event | category | flops | bytes accessed | tf_op | source)
XLA Modules:
  0.0 84.1 jit_solution(10479362908248271660)
XLA Ops:
  0.6 80.1 %shard_map.157 = (bf16[128,2560]{1,0:T(8,128)(2,1)}, f32[16,1280]{1,0:T(8,128)}, f32[16,2560]{1,0:T(8,128)}) custom-call(bf16[128,5120]{1,0:T(8,128)(2,1)} %bitcast.15, bf16[128,256]{1,0:T(8,128)(2,1)} %bitcast.20, bf16[128,5120]{1,0:T(8,128)(2,1)} %bitcast.16, bf16[80,128]{1,0:T(8,128)(2,1)} %bitcast.23, bf16[1280,640]{1,0:T(8,128)(2,1)} %w_in.1, ...), custom_call_target="tpu_custom_call" | custom-call | tf_op jit(solution)/shard_map/pallas_call | solution.py:694
  80.8 0.0 copy-start.1
  80.8 0.0 copy-start
  80.8 2.0 %copy.20 = bf16[1,128,2560]{2,1,0:T(8,128)(2,1)} copy(bf16[1,128,2560]{2,1,0:T(8,128)(2,1)} %bitcast.18) | data formatting | bytes 1310720
  82.8 0.0 copy-done.1
  82.8 0.6 copy.21
  83.5 0.0 copy-done
  83.5 0.7 copy.22
Async XLA Ops:
  80.8 2.0 %copy-start.1 = (f32[16,1280]{1,0:T(8,128)S(1)}, f32[16,1280]{1,0:T(8,128)}, u32[]{:S(2)}) copy-start(f32[16,1280]{1,0:T(8,128)} %get-tuple-element.7) | copy-start | bytes 245764
  80.8 2.7 %copy-start = (f32[16,2560]{1,0:T(8,128)S(1)}, f32[16,2560]{1,0:T(8,128)}, u32[]{:S(2)}) copy-start(f32[16,2560]{1,0:T(8,128)} %get-tuple-element.14) | copy-start | bytes 491524

commit v4 on v3

--- a/solution.py
+++ b/solution.py
@@ -40,14 +40,14 @@
 def kernel(
     x_in, bc_in, z_in, dt_in, w_in, cot_in, taps_in, bias_in, step_bias_in, rate_in, skip_in, gain_in, down_in, up_in,
     mixed, grad_a, grad_b,
-    x_ext, xr, xc, bc_ext, bcc, dt_all, gate, zr, wt, cot,
+    x_ext, xr, rim_x, rim_b, xc, bc_ext, bcc, dt_all, gate, zr, wt, cot,
     taps_x, taps_bc, bias, head_par, gain_rows, gain, down_t, up, skip, weights, tails,
     spread, step, cum, log_start, log_tail, y_in, blocks, kept, state, peer_state,
     st_send, st_recv, dec_all, dec_wide, back_send, back_recv, in_send, in_recv, s_in,
     gated, gt, sq, ap_send, ap_recv,
     rs_send, rs_recv, own,
     v_send, v_recv, y_recv, t_recv, v_all, mixed_here, a_here, b_here,
-    sx, rx, sl, sc, rc_, sd, rd, sb, rb, sv, rv, sg, rg,
+    sx, rx, sl, sc, rc_, sd, rd, sb, rb, sv, rv, sg, rg, sr, rr, rr_end,
 ):
     z, k = lax.axis_index("context_0"), lax.axis_index("context_1")
     t, s = lax.axis_index("tensor"), lax.axis_index("fsdp")
@@ -97,15 +97,9 @@
 
         lax.fori_loop(1, how_many, go, 0)
 
-    def settle(make, how_many=16, received=True):
-        def go(j, carry):
-            if received:
-                make(j).wait_recv()
-            else:
-                make(j).wait_send()
-            return carry
-
-        lax.fori_loop(1, how_many, go, 0)
+    def settle(buffer, sem, how_many=15):
+        several = buffer.at[pl.ds(0, how_many)]
+        pltpu.make_async_copy(several, several, sem).wait()
 
     def tile(i):
         return pl.ds(pl.multiple_of(i * 128, 128), 128)
@@ -226,6 +220,23 @@
         arrived(rows(far, 0, 64), name + "4")
         arrived(rows(far, 64, 64), name + "5")
 
+    def rim_copies():
+        copies = []
+        for p in range(4):
+            where = {"context_0": lax.div(after, 2), "context_1": lax.rem(after, 2), "tensor": p}
+            copies.append(pltpu.make_async_remote_copy(
+                src_ref=x_in.at[pl.ds(120, 8), pl.ds(p * WIDTH, WIDTH)], dst_ref=rim_x,
+                send_sem=sl.at[p], recv_sem=rx.at[slot("rim_x")], device_id=where, device_id_type=MESH))
+            copies.append(pltpu.make_async_remote_copy(
+                src_ref=bc_in.at[pl.ds(120, 8)], dst_ref=rim_b,
+                send_sem=sl.at[4 + p], recv_sem=rx.at[slot("rim_b")], device_id=where, device_id_type=MESH))
+        return copies
+
+    @pl.when(gives_rim)
+    def _():
+        for copy in rim_copies():
+            copy.start()
+
     far_start(x_in, xr, "x")
     send(bc_in.at[pl.ds(0, 64)], bc_rows(t, 0, 64), "b0", {"tensor": right})
     send(bc_in.at[pl.ds(64, 64)], bc_rows(t, 64, 64), "b1", {"tensor": left})
@@ -235,23 +246,6 @@
         peer = lax.rem(t + j, 4)
         send(dt_window(peer), dt_all.at[t], "dt%d" % j, {"tensor": peer})
     near_start(x_in, x_rows, "x")
-
-    def rim_copies():
-        copies = []
-        for p in range(4):
-            where = {"context_0": lax.div(after, 2), "context_1": lax.rem(after, 2), "tensor": p}
-            copies.append(pltpu.make_async_remote_copy(
-                src_ref=x_in.at[pl.ds(112, 16), pl.ds(p * WIDTH, WIDTH)], dst_ref=x_ext.at[pl.ds(0, 16)],
-                send_sem=sl.at[p], recv_sem=rx.at[slot("rim_x")], device_id=where, device_id_type=MESH))
-            copies.append(pltpu.make_async_remote_copy(
-                src_ref=bc_in.at[pl.ds(112, 16)], dst_ref=bc_ext.at[pl.ds(0, 16)],
-                send_sem=sl.at[4 + p], recv_sem=rx.at[slot("rim_b")], device_id=where, device_id_type=MESH))
-        return copies
-
-    @pl.when(gives_rim)
-    def _():
-        for copy in rim_copies():
-            copy.start()
 
     @pl.when(c == 0)
     def _():
@@ -312,14 +306,23 @@
     send(bc_rows(left, 0, 64), bc_rows(left, 0, 64), "b4", {"tensor": right})
     arrived(bc_rows(right, 64, 64), "b1")
     send(bc_rows(right, 64, 64), bc_rows(right, 64, 64), "b5", {"tensor": left})
-    far_forward(x_rows, xr, "x")
+    def x_lanes(p, first, half):
+        return x_ext.at[
+            pl.ds(pl.multiple_of(16 + p * ROWS + first, 16), 64), pl.ds(half * 640, 640)]
+
+    arrived(xr.at[0], "x0")
+    arrived(xr.at[1], "x1")
+    for half in range(2):
+        lanes = pl.ds(half * 640, 640)
+        send(xr.at[0, :, lanes], x_lanes(left, 0, half), "x4%d" % half, {"tensor": right})
+        send(xr.at[1, :, lanes], x_lanes(right, 64, half), "x5%d" % half, {"tensor": left})
     far_start(z_in, zr, "z")
     near_start(z_in, z_rows, "z")
 
     def decay_copy(j):
         return pltpu.make_async_remote_copy(
             src_ref=dec_all.at[c], dst_ref=dec_all.at[c],
-            send_sem=sd.at[j], recv_sem=rd.at[j], device_id=context_peer(j), device_id_type=MESH)
+            send_sem=sd, recv_sem=rd, device_id=context_peer(j), device_id_type=MESH)
 
     exchange(decay_copy)
     for j in range(1, 4):
@@ -335,26 +338,36 @@
 
     @pl.when(c > 0)
     def _():
-        arrived(x_ext.at[pl.ds(0, 16)], "rim_x")
-        arrived(bc_ext.at[pl.ds(0, 16)], "rim_b")
+        arrived(rim_x, "rim_x")
+        arrived(rim_b, "rim_b")
+        x_ext[0:16, :] = jnp.concatenate([rim_x[...], rim_x[...]], axis=0)
+        bc_ext[0:16, :] = jnp.concatenate([rim_b[...], rim_b[...]], axis=0)
 
     state[...] = jnp.zeros((STATE, WIDTH), F32)
 
-    def block(i, carry):
+    def shared(i, carry):
         p = lax.rem(t + i, 4)
         for half in range(2):
             bcc[p, :, pl.ds(half * 128, 128)] = convolved(bc_ext, p, pl.ds(half * 128, 128), taps_bc, 40 + half)
-
-        def lanes_of(j, inner):
-            xc[p, :, tile(j)] = convolved(x_ext, p, tile(j), taps_x, 10 * t + j)
-            return inner
-
-        lax.fori_loop(0, 10, lanes_of, 0)
-        scaled = (xc[p].astype(F32) * weights[p]).astype(BF16)
-        fresh = dot(bcc[p, :, 0:128], scaled, TN)
-        blocks[p] = fresh
-        state[...] = state[...] + tails[p, 0:1, :] * fresh
-        return carry
+        return carry
+
+    def block(first, count):
+        def of(i, carry):
+            p = lax.rem(t + i, 4)
+            lanes = pl.ds(first * 128, count * 128)
+
+            def lanes_of(j, inner):
+                xc[p, :, tile(j)] = convolved(x_ext, p, tile(j), taps_x, 10 * t + j)
+                return inner
+
+            lax.fori_loop(first, first + count, lanes_of, 0)
+            scaled = (xc[p, :, lanes].astype(F32) * weights[p, :, lanes]).astype(BF16)
+            fresh = dot(bcc[p, :, 0:128], scaled, TN)
+            blocks[p, :, lanes] = fresh
+            state[:, lanes] = state[:, lanes] + tails[p, 0:1, lanes] * fresh
+            return carry
+
+        return of
 
     def weigh(p, carry):
         cum_now = cum[p]
@@ -363,14 +376,22 @@
         return carry
 
     lax.fori_loop(0, 4, weigh, 0)
+    arrived(w_part(mine, 320, down_y), "w0")
+    send(w_part(mine, 320, down_y), w_part(mine, 320, down_y), "w4", {"fsdp": up_y})
+    arrived(w_part(mine + 320, 320, up_y), "w1")
+    send(w_part(mine + 320, 320, up_y), w_part(mine + 320, 320, up_y), "w5", {"fsdp": down_y})
     arrived(bc_rows(left, 64, 64), "b2")
     arrived(bc_rows(right, 0, 64), "b3")
+    lax.fori_loop(0, 2, shared, 0)
     near_wait(x_rows, "x")
-    lax.fori_loop(0, 2, block, 0)
+    lax.fori_loop(0, 2, block(0, 10), 0)
     arrived(bc_rows(far, 0, 64), "b4")
     arrived(bc_rows(far, 64, 64), "b5")
-    far_wait(x_rows, "x")
-    lax.fori_loop(2, 4, block, 0)
+    lax.fori_loop(2, 4, shared, 0)
+    for half in range(2):
+        arrived(x_lanes(far, 0, half), "x4%d" % half)
+        arrived(x_lanes(far, 64, half), "x5%d" % half)
+        lax.fori_loop(2, 4, block(5 * half, 5), 0)
 
     core = {"context_1": 1 - k}
 
@@ -378,7 +399,7 @@
         return pl.ds(pl.multiple_of(i * 640, 640), 640)
 
     send(state.at[:, half_lanes(1 - k)], peer_state, "pair", core)
-    settle(decay_copy)
+    settle(dec_all, rd)
     dec_wide[...] = widen(dec_all[...].reshape(128, 128))
     arrived(peer_state, "pair")
 
@@ -401,15 +422,15 @@
     def state_copy(j):
         return pltpu.make_async_remote_copy(
             src_ref=st_send.at[chip_at(j - 1)], dst_ref=st_recv.at[z],
-            send_sem=sc.at[j], recv_sem=rc_.at[j], device_id=chip_peer(j), device_id_type=MESH)
+            send_sem=sc, recv_sem=rc_, device_id=chip_peer(j), device_id_type=MESH)
 
     exchange(state_copy, 8)
     st_recv[z] = st_send[z]
 
-    arrived(w_part(mine, 320, down_y), "w0")
-    send(w_part(mine, 320, down_y), w_part(mine, 320, down_y), "w4", {"fsdp": up_y})
-    arrived(w_part(mine + 320, 320, up_y), "w1")
-    send(w_part(mine + 320, 320, up_y), w_part(mine + 320, 320, up_y), "w5", {"fsdp": down_y})
+    arrived(w_part(mine + 320, 320, down_y), "w2")
+    send(w_part(mine, 640, down_y), w_part(mine, 640, down_y), "w6", core)
+    arrived(w_part(mine, 320, up_y), "w3")
+    send(w_part(mine, 640, up_y), w_part(mine, 640, up_y), "w7", core)
     far_forward(z_rows, zr, "z")
 
     def inside(p, carry):
@@ -432,7 +453,7 @@
 
     lax.fori_loop(0, 4, inside, 0)
 
-    settle(state_copy, 8)
+    settle(st_recv, rc_, 7)
 
     def chain(i, held):
         back_send[i] = held.astype(BF16)
@@ -443,7 +464,7 @@
     def back_copy(j):
         return pltpu.make_async_remote_copy(
             src_ref=back_send.at[chip_at(j - 1)], dst_ref=back_recv.at[z],
-            send_sem=sb.at[j], recv_sem=rb.at[j], device_id=chip_peer(j), device_id_type=MESH)
+            send_sem=sb, recv_sem=rb, device_id=chip_peer(j), device_id_type=MESH)
 
     exchange(back_copy, 8)
     back_recv[z] = back_send[z]
@@ -458,10 +479,6 @@
 
     lax.fori_loop(0, 10, starts, 0)
 
-    arrived(w_part(mine + 320, 320, down_y), "w2")
-    send(w_part(mine, 640, down_y), w_part(mine, 640, down_y), "w6", core)
-    arrived(w_part(mine, 320, up_y), "w3")
-    send(w_part(mine, 640, up_y), w_part(mine, 640, up_y), "w7", core)
     arrived(w_part(mine, 320, far_y), "w4")
     arrived(w_part(mine + 320, 320, far_y), "w5")
     send(w_part(mine, 640, far_y), w_part(mine, 640, far_y), "w8", core)
@@ -469,7 +486,7 @@
     local["gate"].wait()
     near_wait(z_rows, "z")
     far_wait(z_rows, "z")
-    settle(back_copy, 8)
+    settle(back_recv, rb, 7)
 
     decay_first = dec_wide[pl.ds(pl.multiple_of(16 * z, 8), 8), half_lanes(k)][0:1, :]
 
@@ -526,10 +543,14 @@
         return ref.at[which, :, pl.ds(i * 256, 256)]
 
     def ship(which, where, i):
-        send(piece_at(rs_send, which, i), piece_at(rs_recv, which, i), "r%d_%d" % (which, i), {"tensor": where})
+        pltpu.make_async_remote_copy(
+            src_ref=piece_at(rs_send, which, i), dst_ref=piece_at(rs_recv, which, i),
+            send_sem=sr, recv_sem=rr.at[5 * which + i] if which < 2 else rr_end.at[which - 2],
+            device_id={"tensor": where}, device_id_type=MESH).start()
 
     def landed(which, i):
-        arrived(piece_at(rs_recv, which, i), "r%d_%d" % (which, i))
+        piece = piece_at(rs_recv, which, i)
+        pltpu.make_async_copy(piece, piece, rr.at[5 * which + i]).wait()
 
     lax.fori_loop(2, 3, finish, 0)
     for i in range(5):
@@ -582,11 +603,11 @@
     def v_copy(j):
         return pltpu.make_async_remote_copy(
             src_ref=v_send.at[context_index(j)], dst_ref=v_recv.at[c],
-            send_sem=sv.at[j], recv_sem=rv.at[j], device_id=context_peer(j), device_id_type=MESH)
+            send_sem=sv, recv_sem=rv, device_id=context_peer(j), device_id_type=MESH)
 
     exchange(v_copy)
 
-    for i in range(2):
+    for i in range(1):
         landed(0, i)
         project(right, 0, to_slot(4, 0), i, 1)
         ship(4, right, i)
@@ -594,7 +615,7 @@
         project(left, 1, to_slot(5, 1), i, 1)
         ship(5, left, i)
 
-    settle(v_copy)
+    settle(v_recv, rv)
 
     def add_v(i, held):
         return held + v_recv[i].astype(F32)
@@ -602,7 +623,7 @@
     y_recv[s] = lax.fori_loop(0, 16, add_v, jnp.zeros((2, RANK, 128), F32))
     for j in range(1, 4):
         send(y_recv.at[s], y_recv.at[s], "y%d" % j, {"fsdp": lax.rem(s + j, 4)})
-    for i in range(2, 5):
+    for i in range(1, 5):
         landed(0, i)
         project(right, 0, to_slot(4, 0), i, 1)
         landed(1, i)
@@ -612,7 +633,7 @@
     t_recv[t] = ((y_recv[0] + y_recv[1]) + (y_recv[2] + y_recv[3])).astype(BF16)
     for j in range(1, 4):
         send(t_recv.at[t], t_recv.at[t], "t%d" % j, {"tensor": lax.rem(t + j, 4)})
-    for i in range(2, 5):
+    for i in range(1, 5):
         ship(4, right, i)
         ship(5, left, i)
 
@@ -638,17 +659,13 @@
     def all_copy(j):
         return pltpu.make_async_remote_copy(
             src_ref=v_all.at[c], dst_ref=v_all.at[c],
-            send_sem=sg.at[j], recv_sem=rg.at[j], device_id=context_peer(j), device_id_type=MESH)
+            send_sem=sg, recv_sem=rg, device_id=context_peer(j), device_id_type=MESH)
 
     exchange(all_copy)
 
     scale_col = jnp.broadcast_to(own_scale[0:1, :], (128, 128)).T
-    for i in range(5):
-        landed(2, i)
-        landed(3, i)
-    for i in range(5):
-        landed(4, i)
-        landed(5, i)
+    for which in range(2, 6):
+        pltpu.make_async_copy(rs_recv.at[which], rs_recv.at[which], rr_end.at[which - 2]).wait()
 
     def close(i, carry):
         lanes = tile(i)
@@ -661,7 +678,7 @@
     lax.fori_loop(0, 10, close, 0)
     copy_here("mixed", mixed_here, mixed)
 
-    settle(all_copy)
+    settle(v_all, rg)
     for i in range(10):
         a_here[:, i * 128 : i * 128 + 128] = v_all[i // 2, i % 2].astype(F32)
     for i in range(20):
@@ -669,10 +686,12 @@
     copy_here("grad_a", a_here, grad_a)
     copy_here("grad_b", b_here, grad_b)
 
-    for make, how_many in (
-        (decay_copy, 16), (state_copy, 8), (back_copy, 8), (v_copy, 16), (all_copy, 16)
-    ):
-        settle(make, how_many, received=False)
+    settle(dec_all, sd)
+    settle(st_send, sc, 7)
+    settle(back_send, sb, 7)
+    settle(v_send, sv)
+    settle(v_all, sg)
+    pltpu.make_async_copy(rs_send, rs_send, sr).wait()
     for copy in started:
         copy.wait_send()
 
@@ -703,6 +722,8 @@
         scratch_shapes=[
             pltpu.VMEM((16 + 512, WIDTH), BF16),
             pltpu.VMEM((2, 64, WIDTH), BF16),
+            pltpu.VMEM((8, WIDTH), BF16),
+            pltpu.VMEM((8, 256), BF16),
             pltpu.VMEM((4, ROWS, WIDTH), BF16),
             pltpu.VMEM((16 + 512, 256), BF16),
             pltpu.VMEM((4, ROWS, 256), BF16),
@@ -757,9 +778,8 @@
             pltpu.VMEM((ROWS, OUT), BF16),
             pltpu.VMEM((RANK, WIDTH), F32),
             pltpu.VMEM((RANK, OUT), F32),
-            dma((100,)), dma((100,)), dma((32,)),
-            dma((8,)), dma((8,)), dma((16,)), dma((16,)), dma((8,)), dma((8,)),
-            dma((16,)), dma((16,)), dma((16,)), dma((16,)),
+            dma((60,)), dma((60,)), dma((26,)),
+            dma, dma, dma, dma, dma, dma, dma, dma, dma, dma, dma, dma((10,)), dma((4,)),
         ],
         compiler_params=pltpu.CompilerParams(
             collective_id=0, has_side_effects=True, vmem_limit_bytes=64 * 1000 * 1000),

time: 84.2 us -> 78.9 us (0.937)
  Pallas kernels: 80.1 us -> 74.8 us
    pallas_call x1, Pallas kernels: 80.1 us -> 74.8 us  [shards(): pl.pallas_call(kernel, out_shape=(jax.ShapeDtypeStruct((ROWS, OUT), BF16)...]
where the time goes in v4:
time: 78.9 us; the launch traced here: 78.8 us
  Pallas kernels  74.8 us (95%)
  local copies, waits for them, and re-layouts  3.32 us (4%)
    pallas_call x1, Pallas kernels, shards(): pl.pallas_call(kernel, out_shape=(jax.ShapeDtypeStruct((ROWS, OUT), BF16)...  74.8 us
    unnamed x7, local copies, waits for them, and re-layouts  3.32 us

profile of v4, /device:TPU:1, one launch (start us, length us, event | category | flops | bytes accessed | tf_op | source)
XLA Modules:
  0.0 78.8 jit_solution(14723608064944635262)
XLA Ops:
  0.6 74.8 %shard_map.157 = (bf16[128,2560]{1,0:T(8,128)(2,1)}, f32[16,1280]{1,0:T(8,128)}, f32[16,2560]{1,0:T(8,128)}) custom-call(bf16[128,5120]{1,0:T(8,128)(2,1)} %bitcast.15, bf16[128,256]{1,0:T(8,128)(2,1)} %bitcast.20, bf16[128,5120]{1,0:T(8,128)(2,1)} %bitcast.16, bf16[80,128]{1,0:T(8,128)(2,1)} %bitcast.23, bf16[1280,640]{1,0:T(8,128)(2,1)} %w_in.1, ...), custom_call_target="tpu_custom_call" | custom-call | tf_op jit(solution)/shard_map/pallas_call | solution.py:713
  75.5 0.0 copy-start.1
  75.5 0.0 copy-start
  75.5 2.0 %copy.20 = bf16[1,128,2560]{2,1,0:T(8,128)(2,1)} copy(bf16[1,128,2560]{2,1,0:T(8,128)(2,1)} %bitcast.18) | data formatting | bytes 1310720
  77.5 0.0 copy-done.1
  77.5 0.6 copy.21
  78.1 0.0 copy-done
  78.1 0.7 copy.22
Async XLA Ops:
  75.5 2.0 %copy-start.1 = (f32[16,1280]{1,0:T(8,128)S(1)}, f32[16,1280]{1,0:T(8,128)}, u32[]{:S(2)}) copy-start(f32[16,1280]{1,0:T(8,128)} %get-tuple-element.7) | copy-start | bytes 245764
  75.5 2.7 %copy-start = (f32[16,2560]{1,0:T(8,128)S(1)}, f32[16,2560]{1,0:T(8,128)}, u32[]{:S(2)}) copy-start(f32[16,2560]{1,0:T(8,128)} %get-tuple-element.14) | copy-start | bytes 491524

commit v5 on v4

--- a/solution.py
+++ b/solution.py
@@ -43,11 +43,11 @@
     x_ext, xr, rim_x, rim_b, xc, bc_ext, bcc, dt_all, gate, zr, wt, cot,
     taps_x, taps_bc, bias, head_par, gain_rows, gain, down_t, up, skip, weights, tails,
     spread, step, cum, log_start, log_tail, y_in, blocks, kept, state, peer_state,
-    st_send, st_recv, dec_all, dec_wide, back_send, back_recv, in_send, in_recv, s_in,
+    st_send, st_recv, dec_all, dec_wide, back_send, back_recv, in_send, s_in,
     gated, gt, sq, ap_send, ap_recv,
     rs_send, rs_recv, own,
     v_send, v_recv, y_recv, t_recv, v_all, mixed_here, a_here, b_here,
-    sx, rx, sl, sc, rc_, sd, rd, sb, rb, sv, rv, sg, rg, sr, rr, rr_end,
+    sx, rx, sl, sc, rc_, sd, rd, sb, rb, sv, rv, sg, rg, sr, rr, rr_end, sgroup, s3, r3, s_head,
 ):
     z, k = lax.axis_index("context_0"), lax.axis_index("context_1")
     t, s = lax.axis_index("tensor"), lax.axis_index("fsdp")
@@ -55,24 +55,39 @@
     right, left, far = lax.rem(t + 1, 4), lax.rem(t + 3, 4), lax.rem(t + 2, 4)
     up_y, down_y, far_y = lax.rem(s + 1, 4), lax.rem(s + 3, 4), lax.rem(s + 2, 4)
     started = []
-    slots = {}
+    slots, send_slots = {}, {}
 
     def slot(name):
         return slots.setdefault(name, len(slots))
 
-    def remote(src, dst, name, where):
-        return pltpu.make_async_remote_copy(
-            src_ref=src, dst_ref=dst, send_sem=sx.at[slot(name)], recv_sem=rx.at[slot(name)],
-            device_id=where, device_id_type=MESH,
+    def send_slot(name):
+        return send_slots.setdefault(name, len(send_slots))
+
+    groups = {"x": 0, "z": 1, "w": 2}
+
+    def send(src, dst, name, where):
+        grouped = groups.get(name[0])
+        copy = pltpu.make_async_remote_copy(
+            src_ref=src, dst_ref=dst,
+            send_sem=sx.at[send_slot(name)] if grouped is None else sgroup.at[grouped],
+            recv_sem=rx.at[slot(name)], device_id=where, device_id_type=MESH,
         )
-
-    def send(src, dst, name, where):
-        copy = remote(src, dst, name, where)
         copy.start()
-        started.append(copy)
+        if groups.get(name[0]) is None:
+            started.append(copy)
+
+    def send_triple(make, which):
+        for j in (2, 1, 3):
+            src, dst, where = make(j)
+            pltpu.make_async_remote_copy(
+                src_ref=src, dst_ref=dst, send_sem=s3.at[which], recv_sem=r3.at[which],
+                device_id=where, device_id_type=MESH).start()
+
+    def tensor_peer(j):
+        return lax.rem(t + j, 4)
 
     def arrived(dst, name):
-        remote(dst, dst, name, {"tensor": right}).wait_recv()
+        pltpu.make_async_copy(dst, dst, rx.at[slot(name)]).wait()
 
     def chip_at(i):
         step_now = lax.div(i + 1, 2)
@@ -97,8 +112,7 @@
 
         lax.fori_loop(1, how_many, go, 0)
 
-    def settle(buffer, sem, how_many=15):
-        several = buffer.at[pl.ds(0, how_many)]
+    def settle(several, sem):
         pltpu.make_async_copy(several, several, sem).wait()
 
     def tile(i):
@@ -137,6 +151,12 @@
     def bc_rows(p, first, count):
         return bc_ext.at[pl.ds(pl.multiple_of(16 + p * ROWS + first, 16), count)]
 
+    def b_lanes(p, first):
+        return bc_ext.at[pl.ds(pl.multiple_of(16 + p * ROWS + first, 16), 64), pl.ds(0, 128)]
+
+    def c_lanes(p, first):
+        return bc_ext.at[pl.ds(pl.multiple_of(16 + p * ROWS + first, 16), 64), pl.ds(128, 128)]
+
     def w_part(rows_from, count, y):
         return wt.at[
             pl.ds(pl.multiple_of(rows_from, 64), count), pl.ds(pl.multiple_of(y * COLS, COLS), COLS)
@@ -153,9 +173,8 @@
 
     copy_here("cot", cot_in, cot)
     copy_here("up", up_in, up)
-    copy_here("step_bias", step_bias_in, head_par.at[0])
-    copy_here("rate", rate_in, head_par.at[1])
-    copy_here("skip", skip_in, head_par.at[2])
+    for i, source in enumerate((step_bias_in, rate_in, skip_in)):
+        pltpu.make_async_copy(source, head_par.at[i], s_head).start()
     copy_here("bc", bc_in, bc_rows(t, 0, ROWS))
     copy_here("dt", dt_window(t), dt_all.at[t])
     copy_here("taps_x", taps_in.at[:, columns(t)], taps_x)
@@ -240,11 +259,9 @@
     far_start(x_in, xr, "x")
     send(bc_in.at[pl.ds(0, 64)], bc_rows(t, 0, 64), "b0", {"tensor": right})
     send(bc_in.at[pl.ds(64, 64)], bc_rows(t, 64, 64), "b1", {"tensor": left})
-    send(bc_in.at[pl.ds(64, 64)], bc_rows(t, 64, 64), "b2", {"tensor": right})
-    send(bc_in.at[pl.ds(0, 64)], bc_rows(t, 0, 64), "b3", {"tensor": left})
-    for j in (1, 3, 2):
-        peer = lax.rem(t + j, 4)
-        send(dt_window(peer), dt_all.at[t], "dt%d" % j, {"tensor": peer})
+    send(bc_in.at[pl.ds(64, 64), pl.ds(0, 128)], b_lanes(t, 64), "b2", {"tensor": right})
+    send(bc_in.at[pl.ds(0, 64), pl.ds(0, 128)], b_lanes(t, 0), "b3", {"tensor": left})
+    send_triple(lambda j: (dt_window(tensor_peer(j)), dt_all.at[t], {"tensor": tensor_peer(j)}), 0)
     near_start(x_in, x_rows, "x")
 
     @pl.when(c == 0)
@@ -262,7 +279,8 @@
     send(w_src(320), w_part(mine + 320, 320, s), "w2", {"fsdp": up_y})
     send(w_src(0), w_part(mine, 320, s), "w3", {"fsdp": down_y})
 
-    for name in ("step_bias", "rate", "skip", "bc", "dt", "taps_x", "taps_bc", "bias", "x", "gain", "down"):
+    settle(head_par, s_head)
+    for name in ("bc", "dt", "taps_x", "taps_bc", "bias", "x", "gain", "down"):
         local[name].wait()
     pick20 = jnp.where(
         lax.broadcasted_iota(jnp.int32, (HEADS, 128), 0) == lax.broadcasted_iota(jnp.int32, (HEADS, 128), 1), 1.0, 0.0)
@@ -276,8 +294,7 @@
     for i in range(10):
         gain[:, i * 128 : i * 128 + 128] = gain_rows[i : i + 1, :]
 
-    for j in range(1, 4):
-        arrived(dt_all.at[lax.rem(t + 4 - j, 4)], "dt%d" % j)
+    settle(dt_all.at[pl.ds(0, 3)], r3.at[0])
 
     row = lax.broadcasted_iota(jnp.int32, (128, 128), 0)
     col = lax.broadcasted_iota(jnp.int32, (128, 128), 1)
@@ -303,21 +320,33 @@
     dec_all[c] = jnp.broadcast_to(jnp.exp(total), (8, 128))
 
     arrived(bc_rows(left, 0, 64), "b0")
-    send(bc_rows(left, 0, 64), bc_rows(left, 0, 64), "b4", {"tensor": right})
+    send(b_lanes(left, 0), b_lanes(left, 0), "b4", {"tensor": right})
     arrived(bc_rows(right, 64, 64), "b1")
-    send(bc_rows(right, 64, 64), bc_rows(right, 64, 64), "b5", {"tensor": left})
-    def x_lanes(p, first, half):
+    send(b_lanes(right, 64), b_lanes(right, 64), "b5", {"tensor": left})
+    pieces = ((0, 5), (5, 3), (8, 2))
+
+    def x_lanes(p, first, piece):
         return x_ext.at[
-            pl.ds(pl.multiple_of(16 + p * ROWS + first, 16), 64), pl.ds(half * 640, 640)]
+            pl.ds(pl.multiple_of(16 + p * ROWS + first, 16), 64), pl.ds(piece[0] * 128, piece[1] * 128)]
 
     arrived(xr.at[0], "x0")
     arrived(xr.at[1], "x1")
-    for half in range(2):
-        lanes = pl.ds(half * 640, 640)
-        send(xr.at[0, :, lanes], x_lanes(left, 0, half), "x4%d" % half, {"tensor": right})
-        send(xr.at[1, :, lanes], x_lanes(right, 64, half), "x5%d" % half, {"tensor": left})
+    for piece in pieces:
+        lanes = pl.ds(piece[0] * 128, piece[1] * 128)
+        send(xr.at[0, :, lanes], x_lanes(left, 0, piece), "x4%d" % piece[0], {"tensor": right})
+        send(xr.at[1, :, lanes], x_lanes(right, 64, piece), "x5%d" % piece[0], {"tensor": left})
+    send(bc_in.at[pl.ds(64, 64), pl.ds(128, 128)], c_lanes(t, 64), "c2", {"tensor": right})
+    send(bc_in.at[pl.ds(0, 64), pl.ds(128, 128)], c_lanes(t, 0), "c3", {"tensor": left})
+    send(c_lanes(left, 0), c_lanes(left, 0), "c4", {"tensor": right})
+    send(c_lanes(right, 64), c_lanes(right, 64), "c5", {"tensor": left})
     far_start(z_in, zr, "z")
-    near_start(z_in, z_rows, "z")
+
+    def gate_near(first):
+        rows = pl.ds(first, 64)
+        send(z_in.at[rows, columns(right)], z_rows(t, first, 64), "z2%d" % first, {"tensor": right})
+        send(z_in.at[rows, columns(left)], z_rows(t, first, 64), "z3%d" % first, {"tensor": left})
+
+    gate_near(0)
 
     def decay_copy(j):
         return pltpu.make_async_remote_copy(
@@ -325,8 +354,7 @@
             send_sem=sd, recv_sem=rd, device_id=context_peer(j), device_id_type=MESH)
 
     exchange(decay_copy)
-    for j in range(1, 4):
-        send(gt.at[t], gt.at[t], "g%d" % j, {"tensor": lax.rem(t + j, 4)})
+    send_triple(lambda j: (gt.at[t], gt.at[t], {"tensor": tensor_peer(j)}), 1)
 
     def convolved(ext, p, lanes, taps, bias_row):
         v = ext[pl.ds(pl.multiple_of(p * ROWS, 16), ROWS + 16), lanes].astype(F32)
@@ -345,11 +373,13 @@
 
     state[...] = jnp.zeros((STATE, WIDTH), F32)
 
-    def shared(i, carry):
-        p = lax.rem(t + i, 4)
-        for half in range(2):
+    def shared(half):
+        def of(i, carry):
+            p = lax.rem(t + i, 4)
             bcc[p, :, pl.ds(half * 128, 128)] = convolved(bc_ext, p, pl.ds(half * 128, 128), taps_bc, 40 + half)
-        return carry
+            return carry
+
+        return of
 
     def block(first, count):
         def of(i, carry):
@@ -380,58 +410,75 @@
     send(w_part(mine, 320, down_y), w_part(mine, 320, down_y), "w4", {"fsdp": up_y})
     arrived(w_part(mine + 320, 320, up_y), "w1")
     send(w_part(mine + 320, 320, up_y), w_part(mine + 320, 320, up_y), "w5", {"fsdp": down_y})
-    arrived(bc_rows(left, 64, 64), "b2")
-    arrived(bc_rows(right, 0, 64), "b3")
-    lax.fori_loop(0, 2, shared, 0)
+    settle(dec_all.at[pl.ds(0, 15)], rd)
+    dec_wide[...] = widen(dec_all[...].reshape(128, 128))
+    arrived(b_lanes(left, 64), "b2")
+    arrived(b_lanes(right, 0), "b3")
+    lax.fori_loop(0, 2, shared(0), 0)
     near_wait(x_rows, "x")
     lax.fori_loop(0, 2, block(0, 10), 0)
-    arrived(bc_rows(far, 0, 64), "b4")
-    arrived(bc_rows(far, 64, 64), "b5")
-    lax.fori_loop(2, 4, shared, 0)
-    for half in range(2):
-        arrived(x_lanes(far, 0, half), "x4%d" % half)
-        arrived(x_lanes(far, 64, half), "x5%d" % half)
-        lax.fori_loop(2, 4, block(5 * half, 5), 0)
-
     core = {"context_1": 1 - k}
 
-    def half_lanes(i):
-        return pl.ds(pl.multiple_of(i * 640, 640), 640)
-
-    send(state.at[:, half_lanes(1 - k)], peer_state, "pair", core)
-    settle(dec_all, rd)
-    dec_wide[...] = widen(dec_all[...].reshape(128, 128))
-    arrived(peer_state, "pair")
-
-    def chip_decay(of):
-        return dec_wide[pl.ds(pl.multiple_of(16 * of, 16), 8), half_lanes(k)] * dec_wide[
-            pl.ds(pl.multiple_of(16 * of + 8, 8), 8), half_lanes(k)]
-
-    decay_second = dec_wide[pl.ds(pl.multiple_of(16 * z + 8, 8), 8), half_lanes(k)][0:1, :]
+    def half_lanes(h):
+        return pl.ds(h * 640, 640)
+
+    rows_mine = pl.ds(pl.multiple_of(64 * k, 64), 64)
+    rows_other = pl.ds(pl.multiple_of(64 * (1 - k), 64), 64)
+
+    def pair(h):
+        send(state.at[rows_other, half_lanes(h)], peer_state.at[:, half_lanes(h)], "pair%d" % h, core)
+
+    arrived(b_lanes(far, 0), "b4")
+    arrived(b_lanes(far, 64), "b5")
+    lax.fori_loop(2, 4, shared(0), 0)
+    for piece in pieces:
+        arrived(x_lanes(far, 0, piece), "x4%d" % piece[0])
+        arrived(x_lanes(far, 64, piece), "x5%d" % piece[0])
+        lax.fori_loop(2, 4, block(*piece), 0)
+        if piece[0] == 0:
+            pair(0)
+    pair(1)
+
+    decay_second = dec_wide[pl.ds(pl.multiple_of(16 * z + 8, 8), 8), :]
     weight_mine = jnp.where(k == 0, decay_second, jnp.ones_like(decay_second))
     weight_peer = jnp.where(k == 0, jnp.ones_like(decay_second), decay_second)
 
-    def pack_state(i, carry):
-        rows = pl.ds(pl.multiple_of(i * 16, 16), 16)
-        both = weight_mine * state[rows, half_lanes(k)] + weight_peer * peer_state[rows, :]
-        st_send[i] = both.astype(BF16)
-        return carry
-
-    lax.fori_loop(0, 8, pack_state, 0)
-
-    def state_copy(j):
-        return pltpu.make_async_remote_copy(
-            src_ref=st_send.at[chip_at(j - 1)], dst_ref=st_recv.at[z],
-            send_sem=sc, recv_sem=rc_, device_id=chip_peer(j), device_id_type=MESH)
-
-    exchange(state_copy, 8)
-    st_recv[z] = st_send[z]
+    def state_copy(h):
+        def of(j):
+            return pltpu.make_async_remote_copy(
+                src_ref=st_send.at[h, chip_at(j - 1)], dst_ref=st_recv.at[h, z],
+                send_sem=sc.at[h], recv_sem=rc_.at[h], device_id=chip_peer(j), device_id_type=MESH)
+
+        return of
+
+    for h in range(2):
+        arrived(peer_state.at[:, half_lanes(h)], "pair%d" % h)
+        first_lane, last_lane = h * 640, h * 640 + 640
+
+        def pack_state(i, carry):
+            rows = pl.ds(pl.multiple_of(64 * k + i * 8, 8), 8)
+            rows_peer = pl.ds(pl.multiple_of(i * 8, 8), 8)
+            both = (weight_mine[:, first_lane:last_lane] * state[rows, half_lanes(h)]
+                    + weight_peer[:, first_lane:last_lane] * peer_state[rows_peer, half_lanes(h)])
+            st_send[h, i] = both.astype(BF16)
+            return carry
+
+        lax.fori_loop(0, 8, pack_state, 0)
+        exchange(state_copy(h), 8)
+        st_recv[h, z] = st_send[h, z]
 
     arrived(w_part(mine + 320, 320, down_y), "w2")
     send(w_part(mine, 640, down_y), w_part(mine, 640, down_y), "w6", core)
     arrived(w_part(mine, 320, up_y), "w3")
     send(w_part(mine, 640, up_y), w_part(mine, 640, up_y), "w7", core)
     far_forward(z_rows, zr, "z")
+    gate_near(64)
+
+    arrived(c_lanes(left, 64), "c2")
+    arrived(c_lanes(right, 0), "c3")
+    arrived(c_lanes(far, 0), "c4")
+    arrived(c_lanes(far, 64), "c5")
+    lax.fori_loop(0, 4, shared(1), 0)
 
     def inside(p, carry):
         b_now, c_now = bcc[p, :, 0:128], bcc[p, :, 128:256]
@@ -451,23 +498,27 @@
             y_in[p, :, pl.ds(q * 128, 128)] = dot(both, x_two) + x_pair * skip[0:1, pl.ds(q * 128, 128)]
         return carry
 
-    lax.fori_loop(0, 4, inside, 0)
-
-    settle(st_recv, rc_, 7)
-
-    def chain(i, held):
-        back_send[i] = held.astype(BF16)
-        return chip_decay(i)[0:1, :] * held + st_recv[i].astype(F32)
-
-    lax.fori_loop(0, 8, chain, jnp.zeros((16, 640), F32))
-
-    def back_copy(j):
-        return pltpu.make_async_remote_copy(
-            src_ref=back_send.at[chip_at(j - 1)], dst_ref=back_recv.at[z],
-            send_sem=sb, recv_sem=rb, device_id=chip_peer(j), device_id_type=MESH)
-
-    exchange(back_copy, 8)
-    back_recv[z] = back_send[z]
+    def back_copy(h):
+        def of(j):
+            return pltpu.make_async_remote_copy(
+                src_ref=back_send.at[h, chip_at(j - 1)], dst_ref=back_recv.at[h, z],
+                send_sem=sb.at[h], recv_sem=rb.at[h], device_id=chip_peer(j), device_id_type=MESH)
+
+        return of
+
+    for h in range(2):
+        lax.fori_loop(2 * h, 2 * h + 2, inside, 0)
+        settle(st_recv.at[h, pl.ds(0, 7)], rc_.at[h])
+
+        def chain(i, held):
+            back_send[h, i] = held.astype(BF16)
+            decay = dec_wide[pl.ds(pl.multiple_of(16 * i, 8), 8), half_lanes(h)] * dec_wide[
+                pl.ds(pl.multiple_of(16 * i + 8, 8), 8), half_lanes(h)]
+            return decay * held + st_recv[h, i].astype(F32)
+
+        lax.fori_loop(0, 8, chain, jnp.zeros((8, 640), F32))
+        exchange(back_copy(h), 8)
+        back_recv[h, z] = back_send[h, z]
 
     def starts(j, carry):
         held = jnp.zeros((STATE, 128), F32)
@@ -483,31 +534,29 @@
     arrived(w_part(mine + 320, 320, far_y), "w5")
     send(w_part(mine, 640, far_y), w_part(mine, 640, far_y), "w8", core)
 
-    local["gate"].wait()
-    near_wait(z_rows, "z")
-    far_wait(z_rows, "z")
-    settle(back_recv, rb, 7)
-
-    decay_first = dec_wide[pl.ds(pl.multiple_of(16 * z, 8), 8), half_lanes(k)][0:1, :]
-
-    def unpack_state(i, carry):
-        rows = pl.ds(pl.multiple_of(i * 16, 16), 16)
-        first = back_recv[i].astype(F32)
-        span = jnp.where(k == 0, state[rows, half_lanes(k)], peer_state[rows, :])
-        second = decay_first * first + span
-        s_in[rows, half_lanes(k)] = jnp.where(k == 0, first, second)
-        in_send[rows, :] = jnp.where(k == 0, second, first).astype(BF16)
-        return carry
-
-    lax.fori_loop(0, 8, unpack_state, 0)
-    send(in_send, in_recv, "in", core)
+    for h in range(2):
+        settle(back_recv.at[h, pl.ds(0, 7)], rb.at[h])
+        decay_first = dec_wide[pl.ds(pl.multiple_of(16 * z, 8), 8), half_lanes(h)]
+
+        def unpack_state(i, carry):
+            rows = pl.ds(pl.multiple_of(64 * k + i * 8, 8), 8)
+            rows_peer = pl.ds(pl.multiple_of(i * 8, 8), 8)
+            first = back_recv[h, i].astype(F32)
+            span = jnp.where(k == 0, state[rows, half_lanes(h)], peer_state[rows_peer, half_lanes(h)])
+            second = decay_first * first + span
+            s_in[rows, half_lanes(h)] = jnp.where(k == 0, first, second)
+            in_send[rows_peer, half_lanes(h)] = jnp.where(k == 0, second, first)
+            return carry
+
+        lax.fori_loop(0, 8, unpack_state, 0)
+        send(in_send.at[:, half_lanes(h)], s_in.at[rows_mine, half_lanes(h)], "in%d" % h, core)
 
     local["w"].wait()
     arrived(w_part(other, 640, down_y), "w6")
     arrived(w_part(other, 640, up_y), "w7")
     arrived(w_part(other, 640, far_y), "w8")
-    arrived(in_recv, "in")
-    s_in[:, half_lanes(1 - k)] = in_recv[...].astype(F32)
+    for h in range(2):
+        arrived(s_in.at[rows_other, half_lanes(h)], "in%d" % h)
 
     def finish(i, carry):
         p = lax.rem(t + i, 4)
@@ -552,6 +601,7 @@
         piece = piece_at(rs_recv, which, i)
         pltpu.make_async_copy(piece, piece, rr.at[5 * which + i]).wait()
 
+    far_wait(z_rows, "z")
     lax.fori_loop(2, 3, finish, 0)
     for i in range(5):
         project(far, 0, to_slot(0), i, 1)
@@ -559,12 +609,14 @@
         if i < 3:
             ship(0, right, i)
             ship(1, left, i)
+    local["gate"].wait()
+    for first in (0, 64):
+        arrived(z_rows(left, first, 64), "z2%d" % first)
+        arrived(z_rows(right, first, 64), "z3%d" % first)
     lax.fori_loop(3, 6, finish, 0)
     ap_recv[t] = ap_send[t]
-    for j in (2, 1, 3):
-        peer = lax.rem(t + j, 4)
-        send(sq.at[t], sq.at[t], "q%d" % j, {"tensor": peer})
-        send(ap_send.at[peer], ap_recv.at[t], "a%d" % j, {"tensor": peer})
+    send_triple(lambda j: (sq.at[t], sq.at[t], {"tensor": tensor_peer(j)}), 2)
+    send_triple(lambda j: (ap_send.at[tensor_peer(j)], ap_recv.at[t], {"tensor": tensor_peer(j)}), 3)
     for i in range(3, 5):
         ship(0, right, i)
         ship(1, left, i)
@@ -574,11 +626,9 @@
         project(left, 0, to_slot(3), i, 1)
         ship(3, left, i)
 
-    for j in range(1, 4):
-        source = lax.rem(t + 4 - j, 4)
-        arrived(gt.at[source], "g%d" % j)
-        arrived(sq.at[source], "q%d" % j)
-        arrived(ap_recv.at[source], "a%d" % j)
+    settle(gt.at[pl.ds(0, 3)], r3.at[1])
+    settle(sq.at[pl.ds(0, 3)], r3.at[2])
+    settle(ap_recv.at[pl.ds(0, 3)], r3.at[3])
 
     def row_scale(p):
         rows = pl.ds(p, 1)
@@ -615,24 +665,21 @@
         project(left, 1, to_slot(5, 1), i, 1)
         ship(5, left, i)
 
-    settle(v_recv, rv)
+    settle(v_recv.at[pl.ds(0, 15)], rv)
 
     def add_v(i, held):
         return held + v_recv[i].astype(F32)
 
     y_recv[s] = lax.fori_loop(0, 16, add_v, jnp.zeros((2, RANK, 128), F32))
-    for j in range(1, 4):
-        send(y_recv.at[s], y_recv.at[s], "y%d" % j, {"fsdp": lax.rem(s + j, 4)})
+    send_triple(lambda j: (y_recv.at[s], y_recv.at[s], {"fsdp": lax.rem(s + j, 4)}), 4)
     for i in range(1, 5):
         landed(0, i)
         project(right, 0, to_slot(4, 0), i, 1)
         landed(1, i)
         project(left, 1, to_slot(5, 1), i, 1)
-    for j in range(1, 4):
-        arrived(y_recv.at[lax.rem(s + 4 - j, 4)], "y%d" % j)
+    settle(y_recv.at[pl.ds(0, 3)], r3.at[4])
     t_recv[t] = ((y_recv[0] + y_recv[1]) + (y_recv[2] + y_recv[3])).astype(BF16)
-    for j in range(1, 4):
-        send(t_recv.at[t], t_recv.at[t], "t%d" % j, {"tensor": lax.rem(t + j, 4)})
+    send_triple(lambda j: (t_recv.at[t], t_recv.at[t], {"tensor": tensor_peer(j)}), 5)
     for i in range(1, 5):
         ship(4, right, i)
         ship(5, left, i)
@@ -647,8 +694,7 @@
     project(t, 0, own_part(0))
     project(t, 1, own_part(1))
 
-    for j in range(1, 4):
-        arrived(t_recv.at[lax.rem(t + 4 - j, 4)], "t%d" % j)
+    settle(t_recv.at[pl.ds(0, 3)], r3.at[5])
 
     def add_t(i, held):
         keep = jnp.where(jnp.logical_or(c >= 5, i == t), 1.0, 0.0)
@@ -678,7 +724,7 @@
     lax.fori_loop(0, 10, close, 0)
     copy_here("mixed", mixed_here, mixed)
 
-    settle(v_all, rg)
+    settle(v_all.at[pl.ds(0, 15)], rg)
     for i in range(10):
         a_here[:, i * 128 : i * 128 + 128] = v_all[i // 2, i % 2].astype(F32)
     for i in range(20):
@@ -686,14 +732,21 @@
     copy_here("grad_a", a_here, grad_a)
     copy_here("grad_b", b_here, grad_b)
 
-    settle(dec_all, sd)
-    settle(st_send, sc, 7)
-    settle(back_send, sb, 7)
-    settle(v_send, sv)
-    settle(v_all, sg)
+    for which, buffer in enumerate((dt_all, gt, sq, ap_send, y_recv, t_recv)):
+        settle(buffer.at[pl.ds(0, 3)], s3.at[which])
+    settle(dec_all.at[pl.ds(0, 15)], sd)
+    for h in range(2):
+        settle(st_send.at[h, pl.ds(0, 7)], sc.at[h])
+        settle(back_send.at[h, pl.ds(0, 7)], sb.at[h])
+    settle(v_send.at[pl.ds(0, 15)], sv)
+    settle(v_all.at[pl.ds(0, 15)], sg)
     pltpu.make_async_copy(rs_send, rs_send, sr).wait()
+    pltpu.make_async_copy(x_ext.at[pl.ds(16, 512)], x_ext.at[pl.ds(16, 512)], sgroup.at[0]).wait()
+    pltpu.make_async_copy(gate, gate, sgroup.at[1]).wait()
+    pltpu.make_async_copy(wt.at[:, pl.ds(0, 1920)], wt.at[:, pl.ds(0, 1920)], sgroup.at[2]).wait()
     for copy in started:
         copy.wait_send()
+    assert len(slots) <= 43 and len(send_slots) <= 14 and len(local) <= 15
 
     @pl.when(gives_rim)
     def _():
@@ -752,15 +805,14 @@
             pltpu.VMEM((4, STATE, WIDTH), F32),
             pltpu.VMEM((4, 8, WIDTH), F32),
             pltpu.VMEM((STATE, WIDTH), F32),
-            pltpu.VMEM((STATE, 640), F32),
-            pltpu.VMEM((8, 16, 640), BF16),
-            pltpu.VMEM((8, 16, 640), BF16),
+            pltpu.VMEM((64, WIDTH), F32),
+            pltpu.VMEM((2, 8, 8, 640), BF16),
+            pltpu.VMEM((2, 8, 8, 640), BF16),
             pltpu.VMEM((16, 8, 128), F32),
             pltpu.VMEM((128, WIDTH), F32),
-            pltpu.VMEM((8, 16, 640), BF16),
-            pltpu.VMEM((8, 16, 640), BF16),
-            pltpu.VMEM((STATE, 640), BF16),
-            pltpu.VMEM((STATE, 640), BF16),
+            pltpu.VMEM((2, 8, 8, 640), BF16),
+            pltpu.VMEM((2, 8, 8, 640), BF16),
+            pltpu.VMEM((64, WIDTH), F32),
             pltpu.VMEM((STATE, WIDTH), F32),
             pltpu.VMEM((4, ROWS, WIDTH), BF16),
             pltpu.VMEM((4, RANK, 128), F32),
@@ -778,8 +830,8 @@
             pltpu.VMEM((ROWS, OUT), BF16),
             pltpu.VMEM((RANK, WIDTH), F32),
             pltpu.VMEM((RANK, OUT), F32),
-            dma((60,)), dma((60,)), dma((26,)),
-            dma, dma, dma, dma, dma, dma, dma, dma, dma, dma, dma, dma((10,)), dma((4,)),
+            dma((14,)), dma((43,)), dma((23,)),
+            dma((2,)), dma((2,)), dma, dma, dma((2,)), dma((2,)), dma, dma, dma, dma, dma, dma((10,)), dma((4,)), dma((3,)), dma((6,)), dma((6,)), dma,
         ],
         compiler_params=pltpu.CompilerParams(
             collective_id=0, has_side_effects=True, vmem_limit_bytes=64 * 1000 * 1000),

time: 78.9 us -> 75.2 us (0.953)
  Pallas kernels: 74.8 us -> 71.1 us
    pallas_call x1, Pallas kernels: 74.8 us -> 71.1 us  [shards(): pl.pallas_call(kernel, out_shape=(jax.ShapeDtypeStruct((ROWS, OUT), BF16)...]
where the time goes in v5:
time: 75.2 us; the launch traced here: 75.1 us
  Pallas kernels  71.1 us (95%)
  local copies, waits for them, and re-layouts  3.32 us (4%)
    pallas_call x1, Pallas kernels, shards(): pl.pallas_call(kernel, out_shape=(jax.ShapeDtypeStruct((ROWS, OUT), BF16)...  71.1 us
    unnamed x7, local copies, waits for them, and re-layouts  3.32 us

profile of v5, /device:TPU:1, one launch (start us, length us, event | category | flops | bytes accessed | tf_op | source)
XLA Modules:
  0.0 75.1 jit_solution(9521545526884013223)
XLA Ops:
  0.6 71.1 %shard_map.157 = (bf16[128,2560]{1,0:T(8,128)(2,1)}, f32[16,1280]{1,0:T(8,128)}, f32[16,2560]{1,0:T(8,128)}) custom-call(bf16[128,5120]{1,0:T(8,128)(2,1)} %bitcast.15, bf16[128,256]{1,0:T(8,128)(2,1)} %bitcast.20, bf16[128,5120]{1,0:T(8,128)(2,1)} %bitcast.16, bf16[80,128]{1,0:T(8,128)(2,1)} %bitcast.23, bf16[1280,640]{1,0:T(8,128)(2,1)} %w_in.1, ...), custom_call_target="tpu_custom_call" | custom-call | tf_op jit(solution)/shard_map/pallas_call | solution.py:766
  71.8 0.0 copy-start.1
  71.8 0.0 copy-start
  71.8 2.0 %copy.20 = bf16[1,128,2560]{2,1,0:T(8,128)(2,1)} copy(bf16[1,128,2560]{2,1,0:T(8,128)(2,1)} %bitcast.18) | data formatting | bytes 1310720
  73.8 0.0 copy-done.1
  73.8 0.6 copy.21
  74.4 0.0 copy-done
  74.4 0.7 copy.22
Async XLA Ops:
  71.8 2.0 %copy-start.1 = (f32[16,1280]{1,0:T(8,128)S(1)}, f32[16,1280]{1,0:T(8,128)}, u32[]{:S(2)}) copy-start(f32[16,1280]{1,0:T(8,128)} %get-tuple-element.7) | copy-start | bytes 245764
  71.8 2.7 %copy-start = (f32[16,2560]{1,0:T(8,128)S(1)}, f32[16,2560]{1,0:T(8,128)}, u32[]{:S(2)}) copy-start(f32[16,2560]{1,0:T(8,128)} %get-tuple-element.14) | copy-start | bytes 491524

commit v6 on v5

--- a/solution.py
+++ b/solution.py
@@ -46,7 +46,7 @@
     st_send, st_recv, dec_all, dec_wide, back_send, back_recv, in_send, s_in,
     gated, gt, sq, ap_send, ap_recv,
     rs_send, rs_recv, own,
-    v_send, v_recv, y_recv, t_recv, v_all, mixed_here, a_here, b_here,
+    v_send, v_recv, y_recv, t_recv, v_all,
     sx, rx, sl, sc, rc_, sd, rd, sb, rb, sv, rv, sg, rg, sr, rr, rr_end, sgroup, s3, r3, s_head,
 ):
     z, k = lax.axis_index("context_0"), lax.axis_index("context_1")
@@ -57,13 +57,16 @@
     started = []
     slots, send_slots = {}, {}
 
+    together = {"c3": "c2", "c4": "c2", "c5": "c2", "z30": "z20", "z264": "z20", "z364": "z20",
+                "b5": "b4", "x3": "x2", "w7": "w6", "w8": "w6"}
+
     def slot(name):
-        return slots.setdefault(name, len(slots))
+        return slots.setdefault(together.get(name, name), len(slots))
 
     def send_slot(name):
         return send_slots.setdefault(name, len(send_slots))
 
-    groups = {"x": 0, "z": 1, "w": 2}
+    groups = {"x": 0, "z": 1, "w": 2, "c": 3, "p": 4, "i": 5}
 
     def send(src, dst, name, where):
         grouped = groups.get(name[0])
@@ -168,7 +171,7 @@
     local = {}
 
     def copy_here(name, src, dst):
-        local[name] = pltpu.make_async_copy(src, dst, sl.at[8 + len(local)])
+        local[name] = pltpu.make_async_copy(src, dst, sl.at[2 + len(local)])
         local[name].start()
 
     copy_here("cot", cot_in, cot)
@@ -231,10 +234,6 @@
         arrived(relay.at[1], name + "1")
         send(relay.at[1], rows(right, 64, 64), name + "5", {"tensor": left})
 
-    def near_wait(rows, name):
-        arrived(rows(left, 0, ROWS), name + "2")
-        arrived(rows(right, 0, ROWS), name + "3")
-
     def far_wait(rows, name):
         arrived(rows(far, 0, 64), name + "4")
         arrived(rows(far, 64, 64), name + "5")
@@ -245,10 +244,10 @@
             where = {"context_0": lax.div(after, 2), "context_1": lax.rem(after, 2), "tensor": p}
             copies.append(pltpu.make_async_remote_copy(
                 src_ref=x_in.at[pl.ds(120, 8), pl.ds(p * WIDTH, WIDTH)], dst_ref=rim_x,
-                send_sem=sl.at[p], recv_sem=rx.at[slot("rim_x")], device_id=where, device_id_type=MESH))
+                send_sem=sl.at[0], recv_sem=rx.at[slot("rim_x")], device_id=where, device_id_type=MESH))
             copies.append(pltpu.make_async_remote_copy(
                 src_ref=bc_in.at[pl.ds(120, 8)], dst_ref=rim_b,
-                send_sem=sl.at[4 + p], recv_sem=rx.at[slot("rim_b")], device_id=where, device_id_type=MESH))
+                send_sem=sl.at[1], recv_sem=rx.at[slot("rim_b")], device_id=where, device_id_type=MESH))
         return copies
 
     @pl.when(gives_rim)
@@ -415,7 +414,7 @@
     arrived(b_lanes(left, 64), "b2")
     arrived(b_lanes(right, 0), "b3")
     lax.fori_loop(0, 2, shared(0), 0)
-    near_wait(x_rows, "x")
+    arrived(x_ext.at[pl.ds(16, 256)], "x2")
     lax.fori_loop(0, 2, block(0, 10), 0)
     core = {"context_1": 1 - k}
 
@@ -428,8 +427,7 @@
     def pair(h):
         send(state.at[rows_other, half_lanes(h)], peer_state.at[:, half_lanes(h)], "pair%d" % h, core)
 
-    arrived(b_lanes(far, 0), "b4")
-    arrived(b_lanes(far, 64), "b5")
+    arrived(bc_ext.at[pl.ds(16, 128), pl.ds(0, 128)], "b4")
     lax.fori_loop(2, 4, shared(0), 0)
     for piece in pieces:
         arrived(x_lanes(far, 0, piece), "x4%d" % piece[0])
@@ -467,17 +465,7 @@
         exchange(state_copy(h), 8)
         st_recv[h, z] = st_send[h, z]
 
-    arrived(w_part(mine + 320, 320, down_y), "w2")
-    send(w_part(mine, 640, down_y), w_part(mine, 640, down_y), "w6", core)
-    arrived(w_part(mine, 320, up_y), "w3")
-    send(w_part(mine, 640, up_y), w_part(mine, 640, up_y), "w7", core)
-    far_forward(z_rows, zr, "z")
-    gate_near(64)
-
-    arrived(c_lanes(left, 64), "c2")
-    arrived(c_lanes(right, 0), "c3")
-    arrived(c_lanes(far, 0), "c4")
-    arrived(c_lanes(far, 64), "c5")
+    arrived(bc_ext.at[pl.ds(16, 256), pl.ds(0, 128)], "c2")
     lax.fori_loop(0, 4, shared(1), 0)
 
     def inside(p, carry):
@@ -508,6 +496,9 @@
 
     for h in range(2):
         lax.fori_loop(2 * h, 2 * h + 2, inside, 0)
+        if h == 0:
+            far_forward(z_rows, zr, "z")
+            gate_near(64)
         settle(st_recv.at[h, pl.ds(0, 7)], rc_.at[h])
 
         def chain(i, held):
@@ -530,11 +521,25 @@
 
     lax.fori_loop(0, 10, starts, 0)
 
+    arrived(w_part(mine + 320, 320, down_y), "w2")
+    send(w_part(mine, 640, down_y), w_part(mine, 640, down_y), "w6", core)
+    arrived(w_part(mine, 320, up_y), "w3")
+    send(w_part(mine, 640, up_y), w_part(mine, 640, up_y), "w7", core)
     arrived(w_part(mine, 320, far_y), "w4")
     arrived(w_part(mine + 320, 320, far_y), "w5")
     send(w_part(mine, 640, far_y), w_part(mine, 640, far_y), "w8", core)
 
+    def prepare():
+        far_wait(z_rows, "z")
+        factor = silu(gate[far].astype(F32))
+        reach = widen(jnp.exp(cum[far]))
+        y_in[far] = (y_in[far] + reach * dot(bcc[far, :, 128:256], blocks[far].astype(BF16))) * factor
+        weights[far] = reach * factor
+        tails[far] = widen(jnp.exp(log_start[far]))
+
     for h in range(2):
+        if h == 1:
+            prepare()
         settle(back_recv.at[h, pl.ds(0, 7)], rb.at[h])
         decay_first = dec_wide[pl.ds(pl.multiple_of(16 * z, 8), 8), half_lanes(h)]
 
@@ -552,23 +557,23 @@
         send(in_send.at[:, half_lanes(h)], s_in.at[rows_mine, half_lanes(h)], "in%d" % h, core)
 
     local["w"].wait()
-    arrived(w_part(other, 640, down_y), "w6")
-    arrived(w_part(other, 640, up_y), "w7")
-    arrived(w_part(other, 640, far_y), "w8")
+    arrived(wt.at[pl.ds(0, 640), pl.ds(0, 1920)], "w6")
     for h in range(2):
         arrived(s_in.at[rows_other, half_lanes(h)], "in%d" % h)
+
+    def close_block(p, now):
+        squares = (now * now).astype(BF16)
+        sq[t, pl.ds(p, 1), :] = dot(jnp.ones((8, WIDTH), BF16), squares, NT)[0:1, :]
+        out = (now * gain[...]).astype(BF16)
+        gated[p] = out
+        ap_send[p] = dot(down_t[...], out, NT).astype(BF16)
 
     def finish(i, carry):
         p = lax.rem(t + i, 4)
         start = blocks[p] + widen(jnp.exp(log_start[p]))[0:1, :] * s_in[...]
         reach = widen(jnp.exp(cum[p]))
         y_now = y_in[p] + reach * dot(bcc[p, :, 128:256], start.astype(BF16))
-        now = y_now * silu(gate[p].astype(F32))
-        squares = (now * now).astype(BF16)
-        sq[t, pl.ds(p, 1), :] = dot(jnp.ones((8, WIDTH), BF16), squares, NT)[0:1, :]
-        out = (now * gain[...]).astype(BF16)
-        gated[p] = out
-        ap_send[p] = dot(down_t[...], out, NT)
+        close_block(p, y_now * silu(gate[p].astype(F32)))
         return carry
 
     def project(p, half, store, first=0, count=5):
@@ -601,8 +606,8 @@
         piece = piece_at(rs_recv, which, i)
         pltpu.make_async_copy(piece, piece, rr.at[5 * which + i]).wait()
 
-    far_wait(z_rows, "z")
-    lax.fori_loop(2, 3, finish, 0)
+    incoming = (tails[far, 0:1, :] * s_in[...]).astype(BF16)
+    close_block(far, y_in[far] + weights[far] * dot(bcc[far, :, 128:256], incoming))
     for i in range(5):
         project(far, 0, to_slot(0), i, 1)
         project(far, 1, to_slot(1), i, 1)
@@ -610,9 +615,7 @@
             ship(0, right, i)
             ship(1, left, i)
     local["gate"].wait()
-    for first in (0, 64):
-        arrived(z_rows(left, first, 64), "z2%d" % first)
-        arrived(z_rows(right, first, 64), "z3%d" % first)
+    arrived(gate.at[pl.ds(0, 2)], "z20")
     lax.fori_loop(3, 6, finish, 0)
     ap_recv[t] = ap_send[t]
     send_triple(lambda j: (sq.at[t], sq.at[t], {"tensor": tensor_peer(j)}), 2)
@@ -635,7 +638,8 @@
         squares = (sq[0, rows, :] + sq[1, rows, :]) + (sq[2, rows, :] + sq[3, rows, :])
         return lax.rsqrt(squares * (1.0 / 5120.0) + EPS)
 
-    adapter = ((ap_recv[0] + ap_recv[1]) + (ap_recv[2] + ap_recv[3])).astype(BF16)
+    part = [ap_recv[i].astype(F32) for i in range(4)]
+    adapter = ((part[0] + part[1]) + (part[2] + part[3])).astype(BF16)
     own_scale = row_scale(t)
     weighted = (scale * own_scale[0:1, :] * adapter.astype(F32)).astype(BF16)
     grad_a_now = jnp.zeros((RANK, WIDTH), F32)
@@ -717,20 +721,17 @@
         lanes = tile(i)
         first = own[0, :, lanes] + rs_recv[4, :, lanes].astype(F32) + rs_recv[3, :, lanes].astype(F32)
         second = own[1, :, lanes] + rs_recv[2, :, lanes].astype(F32) + rs_recv[5, :, lanes].astype(F32)
-        mixed_here[:, lanes] = (scale_col * first).astype(BF16)
-        mixed_here[:, pl.ds(pl.multiple_of(HALF + i * 128, 128), 128)] = (scale_col * second).astype(BF16)
+        mixed[:, lanes] = (scale_col * first).astype(BF16)
+        mixed[:, pl.ds(pl.multiple_of(HALF + i * 128, 128), 128)] = (scale_col * second).astype(BF16)
         return carry
 
     lax.fori_loop(0, 10, close, 0)
-    copy_here("mixed", mixed_here, mixed)
 
     settle(v_all.at[pl.ds(0, 15)], rg)
     for i in range(10):
-        a_here[:, i * 128 : i * 128 + 128] = v_all[i // 2, i % 2].astype(F32)
+        grad_a[:, i * 128 : i * 128 + 128] = v_all[i // 2, i % 2].astype(F32)
     for i in range(20):
-        b_here[:, i * 128 : i * 128 + 128] = v_all[5 + i // 2, i % 2].astype(F32)
-    copy_here("grad_a", a_here, grad_a)
-    copy_here("grad_b", b_here, grad_b)
+        grad_b[:, i * 128 : i * 128 + 128] = v_all[5 + i // 2, i % 2].astype(F32)
 
     for which, buffer in enumerate((dt_all, gt, sq, ap_send, y_recv, t_recv)):
         settle(buffer.at[pl.ds(0, 3)], s3.at[which])
@@ -743,35 +744,36 @@
     pltpu.make_async_copy(rs_send, rs_send, sr).wait()
     pltpu.make_async_copy(x_ext.at[pl.ds(16, 512)], x_ext.at[pl.ds(16, 512)], sgroup.at[0]).wait()
     pltpu.make_async_copy(gate, gate, sgroup.at[1]).wait()
+    settle(bc_ext.at[pl.ds(16, 256), pl.ds(0, 128)], sgroup.at[3])
+    settle(peer_state, sgroup.at[4])
+    settle(in_send, sgroup.at[5])
     pltpu.make_async_copy(wt.at[:, pl.ds(0, 1920)], wt.at[:, pl.ds(0, 1920)], sgroup.at[2]).wait()
     for copy in started:
         copy.wait_send()
-    assert len(slots) <= 43 and len(send_slots) <= 14 and len(local) <= 15
+    assert len(slots) <= 33 and len(send_slots) <= 6 and len(local) <= 12
 
     @pl.when(gives_rim)
     def _():
-        for copy in rim_copies():
-            copy.wait_send()
-
-    for name in ("mixed", "grad_a", "grad_b"):
-        local[name].wait()
+        settle(x_ext.at[pl.ds(16, 32)], sl.at[0])
+        settle(bc_ext.at[pl.ds(16, 32)], sl.at[1])
 
 
 def shards(
     input_raw, state_proj_raw, gate_branch, step_raw, convolution_taps, convolution_bias, step_bias,
     decay_log_rate, skip_weight, gated_norm_gain, output_weight, adapter_down, adapter_up, cotangent,
 ):
-    hbm = pl.BlockSpec(memory_space=pl.ANY)
+    hbm = pl.BlockSpec(memory_space=pltpu.HBM)
+    vmem = pl.BlockSpec(memory_space=pltpu.VMEM)
     dma = pltpu.SemaphoreType.DMA
     mixed, grad_a, grad_b = pl.pallas_call(
         kernel,
         out_shape=(
-            jax.ShapeDtypeStruct((ROWS, OUT), BF16),
-            jax.ShapeDtypeStruct((RANK, WIDTH), F32),
-            jax.ShapeDtypeStruct((RANK, OUT), F32),
+            pltpu.VMEM((ROWS, OUT), BF16),
+            pltpu.VMEM((RANK, WIDTH), F32),
+            pltpu.VMEM((RANK, OUT), F32),
         ),
         in_specs=[hbm] * 14,
-        out_specs=(hbm, hbm, hbm),
+        out_specs=(vmem, vmem, vmem),
         scratch_shapes=[
             pltpu.VMEM((16 + 512, WIDTH), BF16),
             pltpu.VMEM((2, 64, WIDTH), BF16),
@@ -817,8 +819,8 @@
             pltpu.VMEM((4, ROWS, WIDTH), BF16),
             pltpu.VMEM((4, RANK, 128), F32),
             pltpu.VMEM((4, 8, 128), F32),
-            pltpu.VMEM((4, RANK, 128), F32),
-            pltpu.VMEM((4, RANK, 128), F32),
+            pltpu.VMEM((4, RANK, 128), BF16),
+            pltpu.VMEM((4, RANK, 128), BF16),
             pltpu.VMEM((6, ROWS, HALF), BF16),
             pltpu.VMEM((6, ROWS, HALF), BF16),
             pltpu.VMEM((2, ROWS, HALF), F32),
@@ -827,14 +829,11 @@
             pltpu.VMEM((4, 2, RANK, 128), F32),
             pltpu.VMEM((4, 2, RANK, 128), BF16),
             pltpu.VMEM((16, 2, RANK, 128), BF16),
-            pltpu.VMEM((ROWS, OUT), BF16),
-            pltpu.VMEM((RANK, WIDTH), F32),
-            pltpu.VMEM((RANK, OUT), F32),
-            dma((14,)), dma((43,)), dma((23,)),
-            dma((2,)), dma((2,)), dma, dma, dma((2,)), dma((2,)), dma, dma, dma, dma, dma, dma((10,)), dma((4,)), dma((3,)), dma((6,)), dma((6,)), dma,
+            dma((6,)), dma((33,)), dma((14,)),
+            dma((2,)), dma((2,)), dma, dma, dma((2,)), dma((2,)), dma, dma, dma, dma, dma, dma((10,)), dma((4,)), dma((6,)), dma((6,)), dma((6,)), dma,
         ],
         compiler_params=pltpu.CompilerParams(
-            collective_id=0, has_side_effects=True, vmem_limit_bytes=64 * 1000 * 1000),
+            collective_id=0, has_side_effects=True, vmem_limit_bytes=60 * 1000 * 1000),
     )(
         input_raw[0], state_proj_raw[0], gate_branch[0], step_raw[0].T, output_weight, cotangent[0],
         convolution_taps, convolution_bias.reshape(42, 128), step_bias[None, :], decay_log_rate[None, :],

time: 75.2 us -> 72.8 us (0.968)
  Pallas kernels: 71.1 us -> 69.9 us
  local copies, waits for them, and re-layouts: 3.32 us -> 2.14 us
    pallas_call x1, Pallas kernels: 71.1 us -> 69.9 us  [shards(): pl.pallas_call(kernel, out_shape=(pltpu.VMEM((ROWS, OUT), BF16), pltpu.VM...]
    unnamed x7 -> x3, local copies, waits for them, and re-layouts: 3.32 us -> 2.14 us
where the time goes in v6:
time: 72.8 us; the launch traced here: 72.7 us
  Pallas kernels  69.9 us (96%)
  local copies, waits for them, and re-layouts  2.14 us (3%)
    pallas_call x1, Pallas kernels, shards(): pl.pallas_call(kernel, out_shape=(pltpu.VMEM((ROWS, OUT), BF16), pltpu.VM...  69.9 us
    unnamed x3, local copies, waits for them, and re-layouts  2.14 us

profile of v6, /device:TPU:1, one launch (start us, length us, event | category | flops | bytes accessed | tf_op | source)
XLA Modules:
  0.0 72.7 jit_solution(121098380433436205)
XLA Ops:
  0.6 69.9 %shard_map.157 = (bf16[128,2560]{1,0:T(8,128)(2,1)S(1)}, f32[16,1280]{1,0:T(8,128)S(1)}, f32[16,2560]{1,0:T(8,128)S(1)}) custom-call(bf16[128,5120]{1,0:T(8,128)(2,1)} %bitcast.17, bf16[128,256]{1,0:T(8,128)(2,1)} %bitcast.20, bf16[128,5120]{1,0:T(8,128)(2,1)} %bitcast.18, bf16[80,128]{1,0:T(8,128)(2,1)} %bitcast.23, bf16[1280,640]{1,0:T(8,128)(2,1)} %w_in.1, ...), custom_call_target="tpu_custom_call" | custom-call | tf_op jit(solution)/shard_map/pallas_call | solution.py:768
  70.6 0.8 %copy.20 = bf16[1,128,2560]{2,1,0:T(8,128)(2,1)} copy(bf16[1,128,2560]{2,1,0:T(8,128)(2,1)S(1)} %bitcast.15) | data formatting | bytes 1310720
  71.4 0.6 copy.21
  72.1 0.7 copy.22

commit v7 on v6

--- a/solution.py
+++ b/solution.py
@@ -40,7 +40,7 @@
 def kernel(
     x_in, bc_in, z_in, dt_in, w_in, cot_in, taps_in, bias_in, step_bias_in, rate_in, skip_in, gain_in, down_in, up_in,
     mixed, grad_a, grad_b,
-    x_ext, xr, rim_x, rim_b, xc, bc_ext, bcc, dt_all, gate, zr, wt, cot,
+    x_here, x_ext, xr, rim_x, rim_b, xc, bc_ext, bcc, dt_all, gate, zr, wt, cot,
     taps_x, taps_bc, bias, head_par, gain_rows, gain, down_t, up, skip, weights, tails,
     spread, step, cum, log_start, log_tail, y_in, blocks, kept, state, peer_state,
     st_send, st_recv, dec_all, dec_wide, back_send, back_recv, in_send, s_in,
@@ -127,10 +127,10 @@
         pl.semaphore_signal(barrier, inc=1, device_id=context_peer(j), device_id_type=MESH)
         return carry
 
+    lax.fori_loop(1, 16, greet, 0)
     for j in range(1, 4):
         pl.semaphore_signal(barrier, inc=1, device_id={"tensor": lax.rem(t + j, 4)}, device_id_type=MESH)
         pl.semaphore_signal(barrier, inc=1, device_id={"fsdp": lax.rem(s + j, 4)}, device_id_type=MESH)
-    lax.fori_loop(1, 16, greet, 0)
     before = lax.rem(c + 15, 16)
     after = lax.rem(c + 1, 16)
 
@@ -174,6 +174,7 @@
         local[name] = pltpu.make_async_copy(src, dst, sl.at[2 + len(local)])
         local[name].start()
 
+    copy_here("x_all", x_in, x_here)
     copy_here("cot", cot_in, cot)
     copy_here("up", up_in, up)
     for i, source in enumerate((step_bias_in, rate_in, skip_in)):
@@ -189,26 +190,7 @@
     copy_here("gate", z_in.at[:, columns(t)], gate.at[t])
     copy_here("w", w_in, w_part(0, 1280, s))
 
-    def head_mask(i, carry):
-        head = lax.broadcasted_iota(jnp.int32, (256, 128), 0)
-        head = jnp.where(head >= 128, head - 128, head)
-        lane = lax.broadcasted_iota(jnp.int32, (256, 128), 1)
-        own_head = 2 * i + jnp.where(lane >= 64, 1, 0)
-        spread[:, tile(i)] = jnp.where(head == own_head, 1.0, 0.0).astype(BF16)
-        return carry
-
-    lax.fori_loop(0, 10, head_mask, 0)
-
-    def widen(v):
-        high = v.astype(BF16)
-        low = (v - high.astype(F32)).astype(BF16)
-        return dot(jnp.concatenate([high, low], axis=1), spread[...])
-
-    scale = 2.0 / (TOKENS ** 0.5)
-
-    local["cot"].wait()
-    local["up"].wait()
-    gt[t] = dot(up[...], cot[...], NT) * scale
+    local["x_all"].wait()
 
     gives_rim = jnp.logical_and(t == 3, c < 15)
 
@@ -255,13 +237,13 @@
         for copy in rim_copies():
             copy.start()
 
-    far_start(x_in, xr, "x")
+    far_start(x_here, xr, "x")
     send(bc_in.at[pl.ds(0, 64)], bc_rows(t, 0, 64), "b0", {"tensor": right})
     send(bc_in.at[pl.ds(64, 64)], bc_rows(t, 64, 64), "b1", {"tensor": left})
     send(bc_in.at[pl.ds(64, 64), pl.ds(0, 128)], b_lanes(t, 64), "b2", {"tensor": right})
     send(bc_in.at[pl.ds(0, 64), pl.ds(0, 128)], b_lanes(t, 0), "b3", {"tensor": left})
     send_triple(lambda j: (dt_window(tensor_peer(j)), dt_all.at[t], {"tensor": tensor_peer(j)}), 0)
-    near_start(x_in, x_rows, "x")
+    near_start(x_here, x_rows, "x")
 
     @pl.when(c == 0)
     def _():
@@ -277,6 +259,27 @@
     send(w_src(320), w_part(mine + 320, 320, s), "w1", {"fsdp": down_y})
     send(w_src(320), w_part(mine + 320, 320, s), "w2", {"fsdp": up_y})
     send(w_src(0), w_part(mine, 320, s), "w3", {"fsdp": down_y})
+
+    def head_mask(i, carry):
+        head = lax.broadcasted_iota(jnp.int32, (256, 128), 0)
+        head = jnp.where(head >= 128, head - 128, head)
+        lane = lax.broadcasted_iota(jnp.int32, (256, 128), 1)
+        own_head = 2 * i + jnp.where(lane >= 64, 1, 0)
+        spread[:, tile(i)] = jnp.where(head == own_head, 1.0, 0.0).astype(BF16)
+        return carry
+
+    lax.fori_loop(0, 10, head_mask, 0)
+
+    def widen(v):
+        high = v.astype(BF16)
+        low = (v - high.astype(F32)).astype(BF16)
+        return dot(jnp.concatenate([high, low], axis=1), spread[...])
+
+    scale = 2.0 / (TOKENS ** 0.5)
+
+    local["cot"].wait()
+    local["up"].wait()
+    gt[t] = dot(up[...], cot[...], NT) * scale
 
     settle(head_par, s_head)
     for name in ("bc", "dt", "taps_x", "taps_bc", "bias", "x", "gain", "down"):
@@ -750,7 +753,7 @@
     pltpu.make_async_copy(wt.at[:, pl.ds(0, 1920)], wt.at[:, pl.ds(0, 1920)], sgroup.at[2]).wait()
     for copy in started:
         copy.wait_send()
-    assert len(slots) <= 33 and len(send_slots) <= 6 and len(local) <= 12
+    assert len(slots) <= 33 and len(send_slots) <= 6 and len(local) <= 13
 
     @pl.when(gives_rim)
     def _():
@@ -775,6 +778,7 @@
         in_specs=[hbm] * 14,
         out_specs=(vmem, vmem, vmem),
         scratch_shapes=[
+            pltpu.VMEM((ROWS, 4 * WIDTH), BF16),
             pltpu.VMEM((16 + 512, WIDTH), BF16),
             pltpu.VMEM((2, 64, WIDTH), BF16),
             pltpu.VMEM((8, WIDTH), BF16),
@@ -829,7 +833,7 @@
             pltpu.VMEM((4, 2, RANK, 128), F32),
             pltpu.VMEM((4, 2, RANK, 128), BF16),
             pltpu.VMEM((16, 2, RANK, 128), BF16),
-            dma((6,)), dma((33,)), dma((14,)),
+            dma((6,)), dma((33,)), dma((15,)),
             dma((2,)), dma((2,)), dma, dma, dma((2,)), dma((2,)), dma, dma, dma, dma, dma, dma((10,)), dma((4,)), dma((6,)), dma((6,)), dma((6,)), dma,
         ],
         compiler_params=pltpu.CompilerParams(

time: 72.8 us -> 72.8 us (level)
  no operation moved by 1% of the time
where the time goes in v7:
time: 72.8 us
  Pallas kernels  70 us (96%)
  local copies, waits for them, and re-layouts  2.14 us (3%)
    pallas_call x1, Pallas kernels, shards(): pl.pallas_call(kernel, out_shape=(pltpu.VMEM((ROWS, OUT), BF16), pltpu.VM...  70 us
    unnamed x3, local copies, waits for them, and re-layouts  2.14 us

profile of v7, /device:TPU:1, one launch (start us, length us, event | category | flops | bytes accessed | tf_op | source)
XLA Modules:
  0.0 72.8 jit_solution(2474753476485827315)
XLA Ops:
  0.6 70.0 %shard_map.157 = (bf16[128,2560]{1,0:T(8,128)(2,1)S(1)}, f32[16,1280]{1,0:T(8,128)S(1)}, f32[16,2560]{1,0:T(8,128)S(1)}) custom-call(bf16[128,5120]{1,0:T(8,128)(2,1)} %bitcast.17, bf16[128,256]{1,0:T(8,128)(2,1)} %bitcast.20, bf16[128,5120]{1,0:T(8,128)(2,1)} %bitcast.18, bf16[80,128]{1,0:T(8,128)(2,1)} %bitcast.23, bf16[1280,640]{1,0:T(8,128)(2,1)} %w_in.1, ...), custom_call_target="tpu_custom_call" | custom-call | tf_op jit(solution)/shard_map/pallas_call | solution.py:771
  70.6 0.8 %copy.20 = bf16[1,128,2560]{2,1,0:T(8,128)(2,1)} copy(bf16[1,128,2560]{2,1,0:T(8,128)(2,1)S(1)} %bitcast.15) | data formatting | bytes 1310720
  71.5 0.6 copy.21
  72.1 0.7 copy.22
